TPU v7x, 32 devices: a whole 2x2x4 slice. The times are simulated.
32 devices in a mesh: dp: 2 (over core), fsdp: 16 (over z, y, x).
Axes of the slice: x: 2, y: 2, z: 4, core: 2. Of those that a mesh axis runs over, the one named last changes fastest.
Arguments:
- tokens: bfloat16 [8192, 4096], P(('dp', 'fsdp')), may hold values from -6 to 6
- block_codes: bfloat16 [256, 128, 128], P('fsdp'), may hold values from -4 to 4
- scales: float32 [256], P('fsdp'), may hold values from 0.008 to 0.03
- counts: int32 [16], replicated, may hold values from 0 to 16, as said below
- cotangent: bfloat16 [8192, 512], P(('dp', 'fsdp')), may hold values from -6 to 6
Outputs:
- projected: bfloat16 [8192, 512], P(('dp', 'fsdp'))
- token_grad: bfloat16 [8192, 4096], P(('dp', 'fsdp'))
- block_grad: bfloat16 [256, 128, 128], P('fsdp')
Inputs may be any that keep to these rules, and one draw needn't show every extreme that they name: counts sum to 128; each is at most 16, and some owner has exactly 16 and some none; slots past an owner's count hold values that are not used.
All inputs are finite; a program needn't handle non-finite values.
Results may differ from a plain program's by a relative error of at most 0.009.
Values may be sent and summed in bfloat16 or wider, within the bound.
No kernel may reach another device: no remote copies, remote signals or barrier semaphores. Data moves between devices by JAX's collectives and lax.ppermute only.
A program may use at most 128 MiB of HBM per device.

v0:
```python
import math

import jax
import jax.numpy as jnp
from jax import lax
from jax.sharding import PartitionSpec as P


def block_index(counts, owners_total, block_count, most_slots):
    run_ends = jnp.cumsum(counts)
    offsets = run_ends - counts
    block_ids = jnp.arange(block_count, dtype=jnp.int32)
    owners = jnp.sum((run_ends[None, :] <= block_ids[:, None]).astype(jnp.int32), axis=1)
    matched = owners[:, None] == jnp.arange(owners_total, dtype=jnp.int32)[None, :]
    run_start = jnp.sum(jnp.where(matched, offsets[None, :], 0), axis=1)
    source_ids = owners * most_slots + block_ids - run_start
    return (offsets, source_ids)


def body(tokens, block_codes, scales, counts, cotangent):
    owners_total = lax.axis_size("fsdp")
    most_slots = block_codes.shape[0]
    tile_size = block_codes.shape[1]
    width = tokens.shape[1]
    key_width = cotangent.shape[1]
    row_tiles = width // tile_size
    col_tiles = key_width // tile_size
    block_count = row_tiles * col_tiles
    total_tokens = tokens.shape[0] * lax.axis_size("dp") * owners_total
    loss_scale = 1.0 / math.sqrt(total_tokens)
    offsets, source_ids = block_index(counts, owners_total, block_count, most_slots)
    own_blocks = (block_codes.astype(jnp.float32) * scales[:, None, None]).astype(jnp.bfloat16)
    all_blocks_held = lax.all_gather(own_blocks, "fsdp", axis=0, tiled=True)
    blocks = jnp.take(all_blocks_held, source_ids, axis=0)
    weight = (
        blocks.reshape(row_tiles, col_tiles, tile_size, tile_size)
        .transpose(0, 2, 1, 3)
        .reshape(width, key_width)
    )
    projected = jnp.dot(tokens, weight, preferred_element_type=jnp.float32).astype(jnp.bfloat16)
    token_grad = lax.dot_general(
        cotangent, weight, (((1,), (1,)), ((), ())), preferred_element_type=jnp.float32
    ).astype(jnp.bfloat16)
    local_grad = (
        lax.dot_general(
            tokens, cotangent, (((0,), (0,)), ((), ())), preferred_element_type=jnp.float32
        )
        * loss_scale
    )
    grad_blocks = (
        local_grad.reshape(row_tiles, tile_size, col_tiles, tile_size)
        .transpose(0, 2, 1, 3)
        .reshape(block_count, tile_size, tile_size)
    )
    evened = lax.psum_scatter(grad_blocks, "fsdp", scatter_dimension=0, tiled=True)
    evened = lax.psum(evened.astype(jnp.bfloat16), "dp").astype(jnp.float32)
    finished = lax.all_gather(evened.astype(jnp.bfloat16), "fsdp", axis=0, tiled=True)
    my_index = lax.axis_index("fsdp")
    is_mine = jnp.arange(owners_total, dtype=jnp.int32) == my_index
    my_start = jnp.sum(jnp.where(is_mine, offsets, 0))
    my_count = jnp.sum(jnp.where(is_mine, counts, 0))
    within = jnp.arange(most_slots, dtype=jnp.int32)
    wanted = my_start + within
    picked = jnp.take(finished, jnp.clip(wanted, 0, block_count - 1), axis=0)
    block_grad = jnp.where((within < my_count)[:, None, None], picked, jnp.zeros_like(picked))
    return (projected, token_grad, block_grad)


def solution(mesh):
    return jax.shard_map(
        body,
        mesh=mesh,
        in_specs=(
            P(("dp", "fsdp"), None),
            P("fsdp", None, None),
            P("fsdp"),
            P(),
            P(("dp", "fsdp"), None),
        ),
        out_specs=(P(("dp", "fsdp"), None), P(("dp", "fsdp"), None), P("fsdp", None, None)),
        check_vma=False,
    )
```

profile of v0, /device:TPU:0, one launch (start us, length us, event | category | flops | bytes accessed | tf_op | source)
XLA Modules:
  0.0 439.9 jit_solution(7048292042617960575)
XLA Ops:
  7.2 0.0 copy-start
  7.2 0.0 reduce-scatter.2.cloned.1.call-start
  7.2 1.5 copy-done
  8.8 5.5 %convolution_multiply_fusion = f32[4096,512]{1,0:T(8,128)} fusion(bf16[256,4096]{1,0:T(8,128)(2,1)S(1)} %copy-done, bf16[256,512]{1,0:T(8,128)(2,1)} %param.9), kind=kOutput, calls=%fused_computation.2 | convolution fusion | flops 1075838976 | bytes 10747904 | tf_op jit(solution)/shard_map/dot_general | solution.py:45
  14.2 9.9 %reshape.119 = f32[32,128,4,128]{3,2,1,0:T(4,128)} reshape(f32[4096,512]{1,0:T(8,128)} %convolution_multiply_fusion) | data formatting | bytes 16777216 | tf_op jit(solution)/shard_map/reshape | solution.py:51
  24.1 7.9 %copy.33 = f32[32,128,4,128]{3,1,2,0:T(8,128)} copy(f32[32,128,4,128]{3,2,1,0:T(4,128)} %reshape.119) | data formatting | bytes 16777216 | tf_op jit(solution)/shard_map/reshape | solution.py:51
  32.0 0.0 copy-start.2
  32.0 0.0 copy-start.5
  32.0 0.0 copy-start.4
  32.0 0.0 reduce-scatter.2.cloned.1.call-update
  32.0 0.0 all-reduce.2.cloned.1.call-start
  32.1 180.7 %reduce-scatter.2.cloned.1.call-done = f32[8,128,128]{2,1,0:T(8,128)} async-done(((f32[128,128,128]{2,1,0:T(8,128)}), f32[8,128,128]{2,1,0:T(8,128)}) %reduce-scatter.2.cloned.1.call-update) | async-done | bytes 524304 | tf_op jit(solution)/shard_map/reduce_scatter | solution.py:55
  212.7 1.8 convert_element_type.33
  214.5 0.0 all-reduce.2.cloned.1.call-update
  214.5 0.0 all-gather.3.cloned.1.call-start
  214.6 0.0 copy-done.2
  214.6 0.0 copy-done.5
  214.6 1.0 multiply_convert_fusion
  215.6 0.0 all-gather.3.cloned.1.call-update
  215.6 0.0 all-gather.5.cloned.1.call-start
  215.7 20.7 %all-reduce.2.cloned.1.call-done = bf16[8,128,128]{2,1,0:T(8,128)(2,1)} async-done(((bf16[8,128,128]{2,1,0:T(8,128)(2,1)}), bf16[8,128,128]{2,1,0:T(8,128)(2,1)}) %all-reduce.2.cloned.1.call-update) | async-done | bytes 262160 | tf_op jit(solution)/shard_map/psum | solution.py:56
  236.3 0.0 all-gather.5.cloned.1.call-update
  236.3 0.0 copy-done.4
  236.3 0.1 copy.29
  236.5 0.1 reduce
  236.6 0.1 convert_reduce_fusion
  236.7 0.6 fusion.13
  237.3 0.1 select_reduce_fusion
  237.4 0.1 reduce_sum.42
  237.5 0.1 copy.31
  237.6 0.1 mul.38
  237.7 0.1 copy.30
  237.8 0.7 fusion.15
  238.4 1.3 compare_and_fusion
  239.8 113.4 %all-gather.3.cloned.1.call-done = bf16[256,128,128]{2,1,0:T(8,128)(2,1)} async-done(((bf16[16,128,128]{2,1,0:T(8,128)(2,1)}), bf16[256,128,128]{2,1,0:T(8,128)(2,1)}) %all-gather.3.cloned.1.call-update) | async-done | bytes 8388624 | tf_op jit(solution)/shard_map/all_gather | solution.py:33
  353.2 6.4 %gather_fusion = bf16[128,128,128]{2,1,0:T(8,128)(2,1)} fusion(bf16[256,128,128]{2,1,0:T(8,128)(2,1)} %all-gather.3.cloned.1.call-done, s32[1024]{0:T(1024)S(1)} %pad_clamp_fusion.1), kind=kCustom, calls=%fused_computation | custom fusion | bytes 8389120 | tf_op jit(solution)/shard_map/jit(_take)/gather | solution.py:34
  359.6 7.9 %copy.32 = bf16[32,4,128,128]{2,0,3,1:T(8,128)(2,1)} copy(bf16[32,4,128,128]{3,2,1,0:T(8,128)(2,1)} %bitcast.40) | data formatting | bytes 8388608 | tf_op jit(solution)/shard_map/jit(_take)/gather | solution.py:34
  367.6 2.7 broadcast_select_fusion
  370.2 0.0 copy-start.1
  370.2 1.9 copy-done.1
  372.2 1.5 fusion.9
  373.7 0.8 copy.34
  374.5 0.0 copy-done.3
  374.5 8.0 %fusion = bf16[256,4096]{0,1:T(8,128)(2,1)} fusion(bf16[256,512]{1,0:T(8,128)(2,1)S(1)} %copy-done.3, bf16[64,8,32,128]{3,2,1,0:T(8,128)(2,1)} %bitcast.42), kind=kOutput, calls=%fused_computation.4 | convolution fusion | flops 1074790400 | bytes 6553600 | tf_op jit(solution)/shard_map/dot_general | solution.py:41
  382.5 4.1 copy.35
  386.6 43.1 %all-gather.5.cloned.1.call-done = bf16[128,128,128]{2,1,0:T(8,128)(2,1)} async-done(((bf16[8,128,128]{2,1,0:T(8,128)(2,1)}), bf16[128,128,128]{2,1,0:T(8,128)(2,1)}) %all-gather.5.cloned.1.call-update) | async-done | bytes 4194320 | tf_op jit(solution)/shard_map/all_gather | solution.py:57
  429.6 2.8 gather_fusion.1
  432.5 0.9 select_select_fusion
  (7 shorter events, 0.1 us)
Async XLA Ops:
  7.2 1.6 copy-start
  7.2 205.6 %reduce-scatter.2.cloned.1.call-start = ((), (), s32[]{:S(2)}) async-start(), calls=%async_computation.2 | async-start | bytes 8912896 | tf_op jit(solution)/shard_map/reduce_scatter | solution.py:55
  32.0 182.6 %copy-start.2 = (bf16[16,128,128]{2,1,0:T(8,128)(2,1)S(1)}, bf16[16,128,128]{2,1,0:T(8,128)(2,1)}, u32[]{:S(2)}) copy-start(bf16[16,128,128]{2,1,0:T(8,128)(2,1)} %param.6) | copy-start | bytes 1572868
  32.0 182.6 %copy-start.5 = (f32[16]{0:T(128)S(1)}, f32[16]{0:T(128)}, u32[]{:S(2)}) copy-start(f32[16]{0:T(128)} %param.7) | copy-start | bytes 196
  32.0 204.4 %copy-start.4 = (s32[16]{0:T(128)S(1)}, s32[16]{0:T(128)}, u32[]{:S(2)}) copy-start(s32[16]{0:T(128)} %param.8) | copy-start | bytes 196
  32.0 204.3 %all-reduce.2.cloned.1.call-start = ((), (), s32[]{:S(2)}) async-start(), calls=%async_computation.3 | async-start | bytes 524288 | tf_op jit(solution)/shard_map/psum | solution.py:56
  214.5 138.7 %all-gather.3.cloned.1.call-start = ((), (), s32[]{:S(2)}) async-start(), calls=%async_computation.1 | async-start | bytes 8912896 | tf_op jit(solution)/shard_map/all_gather | solution.py:33
  215.6 214.0 %all-gather.5.cloned.1.call-start = ((), (), s32[]{:S(2)}) async-start(), calls=%async_computation.4 | async-start | bytes 4456448 | tf_op jit(solution)/shard_map/all_gather | solution.py:57
  370.2 1.9 copy-start.1
  372.2 2.4 copy-start.3
Sparse Core Ops, SparseCore 0:
  32.1 180.5 reduce-scatter.1
  215.6 20.6 all-reduce.1
  239.7 113.4 all-gather.2
  355.8 73.7 all-gather.4
where the time goes:
time: 441 us; the launch traced here: 440 us
  waiting for transfers between devices  358 us (81%)
  local copies, waits for them, and re-layouts  43.8 us (10%)
  matrix products  14.9 us (3%)
  between operations  13.9 us (3%)
  other arithmetic  9.34 us (2%)
    reduce_scatter x1, waiting for transfers between devices, body(): lax.psum_scatter(grad_blocks, 'fsdp', scatter_dimension=0, tiled=True)  181 us
    all_gather x1, waiting for transfers between devices, body(): all_blocks_held = lax.all_gather(own_blocks, 'fsdp', axis=0, tiled=True)  113 us
    all_gather x1, waiting for transfers between devices, body(): lax.all_gather(evened.astype(jnp.bfloat16), 'fsdp', axis=0, tiled=True)  43.1 us
    psum x1, waiting for transfers between devices, body(): evened = lax.psum(evened.astype(jnp.bfloat16), 'dp').astype(jnp.float32)  20.7 us
    reshape x2, local copies, waits for them, and re-layouts, body(): local_grad.reshape(row_tiles, tile_size, col_tiles, tile_size)  17.8 us
    gather x2, local copies, waits for them, and re-layouts, body(): blocks = jnp.take(all_blocks_held, source_ids, axis=0)  14.4 us
  transfers between devices with their start and end apart: 4, of which 4 were waited for; matrix products, arithmetic and copies ran while one was open for 8% of the time, Pallas kernels for 0%

commit v1 on v0

v1 whole, which is shorter than its diff:
```python
import functools
import math

import jax
import jax.numpy as jnp
from jax import lax
from jax.experimental import pallas as pl
from jax.experimental.pallas import tpu as pltpu
from jax.sharding import PartitionSpec as P


PERIOD = 8
INNER = 4
VMEM = pltpu.VMEM
BF16 = jnp.bfloat16


def class_of(core, place):
    return (place // 2) * 4 + core * 2 + place % 2


def prefix(counts, stop):
    return lax.fori_loop(0, stop, lambda i, total: total + counts[i], jnp.int32(0))


def lead(cls, start):
    return (cls - start) & (PERIOD - 1)


def here():
    me = lax.axis_index("fsdp")
    return lax.axis_index("dp"), me // INNER, me % INNER, me


def spread_kernel(slots, reach, counts, scales, codes, *outs):
    core, _, place, me = here()
    start = prefix(counts, me)
    for step, out in enumerate(outs):
        first = lead(class_of(core, place ^ step), start)
        for t in range(reach):
            slot = jnp.minimum(first + PERIOD * t, slots - 1)
            out[t] = (codes[slot].astype(jnp.float32) * scales[slot]).astype(BF16)


def stack_kernel(reach, *refs):
    out = refs[-1]
    for m, ref in enumerate(refs[:-1]):
        out[pl.ds(m * reach, reach)] = ref[...]


def class_kernel(planes, reach, counts, *refs):
    ins, out, starts = refs[:planes], refs[planes], refs[planes + 1]
    core, plane, place, _ = here()
    cls = class_of(core, place)

    def note(i, total):
        starts[i] = total
        return total + counts[i]

    lax.fori_loop(0, planes * INNER, note, jnp.int32(0))
    for shift, ref in enumerate(ins):
        source = lax.rem(plane + planes - shift, planes)
        for m in range(INNER):
            owner = source * INNER + (place ^ m)
            first = lead(cls, starts[owner])
            for t in range(reach):

                @pl.when(first + PERIOD * t < counts[owner])
                def _(first=first, owner=owner, t=t, m=m, ref=ref):
                    out[(starts[owner] + first) // PERIOD + t] = ref[m * reach + t]


def grad_kernel(scale, tile, per_step, mine, theirs, cot_mine, cot_theirs, *refs):
    outs, quad = refs[:INNER], refs[INNER]
    core, _, place, _ = here()
    half = cot_mine.shape[1] // 2
    columns = pl.ds(pl.multiple_of(core * half, half), half)
    left, right = cot_mine[:, columns], cot_theirs[:, columns]
    for k in range(per_step):
        rows = pl.ds(2 * tile * k, 2 * tile)
        dims = (((0,), (0,)), ((), ()))
        part = lax.dot_general(mine[:, rows], left, dims, preferred_element_type=jnp.float32)
        part += lax.dot_general(theirs[:, rows], right, dims, preferred_element_type=jnp.float32)
        quad[...] = part * scale
        for m, out in enumerate(outs):
            where = place ^ m
            row = pl.multiple_of((where // 2) * tile, tile)
            col = pl.multiple_of((where % 2) * tile, tile)
            out[k] = quad[pl.ds(row, tile), pl.ds(col, tile)].astype(BF16)


def window(counts, cls, plane, blocks, span):
    start = prefix(counts, plane * INNER)
    return jnp.minimum((start + lead(cls, start)) // PERIOD, blocks - span)


def plane_sum_kernel(planes, span, counts, *refs):
    ins, outs, total = refs[:INNER], refs[INNER:-1], refs[-1]
    core, plane, place, _ = here()
    cls = class_of(core, place)
    blocks = total.shape[0]
    for j in range(blocks):
        acc = ins[0][j].astype(jnp.float32)
        for ref in ins[1:]:
            acc += ref[j].astype(jnp.float32)
        total[j] = acc.astype(BF16)
    for shift, out in enumerate(outs):
        target = lax.rem(plane + shift, planes)
        out[...] = total[pl.ds(window(counts, cls, target, blocks, span), span)]


def owner_kernel(blocks, reach, span, planes, counts, *refs):
    ins, outs, total = refs[:planes], refs[planes:-1], refs[-1]
    core, plane, place, _ = here()
    cls = class_of(core, place)
    acc = ins[0][...].astype(jnp.float32)
    for ref in ins[1:]:
        acc += ref[...].astype(jnp.float32)
    total[...] = acc.astype(BF16)
    base = window(counts, cls, plane, blocks, span)
    for m, out in enumerate(outs):
        start = prefix(counts, plane * INNER + (place ^ m))
        j = (start + lead(cls, start)) // PERIOD - base
        for t in range(reach):
            out[t] = total[jnp.clip(j + t, 0, span - 1)]


def slots_kernel(slots, reach, counts, *refs):
    ins, out = refs[:-1], refs[-1]
    core, _, place, me = here()
    start, count = prefix(counts, me), counts[me]
    for n, ref in enumerate(ins):
        side = core ^ (n // INNER)
        first = lead(class_of(side, place ^ (n % INNER)), start)
        for t in range(reach):
            slot = first + PERIOD * t

            @pl.when(slot < slots)
            def _(slot=slot, ref=ref, t=t):
                value = ref[t]
                out[slot] = jnp.where(slot < count, value, jnp.zeros_like(value))


def product_kernel(tile, per_step, tokens, cot, *refs):
    pieces, projected, token_grad, weight, acc = refs[:-4], refs[-4], refs[-3], refs[-2], refs[-1]
    core, _, place, _ = here()
    step = pl.program_id(0)
    for n, ref in enumerate(pieces):
        side, where = core ^ (n // INNER), place ^ (n % INNER)
        col = pl.multiple_of((side * 2 + where % 2) * tile, tile)
        for k in range(per_step):
            row = pl.multiple_of((where // 2) * tile + 2 * tile * k, tile)
            weight[pl.ds(row, tile), pl.ds(col, tile)] = ref[k]

    @pl.when(step == 0)
    def _():
        acc[...] = jnp.zeros_like(acc)

    acc[...] += jnp.dot(tokens[...], weight[...], preferred_element_type=jnp.float32)
    token_grad[...] = lax.dot_general(
        cot[...], weight[...], (((1,), (1,)), ((), ())), preferred_element_type=jnp.float32
    ).astype(BF16)

    @pl.when(step == pl.num_programs(0) - 1)
    def _():
        projected[...] = acc[...].astype(BF16)


def whole():
    return pl.BlockSpec(memory_space=VMEM)


def scalars():
    return pl.BlockSpec(memory_space=pltpu.SMEM)


def room(mebibytes):
    return pltpu.CompilerParams(vmem_limit_bytes=mebibytes * 2**20)


def cost(flops, nbytes):
    return pl.CostEstimate(flops=flops, bytes_accessed=nbytes, transcendentals=0)


def body(tokens, block_codes, scales, counts, cotangent):
    owners = lax.axis_size("fsdp")
    planes = owners // INNER
    slots, tile = block_codes.shape[:2]
    rows, width = tokens.shape
    key_width = cotangent.shape[1]
    blocks = (width // tile) * (key_width // tile) // PERIOD
    reach = -(-slots // PERIOD)
    span = min(-(-slots * INNER // PERIOD), blocks)
    total_tokens = rows * lax.axis_size("dp") * owners

    def many(n):
        return jax.ShapeDtypeStruct((n, tile, tile), BF16)

    block_bytes = tile * tile * 2

    def beside(value, m):
        return lax.ppermute(value, "fsdp", [(i, i ^ m) for i in range(owners)])

    def along(value, shift):
        pairs = [(i, (i + shift * INNER) % owners) for i in range(owners)]
        return lax.ppermute(value, "fsdp", pairs)

    def across(value):
        return lax.ppermute(value, "dp", [(0, 1), (1, 0)])

    def call(kernel, *operands, **how):
        return pl.pallas_call(kernel, **how)(*operands)

    their_tokens, their_cot = across(tokens), across(cotangent)

    spread = call(
        functools.partial(spread_kernel, slots, reach),
        counts, scales, block_codes,
        out_shape=[many(reach)] * INNER,
        in_specs=[scalars(), scalars(), whole()],
        out_specs=[whole()] * INNER,
        cost_estimate=cost(8 * block_bytes, 24 * block_bytes),
        compiler_params=room(8),
    )
    near = [spread[0]] + [beside(spread[m], m) for m in range(1, INNER)]

    per_step = 4
    steps = blocks // per_step
    wide = 2 * tile * per_step
    grads = call(
        functools.partial(grad_kernel, 1.0 / math.sqrt(total_tokens), tile, per_step),
        tokens, their_tokens, cotangent, their_cot,
        out_shape=[many(blocks)] * INNER,
        grid=(steps,),
        in_specs=[pl.BlockSpec((rows, wide), lambda i: (0, i))] * 2
        + [pl.BlockSpec((rows, key_width), lambda i: (0, 0))] * 2,
        out_specs=[pl.BlockSpec((per_step, tile, tile), lambda i: (i, 0, 0))] * INNER,
        scratch_shapes=[VMEM((2 * tile, 2 * tile), jnp.float32)],
        cost_estimate=cost(2 * rows * width * key_width, 6 * rows * width),
        compiler_params=room(20),
    )
    parts = [grads[0]] + [beside(grads[m], m) for m in range(1, INNER)]

    stacked = call(
        functools.partial(stack_kernel, reach),
        *near,
        out_shape=many(INNER * reach),
        in_specs=[whole()] * INNER,
        out_specs=whole(),
        cost_estimate=cost(8 * block_bytes, 16 * block_bytes),
        compiler_params=room(8),
    )
    held = [stacked] + [along(stacked, s) for s in range(1, planes)]

    own_class = call(
        functools.partial(class_kernel, planes, reach),
        counts, *held,
        out_shape=many(blocks),
        in_specs=[scalars()] + [whole()] * planes,
        out_specs=whole(),
        scratch_shapes=[pltpu.SMEM((owners,), jnp.int32)],
        cost_estimate=cost(32 * block_bytes, 48 * block_bytes),
        compiler_params=room(8),
    )
    classes = [own_class] + [beside(own_class, m) for m in range(1, INNER)]

    windows = call(
        functools.partial(plane_sum_kernel, planes, span),
        counts, *parts,
        out_shape=[many(span)] * planes,
        in_specs=[scalars()] + [whole()] * INNER,
        out_specs=[whole()] * planes,
        scratch_shapes=[VMEM((blocks, tile, tile), BF16)],
        cost_estimate=cost(64 * block_bytes, 96 * block_bytes),
        compiler_params=room(12),
    )
    sums = [windows[0]] + [along(windows[s], s) for s in range(1, planes)]

    sent = call(
        functools.partial(owner_kernel, blocks, reach, span, planes),
        counts, *sums,
        out_shape=[many(reach)] * INNER,
        in_specs=[scalars()] + [whole()] * planes,
        out_specs=[whole()] * INNER,
        scratch_shapes=[VMEM((span, tile, tile), BF16)],
        cost_estimate=cost(32 * block_bytes, 48 * block_bytes),
        compiler_params=room(8),
    )
    mine = [sent[0]] + [beside(sent[m], m) for m in range(1, INNER)]

    all_classes = classes + [across(own_class)] + [across(c) for c in classes[1:]]
    projected, token_grad = call(
        functools.partial(product_kernel, tile, per_step),
        tokens, cotangent, *all_classes,
        out_shape=[
            jax.ShapeDtypeStruct((rows, key_width), BF16),
            jax.ShapeDtypeStruct((rows, width), BF16),
        ],
        grid=(steps,),
        in_specs=[
            pl.BlockSpec((rows, wide), lambda i: (0, i)),
            pl.BlockSpec((rows, key_width), lambda i: (0, 0)),
        ]
        + [pl.BlockSpec((per_step, tile, tile), lambda i: (i, 0, 0))] * (2 * INNER),
        out_specs=[
            pl.BlockSpec((rows, key_width), lambda i: (0, 0)),
            pl.BlockSpec((rows, wide), lambda i: (0, i)),
        ],
        scratch_shapes=[VMEM((wide, key_width), BF16), VMEM((rows, key_width), jnp.float32)],
        cost_estimate=cost(4 * rows * width * key_width, 12 * rows * width),
        compiler_params=room(28),
    )

    all_mine = mine + [across(v) for v in mine]
    block_grad = call(
        functools.partial(slots_kernel, slots, reach),
        counts, *all_mine,
        out_shape=many(slots),
        in_specs=[scalars()] + [whole()] * (2 * INNER),
        out_specs=whole(),
        cost_estimate=cost(16 * block_bytes, 32 * block_bytes),
        compiler_params=room(8),
    )
    return (projected, token_grad, block_grad)


def solution(mesh):
    return jax.shard_map(
        body,
        mesh=mesh,
        in_specs=(
            P(("dp", "fsdp"), None),
            P("fsdp", None, None),
            P("fsdp"),
            P(),
            P(("dp", "fsdp"), None),
        ),
        out_specs=(P(("dp", "fsdp"), None), P(("dp", "fsdp"), None), P("fsdp", None, None)),
        check_vma=False,
    )
```

time: 441 us -> 96.5 us (0.22)
  waiting for transfers between devices: 358 us -> 48.7 us
  local copies, waits for them, and re-layouts: 43.8 us -> 4.9 us
  starting transfers between devices: 0.16 us -> 29.5 us
  matrix products: 14.9 us -> 0 us
  between operations: 13.9 us -> 0.76 us
  Pallas kernels: 0 us -> 12.4 us
  other arithmetic: 9.34 us -> 0 us
    reduce_scatter x1 -> x0, waiting for transfers between devices: 181 us -> none  [body(): lax.psum_scatter(grad_blocks, 'fsdp', scatter_dimension=0, tiled=True)]
    all_gather x2 -> x0, waiting for transfers between devices: 156 us -> none  [the longest x1 113 us: body(): all_blocks_held = lax.all_gather(own_blocks, 'fsdp', axis=0, tiled=True)]
    ppermute x0 -> x28, waiting for transfers between devices: none -> 48.7 us  [the longest x6 29.6 us: along(): return lax.ppermute(value, 'fsdp', pairs)]
    ppermute x0 -> x28, starting transfers between devices: none -> 29.5 us  [the longest x6 14.2 us: along(): return lax.ppermute(value, 'fsdp', pairs)]
    psum x1 -> x0, waiting for transfers between devices: 20.7 us -> none  [body(): evened = lax.psum(evened.astype(jnp.bfloat16), 'dp').astype(jnp.float32)]
    reshape x2 -> x0, local copies, waits for them, and re-layouts: 17.8 us -> none  [body(): local_grad.reshape(row_tiles, tile_size, col_tiles, tile_size)]
    gather x3 -> x0, local copies, waits for them, and re-layouts: 17.2 us -> none  [the longest x2 14.4 us: body(): blocks = jnp.take(all_blocks_held, source_ids, axis=0)]
    dot_general x3 -> x0, matrix products: 14.9 us -> none  [the longest x1 7.96 us: body(): lax.dot_general(cotangent, weight, (((1,), (1,)), ((), ())), preferred_el...]
  transfers between devices with their start and end apart: 4 -> 28, of which waited for: 4 -> 13; matrix products, arithmetic and copies ran while one was open for 8% -> 0% of each run, Pallas kernels for 0% -> 9%
where the time goes in v1:
time: 96.5 us; the launch traced here: 96.2 us
  waiting for transfers between devices  48.7 us (50%)
  starting transfers between devices  29.5 us (31%)
  Pallas kernels  12.4 us (13%)
  local copies, waits for them, and re-layouts  4.9 us (5%)
    ppermute x6, waiting for transfers between devices, along(): return lax.ppermute(value, 'fsdp', pairs)  29.6 us
    ppermute x12, waiting for transfers between devices, beside(): return lax.ppermute(value, 'fsdp', [(i, i ^ m) for i in range(owners)])  19 us
    ppermute x6, starting transfers between devices, along(): return lax.ppermute(value, 'fsdp', pairs)  14.2 us
    ppermute x12, starting transfers between devices, beside(): return lax.ppermute(value, 'fsdp', [(i, i ^ m) for i in range(owners)])  14.1 us
    pallas_call x8, Pallas kernels, call(): return pl.pallas_call(kernel, **how)(*operands)  12.4 us
    unnamed x16, local copies, waits for them, and re-layouts  4.9 us
  transfers between devices with their start and end apart: 28, of which 13 were waited for; matrix products, arithmetic and copies ran while one was open for 0% of the time, Pallas kernels for 9%

profile of v1, /device:TPU:0, one launch (start us, length us, event | category | flops | bytes accessed | tf_op | source)
XLA Modules:
  0.0 96.2 jit_solution(16184690982615744508)
XLA Ops:
  0.6 0.6 collective-permute-start.13
  1.2 0.1 collective-permute-start.14
  1.3 1.0 %copy-done.2 = bf16[16,128,128]{2,1,0:T(8,128)(2,1)S(1)} copy-done((bf16[16,128,128]{2,1,0:T(8,128)(2,1)S(1)}, bf16[16,128,128]{2,1,0:T(8,128)(2,1)}, u32[]{:S(2)}) %copy-start.2) | copy-done | bytes 524312
  2.3 0.7 copy-done.5
  3.0 0.7 copy-done.7
  3.6 0.6 shard_map.76
  4.2 3.0 %collective-permute-start = (bf16[2,128,128]{2,1,0:T(8,128)(2,1)S(1)}, bf16[2,128,128]{2,1,0:T(8,128)(2,1)S(1)}, u32[]{:S(2)}, u32[]{:S(2)}) collective-permute-start(bf16[2,128,128]{2,1,0:T(8,128)(2,1)S(1)} %get-tuple-element.22), channel_id=1, source_target_pairs={{0,1},{1,0},{2,3},{3,2},{4,5},{5,4},{6,7},{7,6},{8,9},{9,8},{10,11... | collective-permute-start | bytes 196616 | tf_op jit(solution)/shard_map/ppermute | solution.py:202
  7.2 1.5 %collective-permute-start.1 = (bf16[2,128,128]{2,1,0:T(8,128)(2,1)S(1)}, bf16[2,128,128]{2,1,0:T(8,128)(2,1)S(1)}, u32[]{:S(2)}, u32[]{:S(2)}) collective-permute-start(bf16[2,128,128]{2,1,0:T(8,128)(2,1)S(1)} %get-tuple-element.23), channel_id=1, source_target_pairs={{0,2},{1,3},{2,0},{3,1},{4,6},{5,7},{6,4},{7,5},{8,10},{9,11},{10,... | collective-permute-start | bytes 196616 | tf_op jit(solution)/shard_map/ppermute | solution.py:202
  8.7 0.0 collective-permute-start.2
  8.8 0.8 collective-permute-done.refs_1_
  9.6 1.9 %collective-permute-done.1.refs_2_ = bf16[2,128,128]{2,1,0:T(8,128)(2,1)S(1)} collective-permute-done((bf16[2,128,128]{2,1,0:T(8,128)(2,1)S(1)}, bf16[2,128,128]{2,1,0:T(8,128)(2,1)S(1)}, u32[]{:S(2)}, u32[]{:S(2)}) %collective-permute-start.1) | collective-permute-done | bytes 65568 | tf_op jit(solution)/shard_map/ppermute | solution.py:202
  11.5 2.4 %collective-permute-done.2.refs_3_ = bf16[2,128,128]{2,1,0:T(8,128)(2,1)S(1)} collective-permute-done((bf16[2,128,128]{2,1,0:T(8,128)(2,1)S(1)}, bf16[2,128,128]{2,1,0:T(8,128)(2,1)S(1)}, u32[]{:S(2)}, u32[]{:S(2)}) %collective-permute-start.2) | collective-permute-done | bytes 65568 | tf_op jit(solution)/shard_map/ppermute | solution.py:202
  13.9 0.0 collective-permute-done.14.cot_theirs
  13.9 0.0 collective-permute-done.13.theirs
  14.0 0.0 copy-start
  14.0 1.6 %copy-done = bf16[256,4096]{1,0:T(8,128)(2,1)S(1)} copy-done((bf16[256,4096]{1,0:T(8,128)(2,1)S(1)}, bf16[256,4096]{1,0:T(8,128)(2,1)}, u32[]{:S(2)}) %copy-start) | copy-done | bytes 2097176
  15.6 0.9 copy-done.3
  16.5 2.5 %shard_map.80 = (bf16[16,128,128]{2,1,0:T(8,128)(2,1)S(1)}, bf16[16,128,128]{2,1,0:T(8,128)(2,1)S(1)}, bf16[16,128,128]{2,1,0:T(8,128)(2,1)S(1)}, bf16[16,128,128]{2,1,0:T(8,128)(2,1)S(1)}) custom-call(bf16[256,4096]{1,0:T(8,128)(2,1)S(1)} %copy-done, bf16[256,4096]{1,0:T(8,128)(2,1)S(1)} %collective-permute-done.13.theirs, bf16[256,512]{1,0:T(8,128)(2,1)S(1)} %copy-done.3, ...), custom_call_target="tpu_custom_call" | custom-call | flops 1073741824 | bytes 6291456 | tf_op jit(solution)/shard_map/pallas_call | solution.py:212
  19.0 0.6 collective-permute-start.15
  19.6 3.7 %collective-permute-start.5 = (bf16[8,128,128]{2,1,0:T(8,128)(2,1)S(1)}, bf16[8,128,128]{2,1,0:T(8,128)(2,1)S(1)}, u32[]{:S(2)}, u32[]{:S(2)}) collective-permute-start(bf16[8,128,128]{2,1,0:T(8,128)(2,1)S(1)} %shard_map.77.refs_0_), channel_id=1, source_target_pairs={{0,12},{1,13},{2,14},{3,15},{4,0},{5,1},{6,2},{7,3},{8,4},{9,5},{1... | collective-permute-start | bytes 786440 | tf_op jit(solution)/shard_map/ppermute | solution.py:206
  23.2 1.0 %collective-permute-start.3 = (bf16[8,128,128]{2,1,0:T(8,128)(2,1)S(1)}, bf16[8,128,128]{2,1,0:T(8,128)(2,1)S(1)}, u32[]{:S(2)}, u32[]{:S(2)}) collective-permute-start(bf16[8,128,128]{2,1,0:T(8,128)(2,1)S(1)} %shard_map.77.refs_0_), channel_id=1, source_target_pairs={{0,4},{1,5},{2,6},{3,7},{4,8},{5,9},{6,10},{7,11},{8,12},{9,13},{1... | collective-permute-start | bytes 786440 | tf_op jit(solution)/shard_map/ppermute | solution.py:206
  24.2 0.5 collective-permute-start.16
  24.7 5.2 %collective-permute-done.5.refs_3_ = bf16[8,128,128]{2,1,0:T(8,128)(2,1)S(1)} collective-permute-done((bf16[8,128,128]{2,1,0:T(8,128)(2,1)S(1)}, bf16[8,128,128]{2,1,0:T(8,128)(2,1)S(1)}, u32[]{:S(2)}, u32[]{:S(2)}) %collective-permute-start.5) | collective-permute-done | bytes 262176 | tf_op jit(solution)/shard_map/ppermute | solution.py:206
  30.0 1.4 %collective-permute-start.17 = (bf16[16,128,128]{2,1,0:T(8,128)(2,1)S(1)}, bf16[16,128,128]{2,1,0:T(8,128)(2,1)S(1)}, u32[]{:S(2)}, u32[]{:S(2)}) collective-permute-start(bf16[16,128,128]{2,1,0:T(8,128)(2,1)S(1)} %get-tuple-element.30), channel_id=1, source_target_pairs={{0,3},{1,2},{2,1},{3,0},{4,7},{5,6},{6,5},{7,4},{8,11},{9,10},{10,... | collective-permute-start | bytes 1572872 | tf_op jit(solution)/shard_map/ppermute | solution.py:202
  31.4 12.6 %collective-permute-done.4.refs_2_ = bf16[8,128,128]{2,1,0:T(8,128)(2,1)S(1)} collective-permute-done((bf16[8,128,128]{2,1,0:T(8,128)(2,1)S(1)}, bf16[8,128,128]{2,1,0:T(8,128)(2,1)S(1)}, u32[]{:S(2)}, u32[]{:S(2)}) %collective-permute-start.4) | collective-permute-done | bytes 262176 | tf_op jit(solution)/shard_map/ppermute | solution.py:206
  44.0 1.1 %shard_map.78.refs_0_ = bf16[16,128,128]{2,1,0:T(8,128)(2,1)S(1)} custom-call(s32[16]{0:T(128)S(1)} %copy-done.6, bf16[8,128,128]{2,1,0:T(8,128)(2,1)S(1)} %shard_map.77.refs_0_, bf16[8,128,128]{2,1,0:T(8,128)(2,1)S(1)} %collective-permute-done.3.refs_1_, bf16[8,128,128]{2,1,0:T(8,128)(2,1)S(1)} %collective-permute-done.4.refs_2_, ...), custom_call_target="tpu_custom_call" | custom-call | flops 1048576 | bytes 1572864 | tf_op jit(solution)/shard_map/pallas_call | solution.py:212
  45.1 1.4 %collective-permute-start.8 = (bf16[16,128,128]{2,1,0:T(8,128)(2,1)S(1)}, bf16[16,128,128]{2,1,0:T(8,128)(2,1)S(1)}, u32[]{:S(2)}, u32[]{:S(2)}) collective-permute-start(bf16[16,128,128]{2,1,0:T(8,128)(2,1)S(1)} %shard_map.78.refs_0_), channel_id=1, source_target_pairs={{0,3},{1,2},{2,1},{3,0},{4,7},{5,6},{6,5},{7,4},{8,11},{9,10},{10,... | collective-permute-start | bytes 1572872 | tf_op jit(solution)/shard_map/ppermute | solution.py:202
  46.5 1.5 %collective-permute-start.7 = (bf16[16,128,128]{2,1,0:T(8,128)(2,1)S(1)}, bf16[16,128,128]{2,1,0:T(8,128)(2,1)S(1)}, u32[]{:S(2)}, u32[]{:S(2)}) collective-permute-start(bf16[16,128,128]{2,1,0:T(8,128)(2,1)S(1)} %shard_map.78.refs_0_), channel_id=1, source_target_pairs={{0,2},{1,3},{2,0},{3,1},{4,6},{5,7},{6,4},{7,5},{8,10},{9,11},{10,... | collective-permute-start | bytes 1572872 | tf_op jit(solution)/shard_map/ppermute | solution.py:202
  48.0 0.7 collective-permute-start.6
  48.6 7.0 %collective-permute-done.16.refs_2_ = bf16[16,128,128]{2,1,0:T(8,128)(2,1)S(1)} collective-permute-done((bf16[16,128,128]{2,1,0:T(8,128)(2,1)S(1)}, bf16[16,128,128]{2,1,0:T(8,128)(2,1)S(1)}, u32[]{:S(2)}, u32[]{:S(2)}) %collective-permute-start.16) | collective-permute-done | bytes 524320 | tf_op jit(solution)/shard_map/ppermute | solution.py:202
  55.6 1.0 %shard_map.81 = (bf16[8,128,128]{2,1,0:T(8,128)(2,1)S(1)}, bf16[8,128,128]{2,1,0:T(8,128)(2,1)S(1)}, bf16[8,128,128]{2,1,0:T(8,128)(2,1)S(1)}, bf16[8,128,128]{2,1,0:T(8,128)(2,1)S(1)}) custom-call(s32[16]{0:T(128)S(1)} %copy-done.6, bf16[16,128,128]{2,1,0:T(8,128)(2,1)S(1)} %get-tuple-element.27.refs_0_, ...), custom_call_target="tpu_custom_call" | custom-call | flops 2097152 | bytes 3145728 | tf_op jit(solution)/shard_map/pallas_call | solution.py:212
  56.7 0.1 collective-permute-start.18
  56.8 9.2 %collective-permute-start.19 = (bf16[8,128,128]{2,1,0:T(8,128)(2,1)S(1)}, bf16[8,128,128]{2,1,0:T(8,128)(2,1)S(1)}, u32[]{:S(2)}, u32[]{:S(2)}) collective-permute-start(bf16[8,128,128]{2,1,0:T(8,128)(2,1)S(1)} %get-tuple-element.33), channel_id=1, source_target_pairs={{0,8},{1,9},{2,10},{3,11},{4,12},{5,13},{6,14},{7,15},{8,0},{9,1},... | collective-permute-start | bytes 786440 | tf_op jit(solution)/shard_map/ppermute | solution.py:206
  66.0 3.2 %collective-permute-done.7.refs_2_ = bf16[16,128,128]{2,1,0:T(8,128)(2,1)S(1)} collective-permute-done((bf16[16,128,128]{2,1,0:T(8,128)(2,1)S(1)}, bf16[16,128,128]{2,1,0:T(8,128)(2,1)S(1)}, u32[]{:S(2)}, u32[]{:S(2)}) %collective-permute-start.7) | collective-permute-done | bytes 524320 | tf_op jit(solution)/shard_map/ppermute | solution.py:202
  69.2 0.5 collective-permute-start.11
  69.7 0.1 collective-permute-done.18.refs_1_
  69.9 5.5 %collective-permute-done.19.refs_2_ = bf16[8,128,128]{2,1,0:T(8,128)(2,1)S(1)} collective-permute-done((bf16[8,128,128]{2,1,0:T(8,128)(2,1)S(1)}, bf16[8,128,128]{2,1,0:T(8,128)(2,1)S(1)}, u32[]{:S(2)}, u32[]{:S(2)}) %collective-permute-start.19) | collective-permute-done | bytes 262176 | tf_op jit(solution)/shard_map/ppermute | solution.py:206
  75.4 0.2 collective-permute-start.20
  75.6 6.1 %collective-permute-done.20.refs_3_ = bf16[8,128,128]{2,1,0:T(8,128)(2,1)S(1)} collective-permute-done((bf16[8,128,128]{2,1,0:T(8,128)(2,1)S(1)}, bf16[8,128,128]{2,1,0:T(8,128)(2,1)S(1)}, u32[]{:S(2)}, u32[]{:S(2)}) %collective-permute-start.20) | collective-permute-done | bytes 262176 | tf_op jit(solution)/shard_map/ppermute | solution.py:206
  81.8 0.8 shard_map.82
  82.6 1.6 %collective-permute-start.21 = (bf16[2,128,128]{2,1,0:T(8,128)(2,1)S(1)}, bf16[2,128,128]{2,1,0:T(8,128)(2,1)S(1)}, u32[]{:S(2)}, u32[]{:S(2)}) collective-permute-start(bf16[2,128,128]{2,1,0:T(8,128)(2,1)S(1)} %get-tuple-element.36), channel_id=1, source_target_pairs={{0,1},{1,0},{2,3},{3,2},{4,5},{5,4},{6,7},{7,6},{8,9},{9,8},{10,11... | collective-permute-start | bytes 196616 | tf_op jit(solution)/shard_map/ppermute | solution.py:202
  84.1 0.5 collective-permute-start.22
  84.6 1.5 %collective-permute-start.23 = (bf16[2,128,128]{2,1,0:T(8,128)(2,1)S(1)}, bf16[2,128,128]{2,1,0:T(8,128)(2,1)S(1)}, u32[]{:S(2)}, u32[]{:S(2)}) collective-permute-start(bf16[2,128,128]{2,1,0:T(8,128)(2,1)S(1)} %get-tuple-element.38), channel_id=1, source_target_pairs={{0,3},{1,2},{2,1},{3,0},{4,7},{5,6},{6,5},{7,4},{8,11},{9,10},{10,... | collective-permute-start | bytes 196616 | tf_op jit(solution)/shard_map/ppermute | solution.py:202
  86.1 0.8 collective-permute-done.21.refs_1_
  86.9 1.5 %collective-permute-done.22.refs_2_ = bf16[2,128,128]{2,1,0:T(8,128)(2,1)S(1)} collective-permute-done((bf16[2,128,128]{2,1,0:T(8,128)(2,1)S(1)}, bf16[2,128,128]{2,1,0:T(8,128)(2,1)S(1)}, u32[]{:S(2)}, u32[]{:S(2)}) %collective-permute-start.22) | collective-permute-done | bytes 65568 | tf_op jit(solution)/shard_map/ppermute | solution.py:202
  88.4 1.4 %collective-permute-done.23.refs_3_ = bf16[2,128,128]{2,1,0:T(8,128)(2,1)S(1)} collective-permute-done((bf16[2,128,128]{2,1,0:T(8,128)(2,1)S(1)}, bf16[2,128,128]{2,1,0:T(8,128)(2,1)S(1)}, u32[]{:S(2)}, u32[]{:S(2)}) %collective-permute-start.23) | collective-permute-done | bytes 65568 | tf_op jit(solution)/shard_map/ppermute | solution.py:202
  89.8 4.9 %shard_map.79 = (bf16[256,512]{1,0:T(8,128)(2,1)}, bf16[256,4096]{1,0:T(8,128)(2,1)}) custom-call(bf16[256,4096]{1,0:T(8,128)(2,1)S(1)} %copy-done.1, bf16[256,512]{1,0:T(8,128)(2,1)S(1)} %copy-done.4, bf16[16,128,128]{2,1,0:T(8,128)(2,1)S(1)} %shard_map.78.refs_0_, bf16[16,128,128]{2,1,0:T(8,128)(2,1)S(1)} %collective-permute-done.6.refs_1_, ...), custom_call_target="tpu_custom_call" | custom-call | flops 2147483648 | bytes 12582912 | tf_op jit(solution)/shard_map/pallas_call | solution.py:212
  94.7 1.5 %shard_map.83 = bf16[16,128,128]{2,1,0:T(8,128)(2,1)} custom-call(s32[16]{0:T(128)S(1)} %copy-done.6, bf16[2,128,128]{2,1,0:T(8,128)(2,1)S(1)} %get-tuple-element.35.refs_0_, bf16[2,128,128]{2,1,0:T(8,128)(2,1)S(1)} %collective-permute-done.21.refs_1_, bf16[2,128,128]{2,1,0:T(8,128)(2,1)S(1)} %collective-permute-done.22.refs_2_, ...), custom_call_target="tpu_custom_call" | custom-call | flops 524288 | bytes 1048576 | tf_op jit(solution)/shard_map/pallas_call | solution.py:212
  (32 shorter events, 0.1 us)
Async XLA Ops:
  0.6 13.3 %collective-permute-start.13 = (bf16[256,4096]{1,0:T(8,128)(2,1)}, bf16[256,4096]{1,0:T(8,128)(2,1)S(1)}, u32[]{:S(2)}, u32[]{:S(2)}) collective-permute-start(bf16[256,4096]{1,0:T(8,128)(2,1)} %mine.1), channel_id=1, source_target_pairs={{0,16},{16,0},{1,17},{17,1},{2,18},{18,2},{3,19},{19,3},{4,20},{20... | collective-permute-start | bytes 6291464 | tf_op jit(solution)/shard_map/ppermute | solution.py:209
  1.2 12.8 %collective-permute-start.14 = (bf16[256,512]{1,0:T(8,128)(2,1)}, bf16[256,512]{1,0:T(8,128)(2,1)S(1)}, u32[]{:S(2)}, u32[]{:S(2)}) collective-permute-start(bf16[256,512]{1,0:T(8,128)(2,1)} %cot_mine.1), channel_id=1, source_target_pairs={{0,16},{16,0},{1,17},{17,1},{2,18},{18,2},{3,19},{19,3},{4,20},{20... | collective-permute-start | bytes 786440 | tf_op jit(solution)/shard_map/ppermute | solution.py:209
  1.3 1.0 %copy-start.2 = (bf16[16,128,128]{2,1,0:T(8,128)(2,1)S(1)}, bf16[16,128,128]{2,1,0:T(8,128)(2,1)}, u32[]{:S(2)}) copy-start(bf16[16,128,128]{2,1,0:T(8,128)(2,1)} %codes.1) | copy-start | bytes 1572868
  2.3 0.7 copy-start.5
  3.0 0.7 copy-start.7
  4.2 5.3 %collective-permute-start = (bf16[2,128,128]{2,1,0:T(8,128)(2,1)S(1)}, bf16[2,128,128]{2,1,0:T(8,128)(2,1)S(1)}, u32[]{:S(2)}, u32[]{:S(2)}) collective-permute-start(bf16[2,128,128]{2,1,0:T(8,128)(2,1)S(1)} %get-tuple-element.22), channel_id=1, source_target_pairs={{0,1},{1,0},{2,3},{3,2},{4,5},{5,4},{6,7},{7,6},{8,9},{9,8},{10,11... | collective-permute-start | bytes 196616 | tf_op jit(solution)/shard_map/ppermute | solution.py:202
  7.2 4.3 %collective-permute-start.1 = (bf16[2,128,128]{2,1,0:T(8,128)(2,1)S(1)}, bf16[2,128,128]{2,1,0:T(8,128)(2,1)S(1)}, u32[]{:S(2)}, u32[]{:S(2)}) collective-permute-start(bf16[2,128,128]{2,1,0:T(8,128)(2,1)S(1)} %get-tuple-element.23), channel_id=1, source_target_pairs={{0,2},{1,3},{2,0},{3,1},{4,6},{5,7},{6,4},{7,5},{8,10},{9,11},{10,... | collective-permute-start | bytes 196616 | tf_op jit(solution)/shard_map/ppermute | solution.py:202
  8.7 5.2 %collective-permute-start.2 = (bf16[2,128,128]{2,1,0:T(8,128)(2,1)S(1)}, bf16[2,128,128]{2,1,0:T(8,128)(2,1)S(1)}, u32[]{:S(2)}, u32[]{:S(2)}) collective-permute-start(bf16[2,128,128]{2,1,0:T(8,128)(2,1)S(1)} %get-tuple-element.24), channel_id=1, source_target_pairs={{0,3},{1,2},{2,1},{3,0},{4,7},{5,6},{6,5},{7,4},{8,11},{9,10},{10,... | collective-permute-start | bytes 196616 | tf_op jit(solution)/shard_map/ppermute | solution.py:202
  13.9 30.1 %copy-start.6 = (s32[16]{0:T(128)S(1)}, s32[16]{0:T(128)}, u32[]{:S(2)}) copy-start(s32[16]{0:T(128)} %counts.9) | copy-start | bytes 196
  14.0 1.6 %copy-start = (bf16[256,4096]{1,0:T(8,128)(2,1)S(1)}, bf16[256,4096]{1,0:T(8,128)(2,1)}, u32[]{:S(2)}) copy-start(bf16[256,4096]{1,0:T(8,128)(2,1)} %mine.1) | copy-start | bytes 6291460
  15.6 0.9 copy-start.3
  19.0 29.0 %collective-permute-start.15 = (bf16[16,128,128]{2,1,0:T(8,128)(2,1)S(1)}, bf16[16,128,128]{2,1,0:T(8,128)(2,1)S(1)}, u32[]{:S(2)}, u32[]{:S(2)}) collective-permute-start(bf16[16,128,128]{2,1,0:T(8,128)(2,1)S(1)} %get-tuple-element.28), channel_id=1, source_target_pairs={{0,1},{1,0},{2,3},{3,2},{4,5},{5,4},{6,7},{7,6},{8,9},{9,8},{10,11... | collective-permute-start | bytes 1572872 | tf_op jit(solution)/shard_map/ppermute | solution.py:202
  19.6 10.4 %collective-permute-start.5 = (bf16[8,128,128]{2,1,0:T(8,128)(2,1)S(1)}, bf16[8,128,128]{2,1,0:T(8,128)(2,1)S(1)}, u32[]{:S(2)}, u32[]{:S(2)}) collective-permute-start(bf16[8,128,128]{2,1,0:T(8,128)(2,1)S(1)} %shard_map.77.refs_0_), channel_id=1, source_target_pairs={{0,12},{1,13},{2,14},{3,15},{4,0},{5,1},{6,2},{7,3},{8,4},{9,5},{1... | collective-permute-start | bytes 786440 | tf_op jit(solution)/shard_map/ppermute | solution.py:206
  23.2 20.7 %collective-permute-start.4 = (bf16[8,128,128]{2,1,0:T(8,128)(2,1)S(1)}, bf16[8,128,128]{2,1,0:T(8,128)(2,1)S(1)}, u32[]{:S(2)}, u32[]{:S(2)}) collective-permute-start(bf16[8,128,128]{2,1,0:T(8,128)(2,1)S(1)} %shard_map.77.refs_0_), channel_id=1, source_target_pairs={{0,8},{1,9},{2,10},{3,11},{4,12},{5,13},{6,14},{7,15},{8,0},{9,1},... | collective-permute-start | bytes 786440 | tf_op jit(solution)/shard_map/ppermute | solution.py:206
  23.2 20.7 %collective-permute-start.3 = (bf16[8,128,128]{2,1,0:T(8,128)(2,1)S(1)}, bf16[8,128,128]{2,1,0:T(8,128)(2,1)S(1)}, u32[]{:S(2)}, u32[]{:S(2)}) collective-permute-start(bf16[8,128,128]{2,1,0:T(8,128)(2,1)S(1)} %shard_map.77.refs_0_), channel_id=1, source_target_pairs={{0,4},{1,5},{2,6},{3,7},{4,8},{5,9},{6,10},{7,11},{8,12},{9,13},{1... | collective-permute-start | bytes 786440 | tf_op jit(solution)/shard_map/ppermute | solution.py:206
  24.2 31.4 %collective-permute-start.16 = (bf16[16,128,128]{2,1,0:T(8,128)(2,1)S(1)}, bf16[16,128,128]{2,1,0:T(8,128)(2,1)S(1)}, u32[]{:S(2)}, u32[]{:S(2)}) collective-permute-start(bf16[16,128,128]{2,1,0:T(8,128)(2,1)S(1)} %get-tuple-element.29), channel_id=1, source_target_pairs={{0,2},{1,3},{2,0},{3,1},{4,6},{5,7},{6,4},{7,5},{8,10},{9,11},{10,... | collective-permute-start | bytes 1572872 | tf_op jit(solution)/shard_map/ppermute | solution.py:202
  30.0 59.8 %copy-start.1 = (bf16[256,4096]{1,0:T(8,128)(2,1)S(1)}, bf16[256,4096]{1,0:T(8,128)(2,1)}, u32[]{:S(2)}) copy-start(bf16[256,4096]{1,0:T(8,128)(2,1)} %mine.1) | copy-start | bytes 6291460
  30.0 59.8 %copy-start.4 = (bf16[256,512]{1,0:T(8,128)(2,1)S(1)}, bf16[256,512]{1,0:T(8,128)(2,1)}, u32[]{:S(2)}) copy-start(bf16[256,512]{1,0:T(8,128)(2,1)} %cot_mine.1) | copy-start | bytes 786436
  30.0 25.7 %collective-permute-start.17 = (bf16[16,128,128]{2,1,0:T(8,128)(2,1)S(1)}, bf16[16,128,128]{2,1,0:T(8,128)(2,1)S(1)}, u32[]{:S(2)}, u32[]{:S(2)}) collective-permute-start(bf16[16,128,128]{2,1,0:T(8,128)(2,1)S(1)} %get-tuple-element.30), channel_id=1, source_target_pairs={{0,3},{1,2},{2,1},{3,0},{4,7},{5,6},{6,5},{7,4},{8,11},{9,10},{10,... | collective-permute-start | bytes 1572872 | tf_op jit(solution)/shard_map/ppermute | solution.py:202
  45.1 20.9 %collective-permute-start.8 = (bf16[16,128,128]{2,1,0:T(8,128)(2,1)S(1)}, bf16[16,128,128]{2,1,0:T(8,128)(2,1)S(1)}, u32[]{:S(2)}, u32[]{:S(2)}) collective-permute-start(bf16[16,128,128]{2,1,0:T(8,128)(2,1)S(1)} %shard_map.78.refs_0_), channel_id=1, source_target_pairs={{0,3},{1,2},{2,1},{3,0},{4,7},{5,6},{6,5},{7,4},{8,11},{9,10},{10,... | collective-permute-start | bytes 1572872 | tf_op jit(solution)/shard_map/ppermute | solution.py:202
  46.5 22.7 %collective-permute-start.7 = (bf16[16,128,128]{2,1,0:T(8,128)(2,1)S(1)}, bf16[16,128,128]{2,1,0:T(8,128)(2,1)S(1)}, u32[]{:S(2)}, u32[]{:S(2)}) collective-permute-start(bf16[16,128,128]{2,1,0:T(8,128)(2,1)S(1)} %shard_map.78.refs_0_), channel_id=1, source_target_pairs={{0,2},{1,3},{2,0},{3,1},{4,6},{5,7},{6,4},{7,5},{8,10},{9,11},{10,... | collective-permute-start | bytes 1572872 | tf_op jit(solution)/shard_map/ppermute | solution.py:202
  48.0 21.3 %collective-permute-start.6 = (bf16[16,128,128]{2,1,0:T(8,128)(2,1)S(1)}, bf16[16,128,128]{2,1,0:T(8,128)(2,1)S(1)}, u32[]{:S(2)}, u32[]{:S(2)}) collective-permute-start(bf16[16,128,128]{2,1,0:T(8,128)(2,1)S(1)} %shard_map.78.refs_0_), channel_id=1, source_target_pairs={{0,1},{1,0},{2,3},{3,2},{4,5},{5,4},{6,7},{7,6},{8,9},{9,8},{10,11... | collective-permute-start | bytes 1572872 | tf_op jit(solution)/shard_map/ppermute | solution.py:202
  56.7 13.2 %collective-permute-start.18 = (bf16[8,128,128]{2,1,0:T(8,128)(2,1)S(1)}, bf16[8,128,128]{2,1,0:T(8,128)(2,1)S(1)}, u32[]{:S(2)}, u32[]{:S(2)}) collective-permute-start(bf16[8,128,128]{2,1,0:T(8,128)(2,1)S(1)} %get-tuple-element.32), channel_id=1, source_target_pairs={{0,4},{1,5},{2,6},{3,7},{4,8},{5,9},{6,10},{7,11},{8,12},{9,13},{1... | collective-permute-start | bytes 786440 | tf_op jit(solution)/shard_map/ppermute | solution.py:206
  56.8 18.6 %collective-permute-start.19 = (bf16[8,128,128]{2,1,0:T(8,128)(2,1)S(1)}, bf16[8,128,128]{2,1,0:T(8,128)(2,1)S(1)}, u32[]{:S(2)}, u32[]{:S(2)}) collective-permute-start(bf16[8,128,128]{2,1,0:T(8,128)(2,1)S(1)} %get-tuple-element.33), channel_id=1, source_target_pairs={{0,8},{1,9},{2,10},{3,11},{4,12},{5,13},{6,14},{7,15},{8,0},{9,1},... | collective-permute-start | bytes 786440 | tf_op jit(solution)/shard_map/ppermute | solution.py:206
  66.0 18.1 %collective-permute-start.9 = (bf16[16,128,128]{2,1,0:T(8,128)(2,1)S(1)}, bf16[16,128,128]{2,1,0:T(8,128)(2,1)S(1)}, u32[]{:S(2)}, u32[]{:S(2)}) collective-permute-start(bf16[16,128,128]{2,1,0:T(8,128)(2,1)S(1)} %shard_map.78.refs_0_), channel_id=1, source_target_pairs={{0,16},{16,0},{1,17},{17,1},{2,18},{18,2},{3,19},{19,3},{4,20},{20... | collective-permute-start | bytes 1572872 | tf_op jit(solution)/shard_map/ppermute | solution.py:209
  69.2 15.4 %collective-permute-start.12 = (bf16[16,128,128]{2,1,0:T(8,128)(2,1)S(1)}, bf16[16,128,128]{2,1,0:T(8,128)(2,1)S(1)}, u32[]{:S(2)}, u32[]{:S(2)}) collective-permute-start(bf16[16,128,128]{2,1,0:T(8,128)(2,1)S(1)} %collective-permute-done.8.refs_3_), channel_id=1, source_target_pairs={{0,16},{16,0},{1,17},{17,1},{2,18},{18,2},{3,19},{19,3},{4,20},{20... | collective-permute-start | bytes 1572872 | tf_op jit(solution)/shard_map/ppermute | solution.py:209
  69.2 16.9 %collective-permute-start.11 = (bf16[16,128,128]{2,1,0:T(8,128)(2,1)S(1)}, bf16[16,128,128]{2,1,0:T(8,128)(2,1)S(1)}, u32[]{:S(2)}, u32[]{:S(2)}) collective-permute-start(bf16[16,128,128]{2,1,0:T(8,128)(2,1)S(1)} %collective-permute-done.7.refs_2_), channel_id=1, source_target_pairs={{0,16},{16,0},{1,17},{17,1},{2,18},{18,2},{3,19},{19,3},{4,20},{20... | collective-permute-start | bytes 1572872 | tf_op jit(solution)/shard_map/ppermute | solution.py:209
  69.9 19.9 %collective-permute-start.10 = (bf16[16,128,128]{2,1,0:T(8,128)(2,1)S(1)}, bf16[16,128,128]{2,1,0:T(8,128)(2,1)S(1)}, u32[]{:S(2)}, u32[]{:S(2)}) collective-permute-start(bf16[16,128,128]{2,1,0:T(8,128)(2,1)S(1)} %collective-permute-done.6.refs_1_), channel_id=1, source_target_pairs={{0,16},{16,0},{1,17},{17,1},{2,18},{18,2},{3,19},{19,3},{4,20},{20... | collective-permute-start | bytes 1572872 | tf_op jit(solution)/shard_map/ppermute | solution.py:209
  75.4 6.4 %collective-permute-start.20 = (bf16[8,128,128]{2,1,0:T(8,128)(2,1)S(1)}, bf16[8,128,128]{2,1,0:T(8,128)(2,1)S(1)}, u32[]{:S(2)}, u32[]{:S(2)}) collective-permute-start(bf16[8,128,128]{2,1,0:T(8,128)(2,1)S(1)} %get-tuple-element.34), channel_id=1, source_target_pairs={{0,12},{1,13},{2,14},{3,15},{4,0},{5,1},{6,2},{7,3},{8,4},{9,5},{1... | collective-permute-start | bytes 786440 | tf_op jit(solution)/shard_map/ppermute | solution.py:206
  82.6 4.3 %collective-permute-start.21 = (bf16[2,128,128]{2,1,0:T(8,128)(2,1)S(1)}, bf16[2,128,128]{2,1,0:T(8,128)(2,1)S(1)}, u32[]{:S(2)}, u32[]{:S(2)}) collective-permute-start(bf16[2,128,128]{2,1,0:T(8,128)(2,1)S(1)} %get-tuple-element.36), channel_id=1, source_target_pairs={{0,1},{1,0},{2,3},{3,2},{4,5},{5,4},{6,7},{7,6},{8,9},{9,8},{10,11... | collective-permute-start | bytes 196616 | tf_op jit(solution)/shard_map/ppermute | solution.py:202
  84.1 4.3 %collective-permute-start.22 = (bf16[2,128,128]{2,1,0:T(8,128)(2,1)S(1)}, bf16[2,128,128]{2,1,0:T(8,128)(2,1)S(1)}, u32[]{:S(2)}, u32[]{:S(2)}) collective-permute-start(bf16[2,128,128]{2,1,0:T(8,128)(2,1)S(1)} %get-tuple-element.37), channel_id=1, source_target_pairs={{0,2},{1,3},{2,0},{3,1},{4,6},{5,7},{6,4},{7,5},{8,10},{9,11},{10,... | collective-permute-start | bytes 196616 | tf_op jit(solution)/shard_map/ppermute | solution.py:202
  84.6 5.2 %collective-permute-start.23 = (bf16[2,128,128]{2,1,0:T(8,128)(2,1)S(1)}, bf16[2,128,128]{2,1,0:T(8,128)(2,1)S(1)}, u32[]{:S(2)}, u32[]{:S(2)}) collective-permute-start(bf16[2,128,128]{2,1,0:T(8,128)(2,1)S(1)} %get-tuple-element.38), channel_id=1, source_target_pairs={{0,3},{1,2},{2,1},{3,0},{4,7},{5,6},{6,5},{7,4},{8,11},{9,10},{10,... | collective-permute-start | bytes 196616 | tf_op jit(solution)/shard_map/ppermute | solution.py:202
  86.1 8.6 %collective-permute-start.24 = (bf16[2,128,128]{2,1,0:T(8,128)(2,1)S(1)}, bf16[2,128,128]{2,1,0:T(8,128)(2,1)S(1)}, u32[]{:S(2)}, u32[]{:S(2)}) collective-permute-start(bf16[2,128,128]{2,1,0:T(8,128)(2,1)S(1)} %get-tuple-element.35.refs_0_), channel_id=1, source_target_pairs={{0,16},{16,0},{1,17},{17,1},{2,18},{18,2},{3,19},{19,3},{4,20},{20... | collective-permute-start | bytes 196616 | tf_op jit(solution)/shard_map/ppermute | solution.py:209
  86.9 7.8 %collective-permute-start.25 = (bf16[2,128,128]{2,1,0:T(8,128)(2,1)S(1)}, bf16[2,128,128]{2,1,0:T(8,128)(2,1)S(1)}, u32[]{:S(2)}, u32[]{:S(2)}) collective-permute-start(bf16[2,128,128]{2,1,0:T(8,128)(2,1)S(1)} %collective-permute-done.21.refs_1_), channel_id=1, source_target_pairs={{0,16},{16,0},{1,17},{17,1},{2,18},{18,2},{3,19},{19,3},{4,20},{20... | collective-permute-start | bytes 196616 | tf_op jit(solution)/shard_map/ppermute | solution.py:209
  88.4 6.3 %collective-permute-start.26 = (bf16[2,128,128]{2,1,0:T(8,128)(2,1)S(1)}, bf16[2,128,128]{2,1,0:T(8,128)(2,1)S(1)}, u32[]{:S(2)}, u32[]{:S(2)}) collective-permute-start(bf16[2,128,128]{2,1,0:T(8,128)(2,1)S(1)} %collective-permute-done.22.refs_2_), channel_id=1, source_target_pairs={{0,16},{16,0},{1,17},{17,1},{2,18},{18,2},{3,19},{19,3},{4,20},{20... | collective-permute-start | bytes 196616 | tf_op jit(solution)/shard_map/ppermute | solution.py:209
  89.8 4.9 %collective-permute-start.27 = (bf16[2,128,128]{2,1,0:T(8,128)(2,1)S(1)}, bf16[2,128,128]{2,1,0:T(8,128)(2,1)S(1)}, u32[]{:S(2)}, u32[]{:S(2)}) collective-permute-start(bf16[2,128,128]{2,1,0:T(8,128)(2,1)S(1)} %collective-permute-done.23.refs_3_), channel_id=1, source_target_pairs={{0,16},{16,0},{1,17},{17,1},{2,18},{18,2},{3,19},{19,3},{4,20},{20... | collective-permute-start | bytes 196616 | tf_op jit(solution)/shard_map/ppermute | solution.py:209

commit v2 on v1

--- a/solution.py
+++ b/solution.py
@@ -32,14 +32,33 @@
     return lax.axis_index("dp"), me // INNER, me % INNER, me
 
 
-def spread_kernel(slots, reach, counts, scales, codes, *outs):
+def spread_kernel(slots, reach, counts_in, scales_in, codes_in, *refs):
+    (tokens_in, cot_in), (tokens, cot), outs = refs[:2], refs[2:4], refs[4 : 4 + INNER]
+    counts, scales, codes, done, wide_done = refs[4 + INNER :]
+    wide_loads = [
+        pltpu.make_async_copy(source, target, wide_done.at[n])
+        for n, (source, target) in enumerate(((tokens_in, tokens), (cot_in, cot)))
+    ]
+    loads = [
+        pltpu.make_async_copy(source, target, done.at[n])
+        for n, (source, target) in enumerate(
+            ((counts_in, counts), (scales_in, scales), (codes_in, codes))
+        )
+    ]
+    for load in loads + wide_loads:
+        load.start()
     core, _, place, me = here()
+    loads[0].wait()
     start = prefix(counts, me)
+    loads[1].wait()
+    loads[2].wait()
     for step, out in enumerate(outs):
         first = lead(class_of(core, place ^ step), start)
         for t in range(reach):
             slot = jnp.minimum(first + PERIOD * t, slots - 1)
             out[t] = (codes[slot].astype(jnp.float32) * scales[slot]).astype(BF16)
+    for load in wide_loads:
+        load.wait()
 
 
 def stack_kernel(reach, *refs):
@@ -49,9 +68,10 @@
 
 
 def class_kernel(planes, reach, counts, *refs):
-    ins, out, starts = refs[:planes], refs[planes], refs[planes + 1]
+    ins, outs, starts = refs[:planes], refs[planes:-1], refs[-1]
     core, plane, place, _ = here()
     cls = class_of(core, place)
+    per_out = outs[0].shape[0]
 
     def note(i, total):
         starts[i] = total
@@ -59,34 +79,44 @@
 
     lax.fori_loop(0, planes * INNER, note, jnp.int32(0))
     for shift, ref in enumerate(ins):
-        source = lax.rem(plane + planes - shift, planes)
+        source = plane ^ shift
         for m in range(INNER):
             owner = source * INNER + (place ^ m)
             first = lead(cls, starts[owner])
             for t in range(reach):
-
-                @pl.when(first + PERIOD * t < counts[owner])
-                def _(first=first, owner=owner, t=t, m=m, ref=ref):
-                    out[(starts[owner] + first) // PERIOD + t] = ref[m * reach + t]
-
-
-def grad_kernel(scale, tile, per_step, mine, theirs, cot_mine, cot_theirs, *refs):
+                j = (starts[owner] + first) // PERIOD + t
+                held = first + PERIOD * t < counts[owner]
+                for n, out in enumerate(outs):
+
+                    @pl.when(held & (j // per_out == n))
+                    def _(j=j, t=t, m=m, n=n, ref=ref, out=out):
+                        out[j - n * per_out] = ref[m * reach + t]
+
+
+def grad_kernel(scale, tile, chunks, mine, theirs, cot_mine, cot_theirs, *refs):
     outs, quad = refs[:INNER], refs[INNER]
     core, _, place, _ = here()
     half = cot_mine.shape[1] // 2
     columns = pl.ds(pl.multiple_of(core * half, half), half)
     left, right = cot_mine[:, columns], cot_theirs[:, columns]
-    for k in range(per_step):
-        rows = pl.ds(2 * tile * k, 2 * tile)
-        dims = (((0,), (0,)), ((), ()))
-        part = lax.dot_general(mine[:, rows], left, dims, preferred_element_type=jnp.float32)
-        part += lax.dot_general(theirs[:, rows], right, dims, preferred_element_type=jnp.float32)
-        quad[...] = part * scale
-        for m, out in enumerate(outs):
-            where = place ^ m
-            row = pl.multiple_of((where // 2) * tile, tile)
-            col = pl.multiple_of((where % 2) * tile, tile)
-            out[k] = quad[pl.ds(row, tile), pl.ds(col, tile)].astype(BF16)
+    wide = mine.shape[1] // chunks
+    per_chunk = wide // (2 * tile)
+    dims = (((0,), (0,)), ((), ()))
+
+    def chunk(i, carry):
+        for k in range(per_chunk):
+            rows = pl.ds(pl.multiple_of(i * wide + 2 * tile * k, 2 * tile), 2 * tile)
+            part = lax.dot_general(mine[:, rows], left, dims, preferred_element_type=jnp.float32)
+            part += lax.dot_general(theirs[:, rows], right, dims, preferred_element_type=jnp.float32)
+            quad[k] = part * scale
+            for m, out in enumerate(outs):
+                where = place ^ m
+                row = pl.multiple_of((where // 2) * tile, tile)
+                col = pl.multiple_of((where % 2) * tile, tile)
+                out[i * per_chunk + k] = quad[k, pl.ds(row, tile), pl.ds(col, tile)].astype(BF16)
+        return carry
+
+    lax.fori_loop(0, chunks, chunk, 0)
 
 
 def window(counts, cls, plane, blocks, span):
@@ -94,7 +124,7 @@
     return jnp.minimum((start + lead(cls, start)) // PERIOD, blocks - span)
 
 
-def plane_sum_kernel(planes, span, counts, *refs):
+def plane_sum_kernel(span, counts, *refs):
     ins, outs, total = refs[:INNER], refs[INNER:-1], refs[-1]
     core, plane, place, _ = here()
     cls = class_of(core, place)
@@ -105,7 +135,7 @@
             acc += ref[j].astype(jnp.float32)
         total[j] = acc.astype(BF16)
     for shift, out in enumerate(outs):
-        target = lax.rem(plane + shift, planes)
+        target = plane ^ shift
         out[...] = total[pl.ds(window(counts, cls, target, blocks, span), span)]
 
 
@@ -141,8 +171,10 @@
                 out[slot] = jnp.where(slot < count, value, jnp.zeros_like(value))
 
 
-def product_kernel(tile, per_step, tokens, cot, *refs):
-    pieces, projected, token_grad, weight, acc = refs[:-4], refs[-4], refs[-3], refs[-2], refs[-1]
+def product_kernel(tile, per_step, last, tokens, cot, *refs):
+    pieces, refs = refs[: 2 * INNER], refs[2 * INNER :]
+    before = refs[0] if last else None
+    projected, token_grad, weight, acc = refs[2:] if last else refs
     core, _, place, _ = here()
     step = pl.program_id(0)
     for n, ref in enumerate(pieces):
@@ -154,7 +186,7 @@
 
     @pl.when(step == 0)
     def _():
-        acc[...] = jnp.zeros_like(acc)
+        acc[...] = before[...] if last else jnp.zeros_like(acc)
 
     acc[...] += jnp.dot(tokens[...], weight[...], preferred_element_type=jnp.float32)
     token_grad[...] = lax.dot_general(
@@ -163,11 +195,19 @@
 
     @pl.when(step == pl.num_programs(0) - 1)
     def _():
-        projected[...] = acc[...].astype(BF16)
+        projected[...] = acc[...].astype(projected.dtype)
 
 
 def whole():
     return pl.BlockSpec(memory_space=VMEM)
+
+
+def far():
+    return pl.BlockSpec(memory_space=pl.ANY)
+
+
+def stays(value):
+    return pltpu.with_memory_space_constraint(value, pltpu.HBM)
 
 
 def scalars():
@@ -202,7 +242,7 @@
         return lax.ppermute(value, "fsdp", [(i, i ^ m) for i in range(owners)])
 
     def along(value, shift):
-        pairs = [(i, (i + shift * INNER) % owners) for i in range(owners)]
+        pairs = [(i, i ^ (shift * INNER)) for i in range(owners)]
         return lax.ppermute(value, "fsdp", pairs)
 
     def across(value):
@@ -213,29 +253,45 @@
 
     their_tokens, their_cot = across(tokens), across(cotangent)
 
-    spread = call(
+    my_tokens, my_cot, *spread = call(
         functools.partial(spread_kernel, slots, reach),
-        counts, scales, block_codes,
-        out_shape=[many(reach)] * INNER,
-        in_specs=[scalars(), scalars(), whole()],
-        out_specs=[whole()] * INNER,
+        stays(counts),
+        stays(scales),
+        stays(block_codes),
+        stays(tokens),
+        stays(cotangent),
+        out_shape=[
+            pltpu.VMEM((rows, width), BF16),
+            pltpu.VMEM((rows, key_width), BF16),
+        ]
+        + [many(reach)] * INNER,
+        in_specs=[far()] * 5,
+        out_specs=[far()] * 2 + [whole()] * INNER,
+        scratch_shapes=[
+            pltpu.SMEM((owners,), jnp.int32),
+            pltpu.SMEM((slots,), jnp.float32),
+            VMEM((slots, tile, tile), BF16),
+            pltpu.SemaphoreType.DMA((3,)),
+            pltpu.SemaphoreType.DMA((2,)),
+        ],
         cost_estimate=cost(8 * block_bytes, 24 * block_bytes),
         compiler_params=room(8),
     )
     near = [spread[0]] + [beside(spread[m], m) for m in range(1, INNER)]
 
-    per_step = 4
-    steps = blocks // per_step
-    wide = 2 * tile * per_step
+    chunks = 4
     grads = call(
-        functools.partial(grad_kernel, 1.0 / math.sqrt(total_tokens), tile, per_step),
-        tokens, their_tokens, cotangent, their_cot,
+        functools.partial(grad_kernel, 1.0 / math.sqrt(total_tokens), tile, chunks),
+        my_tokens,
+        their_tokens,
+        my_cot,
+        their_cot,
         out_shape=[many(blocks)] * INNER,
-        grid=(steps,),
-        in_specs=[pl.BlockSpec((rows, wide), lambda i: (0, i))] * 2
-        + [pl.BlockSpec((rows, key_width), lambda i: (0, 0))] * 2,
-        out_specs=[pl.BlockSpec((per_step, tile, tile), lambda i: (i, 0, 0))] * INNER,
-        scratch_shapes=[VMEM((2 * tile, 2 * tile), jnp.float32)],
+        in_specs=[whole()] * 4,
+        out_specs=[whole()] * INNER,
+        scratch_shapes=[
+            VMEM((width // (2 * tile * chunks), 2 * tile, 2 * tile), jnp.float32)
+        ],
         cost_estimate=cost(2 * rows * width * key_width, 6 * rows * width),
         compiler_params=room(20),
     )
@@ -252,20 +308,20 @@
     )
     held = [stacked] + [along(stacked, s) for s in range(1, planes)]
 
-    own_class = call(
+    own_classes = call(
         functools.partial(class_kernel, planes, reach),
-        counts, *held,
-        out_shape=many(blocks),
+        counts,
+        *held,
+        out_shape=[many(blocks // 2)] * 2,
         in_specs=[scalars()] + [whole()] * planes,
-        out_specs=whole(),
+        out_specs=[whole()] * 2,
         scratch_shapes=[pltpu.SMEM((owners,), jnp.int32)],
         cost_estimate=cost(32 * block_bytes, 48 * block_bytes),
         compiler_params=room(8),
     )
-    classes = [own_class] + [beside(own_class, m) for m in range(1, INNER)]
 
     windows = call(
-        functools.partial(plane_sum_kernel, planes, span),
+        functools.partial(plane_sum_kernel, span),
         counts, *parts,
         out_shape=[many(span)] * planes,
         in_specs=[scalars()] + [whole()] * INNER,
@@ -288,28 +344,40 @@
     )
     mine = [sent[0]] + [beside(sent[m], m) for m in range(1, INNER)]
 
-    all_classes = classes + [across(own_class)] + [across(c) for c in classes[1:]]
-    projected, token_grad = call(
-        functools.partial(product_kernel, tile, per_step),
-        tokens, cotangent, *all_classes,
-        out_shape=[
-            jax.ShapeDtypeStruct((rows, key_width), BF16),
-            jax.ShapeDtypeStruct((rows, width), BF16),
-        ],
-        grid=(steps,),
-        in_specs=[
-            pl.BlockSpec((rows, wide), lambda i: (0, i)),
-            pl.BlockSpec((rows, key_width), lambda i: (0, 0)),
-        ]
-        + [pl.BlockSpec((per_step, tile, tile), lambda i: (i, 0, 0))] * (2 * INNER),
-        out_specs=[
-            pl.BlockSpec((rows, key_width), lambda i: (0, 0)),
-            pl.BlockSpec((rows, wide), lambda i: (0, i)),
-        ],
-        scratch_shapes=[VMEM((wide, key_width), BF16), VMEM((rows, key_width), jnp.float32)],
-        cost_estimate=cost(4 * rows * width * key_width, 12 * rows * width),
-        compiler_params=room(28),
-    )
+    per_step = min(4, blocks // 2)
+    steps = blocks // 2 // per_step
+    wide = 2 * tile * per_step
+
+    def products(part, carried):
+        last = part == 1
+        base = part * steps
+        own = own_classes[part]
+        plane = [own] + [beside(own, m) for m in range(1, INNER)]
+        pieces = plane + [across(c) for c in plane]
+        square = pl.BlockSpec((rows, key_width), lambda i: (0, 0))
+        stripe = pl.BlockSpec((rows, wide), lambda i: (0, base + i))
+        return call(
+            functools.partial(product_kernel, tile, per_step, last),
+            my_tokens,
+            my_cot,
+            *pieces,
+            *carried,
+            out_shape=[
+                jax.ShapeDtypeStruct((rows, key_width), BF16 if last else jnp.float32),
+                jax.ShapeDtypeStruct((rows, width), BF16),
+            ],
+            grid=(steps,),
+            in_specs=[stripe, square]
+            + [pl.BlockSpec((per_step, tile, tile), lambda i: (i, 0, 0))] * (2 * INNER)
+            + ([square, pl.BlockSpec(memory_space=pl.ANY)] if last else []),
+            out_specs=[square, stripe],
+            input_output_aliases={2 * INNER + 3: 1} if last else {},
+            scratch_shapes=[VMEM((wide, key_width), BF16), VMEM((rows, key_width), jnp.float32)],
+            cost_estimate=cost(2 * rows * width * key_width, 6 * rows * width),
+            compiler_params=room(28),
+        )
+
+    projected, token_grad = products(1, products(0, ()))
 
     all_mine = mine + [across(v) for v in mine]
     block_grad = call(

time: 96.5 us -> 128 us (1.33); the launches traced: 96.2 us -> 125 us
  waiting for transfers between devices: 48.7 us -> 71.5 us
  starting transfers between devices: 29.5 us -> 38.6 us
  local copies, waits for them, and re-layouts: 4.9 us -> 0.01 us
  Pallas kernels: 12.4 us -> 14.6 us
    ppermute x12 -> x15, waiting for transfers between devices: 19 us -> 37.8 us  [beside(): return lax.ppermute(value, 'fsdp', [(i, i ^ m) for i in range(owners)])]
    unnamed x16 -> x4, local copies, waits for them, and re-layouts: 4.9 us -> 0.01 us
    ppermute x6, starting transfers between devices: 14.2 us -> 18.4 us  [along(): return lax.ppermute(value, 'fsdp', pairs)]
    ppermute x6, waiting for transfers between devices: 29.6 us -> 33.7 us  [along(): return lax.ppermute(value, 'fsdp', pairs)]
    ppermute x12 -> x15, starting transfers between devices: 14.1 us -> 17 us  [beside(): return lax.ppermute(value, 'fsdp', [(i, i ^ m) for i in range(owners)])]
    pallas_call x8 -> x9, Pallas kernels: 12.4 us -> 14.6 us  [call(): return pl.pallas_call(kernel, **how)(*operands)]
    ppermute x10 -> x14, starting transfers between devices: 1.16 us -> 3.18 us  [across(): return lax.ppermute(value, 'dp', [(0, 1), (1, 0)])]
  transfers between devices with their start and end apart: 28 -> 35, of which waited for: 13 -> 11; matrix products, arithmetic and copies ran while one was open for 0% -> 0% of each run, Pallas kernels for 9% -> 10%
where the time goes in v2:
time: 128 us; the launch traced here: 125 us
  waiting for transfers between devices  71.5 us (56%)
  starting transfers between devices  38.6 us (30%)
  Pallas kernels  14.6 us (11%)
    ppermute x15, waiting for transfers between devices, beside(): return lax.ppermute(value, 'fsdp', [(i, i ^ m) for i in range(owners)])  37.8 us
    ppermute x6, waiting for transfers between devices, along(): return lax.ppermute(value, 'fsdp', pairs)  33.7 us
    ppermute x6, starting transfers between devices, along(): return lax.ppermute(value, 'fsdp', pairs)  18.4 us
    ppermute x15, starting transfers between devices, beside(): return lax.ppermute(value, 'fsdp', [(i, i ^ m) for i in range(owners)])  17 us
    pallas_call x9, Pallas kernels, call(): return pl.pallas_call(kernel, **how)(*operands)  14.6 us
    ppermute x14, starting transfers between devices, across(): return lax.ppermute(value, 'dp', [(0, 1), (1, 0)])  3.18 us
  transfers between devices with their start and end apart: 35, of which 11 were waited for; matrix products, arithmetic and copies ran while one was open for 0% of the time, Pallas kernels for 10%

profile of v2, /device:TPU:0, one launch (start us, length us, event | category | flops | bytes accessed | tf_op | source)
XLA Modules:
  0.0 125.4 jit_solution(5674801430009419805)
XLA Ops:
  0.7 0.6 collective-permute-start.20
  1.2 1.8 %shard_map.76 = (bf16[256,4096]{1,0:T(8,128)(2,1)S(1)}, bf16[256,512]{1,0:T(8,128)(2,1)S(1)}, bf16[2,128,128]{2,1,0:T(8,128)(2,1)S(1)}, bf16[2,128,128]{2,1,0:T(...) custom-call(s32[16]{0:T(128)} %counts.7, f32[16]{0:T(128)} %scales_in.1, ...), custom_call_target="tpu_custom_call" | custom-call | flops 262144 | bytes 786432 | tf_op jit(solution)/shard_map/pallas_call | solution.py:252
  3.0 2.6 %collective-permute-start = (bf16[2,128,128]{2,1,0:T(8,128)(2,1)S(1)}, bf16[2,128,128]{2,1,0:T(8,128)(2,1)S(1)}, u32[]{:S(2)}, u32[]{:S(2)}) collective-permute-start(bf16[2,128,128]{2,1,0:T(8,128)(2,1)S(1)} %get-tuple-element.30), channel_id=1, source_target_pairs={{0,1},{1,0},{2,3},{3,2},{4,5},{5,4},{6,7},{7,6},{8,9},{9,8},{10,11... | collective-permute-start | bytes 196616 | tf_op jit(solution)/shard_map/ppermute | solution.py:242
  5.6 1.5 %collective-permute-start.1 = (bf16[2,128,128]{2,1,0:T(8,128)(2,1)S(1)}, bf16[2,128,128]{2,1,0:T(8,128)(2,1)S(1)}, u32[]{:S(2)}, u32[]{:S(2)}) collective-permute-start(bf16[2,128,128]{2,1,0:T(8,128)(2,1)S(1)} %get-tuple-element.31), channel_id=1, source_target_pairs={{0,2},{1,3},{2,0},{3,1},{4,6},{5,7},{6,4},{7,5},{8,10},{9,11},{10,... | collective-permute-start | bytes 196616 | tf_op jit(solution)/shard_map/ppermute | solution.py:242
  7.1 0.0 collective-permute-start.2
  7.1 1.2 collective-permute-done.refs_1_
  8.3 1.5 %collective-permute-done.1.refs_2_ = bf16[2,128,128]{2,1,0:T(8,128)(2,1)S(1)} collective-permute-done((bf16[2,128,128]{2,1,0:T(8,128)(2,1)S(1)}, bf16[2,128,128]{2,1,0:T(8,128)(2,1)S(1)}, u32[]{:S(2)}, u32[]{:S(2)}) %collective-permute-start.1) | collective-permute-done | bytes 65568 | tf_op jit(solution)/shard_map/ppermute | solution.py:242
  9.8 2.4 %collective-permute-done.2.refs_3_ = bf16[2,128,128]{2,1,0:T(8,128)(2,1)S(1)} collective-permute-done((bf16[2,128,128]{2,1,0:T(8,128)(2,1)S(1)}, bf16[2,128,128]{2,1,0:T(8,128)(2,1)S(1)}, u32[]{:S(2)}, u32[]{:S(2)}) %collective-permute-start.2) | collective-permute-done | bytes 65568 | tf_op jit(solution)/shard_map/ppermute | solution.py:242
  12.3 1.6 %collective-permute-start.3 = (bf16[8,128,128]{2,1,0:T(8,128)(2,1)S(1)}, bf16[8,128,128]{2,1,0:T(8,128)(2,1)S(1)}, u32[]{:S(2)}, u32[]{:S(2)}) collective-permute-start(bf16[8,128,128]{2,1,0:T(8,128)(2,1)S(1)} %shard_map.77.refs_0_), channel_id=1, source_target_pairs={{0,4},{1,5},{2,6},{3,7},{4,0},{5,1},{6,2},{7,3},{8,12},{9,13},{10,... | collective-permute-start | bytes 786440 | tf_op jit(solution)/shard_map/ppermute | solution.py:246
  13.9 2.6 %collective-permute-start.4 = (bf16[8,128,128]{2,1,0:T(8,128)(2,1)S(1)}, bf16[8,128,128]{2,1,0:T(8,128)(2,1)S(1)}, u32[]{:S(2)}, u32[]{:S(2)}) collective-permute-start(bf16[8,128,128]{2,1,0:T(8,128)(2,1)S(1)} %shard_map.77.refs_0_), channel_id=1, source_target_pairs={{0,8},{1,9},{2,10},{3,11},{4,12},{5,13},{6,14},{7,15},{8,0},{9,1},... | collective-permute-start | bytes 786440 | tf_op jit(solution)/shard_map/ppermute | solution.py:246
  16.5 0.2 collective-permute-start.5
  16.7 7.0 %collective-permute-done.3.refs_1_ = bf16[8,128,128]{2,1,0:T(8,128)(2,1)S(1)} collective-permute-done((bf16[8,128,128]{2,1,0:T(8,128)(2,1)S(1)}, bf16[8,128,128]{2,1,0:T(8,128)(2,1)S(1)}, u32[]{:S(2)}, u32[]{:S(2)}) %collective-permute-start.3) | collective-permute-done | bytes 262176 | tf_op jit(solution)/shard_map/ppermute | solution.py:246
  23.7 11.5 %collective-permute-done.4.refs_2_ = bf16[8,128,128]{2,1,0:T(8,128)(2,1)S(1)} collective-permute-done((bf16[8,128,128]{2,1,0:T(8,128)(2,1)S(1)}, bf16[8,128,128]{2,1,0:T(8,128)(2,1)S(1)}, u32[]{:S(2)}, u32[]{:S(2)}) %collective-permute-start.4) | collective-permute-done | bytes 262176 | tf_op jit(solution)/shard_map/ppermute | solution.py:246
  35.2 1.5 %shard_map.78 = (bf16[8,128,128]{2,1,0:T(8,128)(2,1)S(1)}, bf16[8,128,128]{2,1,0:T(8,128)(2,1)S(1)}) custom-call(s32[16]{0:T(128)S(1)} %copy-done, bf16[8,128,128]{2,1,0:T(8,128)(2,1)S(1)} %shard_map.77.refs_0_, bf16[8,128,128]{2,1,0:T(8,128)(2,1)S(1)} %collective-permute-done.3.refs_1_, bf16[8,128,128]{2,1,0:T(8,128)(2,1)S(1)} %collective-permute-done.4.refs_2_, ...), custom_call_target="tpu_custom_call" | custom-call | flops 1048576 | bytes 1572864 | tf_op jit(solution)/shard_map/pallas_call | solution.py:252
  36.8 0.6 collective-permute-start.6
  37.4 0.0 collective-permute-done.20.theirs
  37.4 2.2 %shard_map.81 = (bf16[16,128,128]{2,1,0:T(8,128)(2,1)S(1)}, bf16[16,128,128]{2,1,0:T(8,128)(2,1)S(1)}, bf16[16,128,128]{2,1,0:T(8,128)(2,1)S(1)}, bf16[16,128,128]{2,1,0:T(8,128)(2,1)S(1)}) custom-call(bf16[256,4096]{1,0:T(8,128)(2,1)S(1)} %get-tuple-element.27.tokens.mine, bf16[256,4096]{1,0:T(8,128)(2,1)S(1)} %collective-permute-done.20.theirs, ...), custom_call_target="tpu_custom_call" | custom-call | flops 1073741824 | bytes 6291456 | tf_op jit(solution)/shard_map/pallas_call | solution.py:252
  39.6 1.6 %collective-permute-start.22 = (bf16[16,128,128]{2,1,0:T(8,128)(2,1)S(1)}, bf16[16,128,128]{2,1,0:T(8,128)(2,1)S(1)}, u32[]{:S(2)}, u32[]{:S(2)}) collective-permute-start(bf16[16,128,128]{2,1,0:T(8,128)(2,1)S(1)} %get-tuple-element.40), channel_id=1, source_target_pairs={{0,1},{1,0},{2,3},{3,2},{4,5},{5,4},{6,7},{7,6},{8,9},{9,8},{10,11... | collective-permute-start | bytes 1572872 | tf_op jit(solution)/shard_map/ppermute | solution.py:242
  41.2 0.5 collective-permute-start.23
  41.7 1.5 %collective-permute-start.24 = (bf16[16,128,128]{2,1,0:T(8,128)(2,1)S(1)}, bf16[16,128,128]{2,1,0:T(8,128)(2,1)S(1)}, u32[]{:S(2)}, u32[]{:S(2)}) collective-permute-start(bf16[16,128,128]{2,1,0:T(8,128)(2,1)S(1)} %get-tuple-element.42), channel_id=1, source_target_pairs={{0,3},{1,2},{2,1},{3,0},{4,7},{5,6},{6,5},{7,4},{8,11},{9,10},{10,... | collective-permute-start | bytes 1572872 | tf_op jit(solution)/shard_map/ppermute | solution.py:242
  43.2 0.5 collective-permute-start.7
  43.7 2.3 %collective-permute-done.6.refs_1_ = bf16[8,128,128]{2,1,0:T(8,128)(2,1)S(1)} collective-permute-done((bf16[8,128,128]{2,1,0:T(8,128)(2,1)S(1)}, bf16[8,128,128]{2,1,0:T(8,128)(2,1)S(1)}, u32[]{:S(2)}, u32[]{:S(2)}) %collective-permute-start.6) | collective-permute-done | bytes 262176 | tf_op jit(solution)/shard_map/ppermute | solution.py:242
  46.0 0.5 collective-permute-start.8
  46.5 25.7 %collective-permute-done.7.refs_2_ = bf16[8,128,128]{2,1,0:T(8,128)(2,1)S(1)} collective-permute-done((bf16[8,128,128]{2,1,0:T(8,128)(2,1)S(1)}, bf16[8,128,128]{2,1,0:T(8,128)(2,1)S(1)}, u32[]{:S(2)}, u32[]{:S(2)}) %collective-permute-start.7) | collective-permute-done | bytes 262176 | tf_op jit(solution)/shard_map/ppermute | solution.py:242
  72.2 0.0 collective-permute-start.9
  72.2 0.0 collective-permute-done.8.refs_3_
  72.3 0.5 collective-permute-start.13
  72.8 0.7 collective-permute-start.14
  73.5 2.2 %collective-permute-start.15 = (bf16[8,128,128]{2,1,0:T(8,128)(2,1)S(1)}, bf16[8,128,128]{2,1,0:T(8,128)(2,1)S(1)}, u32[]{:S(2)}, u32[]{:S(2)}) collective-permute-start(bf16[8,128,128]{2,1,0:T(8,128)(2,1)S(1)} %get-tuple-element.34.refs_0_), channel_id=1, source_target_pairs={{0,3},{1,2},{2,1},{3,0},{4,7},{5,6},{6,5},{7,4},{8,11},{9,10},{10,... | collective-permute-start | bytes 786440 | tf_op jit(solution)/shard_map/ppermute | solution.py:242
  75.8 1.0 shard_map.82
  76.8 0.6 collective-permute-start.10
  77.4 4.0 %collective-permute-done.13.refs_1_ = bf16[8,128,128]{2,1,0:T(8,128)(2,1)S(1)} collective-permute-done((bf16[8,128,128]{2,1,0:T(8,128)(2,1)S(1)}, bf16[8,128,128]{2,1,0:T(8,128)(2,1)S(1)}, u32[]{:S(2)}, u32[]{:S(2)}) %collective-permute-start.13) | collective-permute-done | bytes 262176 | tf_op jit(solution)/shard_map/ppermute | solution.py:242
  81.4 6.1 %collective-permute-start.25 = (bf16[8,128,128]{2,1,0:T(8,128)(2,1)S(1)}, bf16[8,128,128]{2,1,0:T(8,128)(2,1)S(1)}, u32[]{:S(2)}, u32[]{:S(2)}) collective-permute-start(bf16[8,128,128]{2,1,0:T(8,128)(2,1)S(1)} %get-tuple-element.44), channel_id=1, source_target_pairs={{0,4},{1,5},{2,6},{3,7},{4,0},{5,1},{6,2},{7,3},{8,12},{9,13},{10,... | collective-permute-start | bytes 786440 | tf_op jit(solution)/shard_map/ppermute | solution.py:246
  87.6 6.6 %collective-permute-start.26 = (bf16[8,128,128]{2,1,0:T(8,128)(2,1)S(1)}, bf16[8,128,128]{2,1,0:T(8,128)(2,1)S(1)}, u32[]{:S(2)}, u32[]{:S(2)}) collective-permute-start(bf16[8,128,128]{2,1,0:T(8,128)(2,1)S(1)} %get-tuple-element.45), channel_id=1, source_target_pairs={{0,8},{1,9},{2,10},{3,11},{4,12},{5,13},{6,14},{7,15},{8,0},{9,1},... | collective-permute-start | bytes 786440 | tf_op jit(solution)/shard_map/ppermute | solution.py:246
  94.1 1.2 collective-permute-start.27
  95.4 0.5 collective-permute-start.18
  95.9 0.3 collective-permute-done.25.refs_1_
  96.1 14.9 %collective-permute-done.26.refs_2_ = bf16[8,128,128]{2,1,0:T(8,128)(2,1)S(1)} collective-permute-done((bf16[8,128,128]{2,1,0:T(8,128)(2,1)S(1)}, bf16[8,128,128]{2,1,0:T(8,128)(2,1)S(1)}, u32[]{:S(2)}, u32[]{:S(2)}) %collective-permute-start.26) | collective-permute-done | bytes 262176 | tf_op jit(solution)/shard_map/ppermute | solution.py:246
  111.0 0.5 collective-permute-start.12
  111.6 0.8 shard_map.83
  112.3 2.7 %collective-permute-start.28 = (bf16[2,128,128]{2,1,0:T(8,128)(2,1)S(1)}, bf16[2,128,128]{2,1,0:T(8,128)(2,1)S(1)}, u32[]{:S(2)}, u32[]{:S(2)}) collective-permute-start(bf16[2,128,128]{2,1,0:T(8,128)(2,1)S(1)} %get-tuple-element.48), channel_id=1, source_target_pairs={{0,1},{1,0},{2,3},{3,2},{4,5},{5,4},{6,7},{7,6},{8,9},{9,8},{10,11... | collective-permute-start | bytes 196616 | tf_op jit(solution)/shard_map/ppermute | solution.py:242
  115.1 1.5 %collective-permute-start.30 = (bf16[2,128,128]{2,1,0:T(8,128)(2,1)S(1)}, bf16[2,128,128]{2,1,0:T(8,128)(2,1)S(1)}, u32[]{:S(2)}, u32[]{:S(2)}) collective-permute-start(bf16[2,128,128]{2,1,0:T(8,128)(2,1)S(1)} %get-tuple-element.50), channel_id=1, source_target_pairs={{0,3},{1,2},{2,1},{3,0},{4,7},{5,6},{6,5},{7,4},{8,11},{9,10},{10,... | collective-permute-start | bytes 196616 | tf_op jit(solution)/shard_map/ppermute | solution.py:242
  116.6 2.8 %shard_map.79 = (f32[256,512]{1,0:T(8,128)S(1)}, bf16[256,4096]{1,0:T(8,128)(2,1)}) custom-call(bf16[256,4096]{1,0:T(8,128)(2,1)S(1)} %get-tuple-element.27.tokens.mine, bf16[256,512]{1,0:T(8,128)(2,1)S(1)} %get-tuple-element.28.cot.cot_mine, bf16[8,128,128]{2,1,0:T(8,128)(2,1)S(1)} %get-tuple-element.34.refs_0_, ...), custom_call_target="tpu_custom_call" | custom-call | flops 1073741824 | bytes 6291456 | tf_op jit(solution)/shard_map/pallas_call | solution.py:252
  119.5 0.5 collective-permute-start.32
  120.0 0.5 collective-permute-done.29.refs_2_
  120.5 0.5 collective-permute-start.34
  121.0 2.9 %shard_map.80 = (bf16[256,512]{1,0:T(8,128)(2,1)}, bf16[256,4096]{1,0:T(8,128)(2,1)}) custom-call(bf16[256,4096]{1,0:T(8,128)(2,1)S(1)} %get-tuple-element.27.tokens.mine, bf16[256,512]{1,0:T(8,128)(2,1)S(1)} %get-tuple-element.28.cot.cot_mine, bf16[8,128,128]{2,1,0:T(8,128)(2,1)S(1)} %get-tuple-element.33.refs_0_, ...), custom_call_target="tpu_custom_call", output_to_operand_aliasing={{1}: (11, {})} | custom-call | flops 1073741824 | bytes 6291456 | tf_op jit(solution)/shard_map/pallas_call | solution.py:252
  123.9 1.5 %shard_map.84 = bf16[16,128,128]{2,1,0:T(8,128)(2,1)} custom-call(s32[16]{0:T(128)S(1)} %copy-done, bf16[2,128,128]{2,1,0:T(8,128)(2,1)S(1)} %get-tuple-element.47.refs_0_, bf16[2,128,128]{2,1,0:T(8,128)(2,1)S(1)} %collective-permute-done.28.refs_1_, bf16[2,128,128]{2,1,0:T(8,128)(2,1)S(1)} %collective-permute-done.29.refs_2_, ...), custom_call_target="tpu_custom_call" | custom-call | flops 524288 | bytes 1048576 | tf_op jit(solution)/shard_map/pallas_call | solution.py:252
  (35 shorter events, 0.1 us)
Async XLA Ops:
  0.6 34.6 %copy-start = (s32[16]{0:T(128)S(1)}, s32[16]{0:T(128)}, u32[]{:S(2)}) copy-start(s32[16]{0:T(128)} %counts.7) | copy-start | bytes 196
  0.6 16.1 %copy-start.1 = (bf16[256,512]{1,0:T(8,128)(2,1)S(1)}, bf16[256,512]{1,0:T(8,128)(2,1)}, u32[]{:S(2)}) copy-start(bf16[256,512]{1,0:T(8,128)(2,1)} %refs_1_.1) | copy-start | bytes 786436
  0.7 36.7 %collective-permute-start.20 = (bf16[256,4096]{1,0:T(8,128)(2,1)}, bf16[256,4096]{1,0:T(8,128)(2,1)S(1)}, u32[]{:S(2)}, u32[]{:S(2)}) collective-permute-start(bf16[256,4096]{1,0:T(8,128)(2,1)} %refs_0_.1), channel_id=1, source_target_pairs={{0,16},{16,0},{1,17},{17,1},{2,18},{18,2},{3,19},{19,3},{4,20},{20... | collective-permute-start | bytes 6291464 | tf_op jit(solution)/shard_map/ppermute | solution.py:249
  3.0 5.3 %collective-permute-start = (bf16[2,128,128]{2,1,0:T(8,128)(2,1)S(1)}, bf16[2,128,128]{2,1,0:T(8,128)(2,1)S(1)}, u32[]{:S(2)}, u32[]{:S(2)}) collective-permute-start(bf16[2,128,128]{2,1,0:T(8,128)(2,1)S(1)} %get-tuple-element.30), channel_id=1, source_target_pairs={{0,1},{1,0},{2,3},{3,2},{4,5},{5,4},{6,7},{7,6},{8,9},{9,8},{10,11... | collective-permute-start | bytes 196616 | tf_op jit(solution)/shard_map/ppermute | solution.py:242
  5.6 4.3 %collective-permute-start.1 = (bf16[2,128,128]{2,1,0:T(8,128)(2,1)S(1)}, bf16[2,128,128]{2,1,0:T(8,128)(2,1)S(1)}, u32[]{:S(2)}, u32[]{:S(2)}) collective-permute-start(bf16[2,128,128]{2,1,0:T(8,128)(2,1)S(1)} %get-tuple-element.31), channel_id=1, source_target_pairs={{0,2},{1,3},{2,0},{3,1},{4,6},{5,7},{6,4},{7,5},{8,10},{9,11},{10,... | collective-permute-start | bytes 196616 | tf_op jit(solution)/shard_map/ppermute | solution.py:242
  7.1 5.2 %collective-permute-start.2 = (bf16[2,128,128]{2,1,0:T(8,128)(2,1)S(1)}, bf16[2,128,128]{2,1,0:T(8,128)(2,1)S(1)}, u32[]{:S(2)}, u32[]{:S(2)}) collective-permute-start(bf16[2,128,128]{2,1,0:T(8,128)(2,1)S(1)} %get-tuple-element.32), channel_id=1, source_target_pairs={{0,3},{1,2},{2,1},{3,0},{4,7},{5,6},{6,5},{7,4},{8,11},{9,10},{10,... | collective-permute-start | bytes 196616 | tf_op jit(solution)/shard_map/ppermute | solution.py:242
  12.3 11.4 %collective-permute-start.3 = (bf16[8,128,128]{2,1,0:T(8,128)(2,1)S(1)}, bf16[8,128,128]{2,1,0:T(8,128)(2,1)S(1)}, u32[]{:S(2)}, u32[]{:S(2)}) collective-permute-start(bf16[8,128,128]{2,1,0:T(8,128)(2,1)S(1)} %shard_map.77.refs_0_), channel_id=1, source_target_pairs={{0,4},{1,5},{2,6},{3,7},{4,0},{5,1},{6,2},{7,3},{8,12},{9,13},{10,... | collective-permute-start | bytes 786440 | tf_op jit(solution)/shard_map/ppermute | solution.py:246
  13.9 21.3 %collective-permute-start.4 = (bf16[8,128,128]{2,1,0:T(8,128)(2,1)S(1)}, bf16[8,128,128]{2,1,0:T(8,128)(2,1)S(1)}, u32[]{:S(2)}, u32[]{:S(2)}) collective-permute-start(bf16[8,128,128]{2,1,0:T(8,128)(2,1)S(1)} %shard_map.77.refs_0_), channel_id=1, source_target_pairs={{0,8},{1,9},{2,10},{3,11},{4,12},{5,13},{6,14},{7,15},{8,0},{9,1},... | collective-permute-start | bytes 786440 | tf_op jit(solution)/shard_map/ppermute | solution.py:246
  16.5 18.7 %collective-permute-start.5 = (bf16[8,128,128]{2,1,0:T(8,128)(2,1)S(1)}, bf16[8,128,128]{2,1,0:T(8,128)(2,1)S(1)}, u32[]{:S(2)}, u32[]{:S(2)}) collective-permute-start(bf16[8,128,128]{2,1,0:T(8,128)(2,1)S(1)} %shard_map.77.refs_0_), channel_id=1, source_target_pairs={{0,12},{1,13},{2,14},{3,15},{4,8},{5,9},{6,10},{7,11},{8,4},{9,5},... | collective-permute-start | bytes 786440 | tf_op jit(solution)/shard_map/ppermute | solution.py:246
  16.7 20.7 %collective-permute-start.21 = (bf16[256,512]{1,0:T(8,128)(2,1)S(1)}, bf16[256,512]{1,0:T(8,128)(2,1)S(1)}, u32[]{:S(2)}, u32[]{:S(2)}) collective-permute-start(bf16[256,512]{1,0:T(8,128)(2,1)S(1)} %copy-done.1), channel_id=1, source_target_pairs={{0,16},{16,0},{1,17},{17,1},{2,18},{18,2},{3,19},{19,3},{4,20},{20... | collective-permute-start | bytes 786440 | tf_op jit(solution)/shard_map/ppermute | solution.py:249
  36.8 9.2 %collective-permute-start.6 = (bf16[8,128,128]{2,1,0:T(8,128)(2,1)S(1)}, bf16[8,128,128]{2,1,0:T(8,128)(2,1)S(1)}, u32[]{:S(2)}, u32[]{:S(2)}) collective-permute-start(bf16[8,128,128]{2,1,0:T(8,128)(2,1)S(1)} %get-tuple-element.33.refs_0_), channel_id=1, source_target_pairs={{0,1},{1,0},{2,3},{3,2},{4,5},{5,4},{6,7},{7,6},{8,9},{9,8},{10,11... | collective-permute-start | bytes 786440 | tf_op jit(solution)/shard_map/ppermute | solution.py:242
  39.6 33.2 %collective-permute-start.22 = (bf16[16,128,128]{2,1,0:T(8,128)(2,1)S(1)}, bf16[16,128,128]{2,1,0:T(8,128)(2,1)S(1)}, u32[]{:S(2)}, u32[]{:S(2)}) collective-permute-start(bf16[16,128,128]{2,1,0:T(8,128)(2,1)S(1)} %get-tuple-element.40), channel_id=1, source_target_pairs={{0,1},{1,0},{2,3},{3,2},{4,5},{5,4},{6,7},{7,6},{8,9},{9,8},{10,11... | collective-permute-start | bytes 1572872 | tf_op jit(solution)/shard_map/ppermute | solution.py:242
  41.2 32.3 %collective-permute-start.23 = (bf16[16,128,128]{2,1,0:T(8,128)(2,1)S(1)}, bf16[16,128,128]{2,1,0:T(8,128)(2,1)S(1)}, u32[]{:S(2)}, u32[]{:S(2)}) collective-permute-start(bf16[16,128,128]{2,1,0:T(8,128)(2,1)S(1)} %get-tuple-element.41), channel_id=1, source_target_pairs={{0,2},{1,3},{2,0},{3,1},{4,6},{5,7},{6,4},{7,5},{8,10},{9,11},{10,... | collective-permute-start | bytes 1572872 | tf_op jit(solution)/shard_map/ppermute | solution.py:242
  41.7 34.1 %collective-permute-start.24 = (bf16[16,128,128]{2,1,0:T(8,128)(2,1)S(1)}, bf16[16,128,128]{2,1,0:T(8,128)(2,1)S(1)}, u32[]{:S(2)}, u32[]{:S(2)}) collective-permute-start(bf16[16,128,128]{2,1,0:T(8,128)(2,1)S(1)} %get-tuple-element.42), channel_id=1, source_target_pairs={{0,3},{1,2},{2,1},{3,0},{4,7},{5,6},{6,5},{7,4},{8,11},{9,10},{10,... | collective-permute-start | bytes 1572872 | tf_op jit(solution)/shard_map/ppermute | solution.py:242
  43.2 29.1 %collective-permute-start.7 = (bf16[8,128,128]{2,1,0:T(8,128)(2,1)S(1)}, bf16[8,128,128]{2,1,0:T(8,128)(2,1)S(1)}, u32[]{:S(2)}, u32[]{:S(2)}) collective-permute-start(bf16[8,128,128]{2,1,0:T(8,128)(2,1)S(1)} %get-tuple-element.33.refs_0_), channel_id=1, source_target_pairs={{0,2},{1,3},{2,0},{3,1},{4,6},{5,7},{6,4},{7,5},{8,10},{9,11},{10,... | collective-permute-start | bytes 786440 | tf_op jit(solution)/shard_map/ppermute | solution.py:242
  46.0 26.2 %collective-permute-start.8 = (bf16[8,128,128]{2,1,0:T(8,128)(2,1)S(1)}, bf16[8,128,128]{2,1,0:T(8,128)(2,1)S(1)}, u32[]{:S(2)}, u32[]{:S(2)}) collective-permute-start(bf16[8,128,128]{2,1,0:T(8,128)(2,1)S(1)} %get-tuple-element.33.refs_0_), channel_id=1, source_target_pairs={{0,3},{1,2},{2,1},{3,0},{4,7},{5,6},{6,5},{7,4},{8,11},{9,10},{10,... | collective-permute-start | bytes 786440 | tf_op jit(solution)/shard_map/ppermute | solution.py:242
  72.2 4.6 %collective-permute-start.9 = (bf16[8,128,128]{2,1,0:T(8,128)(2,1)S(1)}, bf16[8,128,128]{2,1,0:T(8,128)(2,1)S(1)}, u32[]{:S(2)}, u32[]{:S(2)}) collective-permute-start(bf16[8,128,128]{2,1,0:T(8,128)(2,1)S(1)} %get-tuple-element.33.refs_0_), channel_id=1, source_target_pairs={{0,16},{16,0},{1,17},{17,1},{2,18},{18,2},{3,19},{19,3},{4,20},{20... | collective-permute-start | bytes 786440 | tf_op jit(solution)/shard_map/ppermute | solution.py:249
  72.3 9.2 %collective-permute-start.13 = (bf16[8,128,128]{2,1,0:T(8,128)(2,1)S(1)}, bf16[8,128,128]{2,1,0:T(8,128)(2,1)S(1)}, u32[]{:S(2)}, u32[]{:S(2)}) collective-permute-start(bf16[8,128,128]{2,1,0:T(8,128)(2,1)S(1)} %get-tuple-element.34.refs_0_), channel_id=1, source_target_pairs={{0,1},{1,0},{2,3},{3,2},{4,5},{5,4},{6,7},{7,6},{8,9},{9,8},{10,11... | collective-permute-start | bytes 786440 | tf_op jit(solution)/shard_map/ppermute | solution.py:242
  72.8 14.8 %collective-permute-start.14 = (bf16[8,128,128]{2,1,0:T(8,128)(2,1)S(1)}, bf16[8,128,128]{2,1,0:T(8,128)(2,1)S(1)}, u32[]{:S(2)}, u32[]{:S(2)}) collective-permute-start(bf16[8,128,128]{2,1,0:T(8,128)(2,1)S(1)} %get-tuple-element.34.refs_0_), channel_id=1, source_target_pairs={{0,2},{1,3},{2,0},{3,1},{4,6},{5,7},{6,4},{7,5},{8,10},{9,11},{10,... | collective-permute-start | bytes 786440 | tf_op jit(solution)/shard_map/ppermute | solution.py:242
  73.5 20.6 %collective-permute-start.15 = (bf16[8,128,128]{2,1,0:T(8,128)(2,1)S(1)}, bf16[8,128,128]{2,1,0:T(8,128)(2,1)S(1)}, u32[]{:S(2)}, u32[]{:S(2)}) collective-permute-start(bf16[8,128,128]{2,1,0:T(8,128)(2,1)S(1)} %get-tuple-element.34.refs_0_), channel_id=1, source_target_pairs={{0,3},{1,2},{2,1},{3,0},{4,7},{5,6},{6,5},{7,4},{8,11},{9,10},{10,... | collective-permute-start | bytes 786440 | tf_op jit(solution)/shard_map/ppermute | solution.py:242
  75.8 19.6 %collective-permute-start.16 = (bf16[8,128,128]{2,1,0:T(8,128)(2,1)S(1)}, bf16[8,128,128]{2,1,0:T(8,128)(2,1)S(1)}, u32[]{:S(2)}, u32[]{:S(2)}) collective-permute-start(bf16[8,128,128]{2,1,0:T(8,128)(2,1)S(1)} %get-tuple-element.34.refs_0_), channel_id=1, source_target_pairs={{0,16},{16,0},{1,17},{17,1},{2,18},{18,2},{3,19},{19,3},{4,20},{20... | collective-permute-start | bytes 786440 | tf_op jit(solution)/shard_map/ppermute | solution.py:249
  76.8 18.5 %collective-permute-start.10 = (bf16[8,128,128]{2,1,0:T(8,128)(2,1)S(1)}, bf16[8,128,128]{2,1,0:T(8,128)(2,1)S(1)}, u32[]{:S(2)}, u32[]{:S(2)}) collective-permute-start(bf16[8,128,128]{2,1,0:T(8,128)(2,1)S(1)} %collective-permute-done.6.refs_1_), channel_id=1, source_target_pairs={{0,16},{16,0},{1,17},{17,1},{2,18},{18,2},{3,19},{19,3},{4,20},{20... | collective-permute-start | bytes 786440 | tf_op jit(solution)/shard_map/ppermute | solution.py:249
  81.4 14.7 %collective-permute-start.25 = (bf16[8,128,128]{2,1,0:T(8,128)(2,1)S(1)}, bf16[8,128,128]{2,1,0:T(8,128)(2,1)S(1)}, u32[]{:S(2)}, u32[]{:S(2)}) collective-permute-start(bf16[8,128,128]{2,1,0:T(8,128)(2,1)S(1)} %get-tuple-element.44), channel_id=1, source_target_pairs={{0,4},{1,5},{2,6},{3,7},{4,0},{5,1},{6,2},{7,3},{8,12},{9,13},{10,... | collective-permute-start | bytes 786440 | tf_op jit(solution)/shard_map/ppermute | solution.py:246
  87.6 23.5 %collective-permute-start.26 = (bf16[8,128,128]{2,1,0:T(8,128)(2,1)S(1)}, bf16[8,128,128]{2,1,0:T(8,128)(2,1)S(1)}, u32[]{:S(2)}, u32[]{:S(2)}) collective-permute-start(bf16[8,128,128]{2,1,0:T(8,128)(2,1)S(1)} %get-tuple-element.45), channel_id=1, source_target_pairs={{0,8},{1,9},{2,10},{3,11},{4,12},{5,13},{6,14},{7,15},{8,0},{9,1},... | collective-permute-start | bytes 786440 | tf_op jit(solution)/shard_map/ppermute | solution.py:246
  94.1 16.9 %collective-permute-start.27 = (bf16[8,128,128]{2,1,0:T(8,128)(2,1)S(1)}, bf16[8,128,128]{2,1,0:T(8,128)(2,1)S(1)}, u32[]{:S(2)}, u32[]{:S(2)}) collective-permute-start(bf16[8,128,128]{2,1,0:T(8,128)(2,1)S(1)} %get-tuple-element.46), channel_id=1, source_target_pairs={{0,12},{1,13},{2,14},{3,15},{4,8},{5,9},{6,10},{7,11},{8,4},{9,5},... | collective-permute-start | bytes 786440 | tf_op jit(solution)/shard_map/ppermute | solution.py:246
  95.3 17.0 %collective-permute-start.17 = (bf16[8,128,128]{2,1,0:T(8,128)(2,1)S(1)}, bf16[8,128,128]{2,1,0:T(8,128)(2,1)S(1)}, u32[]{:S(2)}, u32[]{:S(2)}) collective-permute-start(bf16[8,128,128]{2,1,0:T(8,128)(2,1)S(1)} %collective-permute-done.13.refs_1_), channel_id=1, source_target_pairs={{0,16},{16,0},{1,17},{17,1},{2,18},{18,2},{3,19},{19,3},{4,20},{20... | collective-permute-start | bytes 786440 | tf_op jit(solution)/shard_map/ppermute | solution.py:249
  95.4 19.7 %collective-permute-start.18 = (bf16[8,128,128]{2,1,0:T(8,128)(2,1)S(1)}, bf16[8,128,128]{2,1,0:T(8,128)(2,1)S(1)}, u32[]{:S(2)}, u32[]{:S(2)}) collective-permute-start(bf16[8,128,128]{2,1,0:T(8,128)(2,1)S(1)} %collective-permute-done.14.refs_2_), channel_id=1, source_target_pairs={{0,16},{16,0},{1,17},{17,1},{2,18},{18,2},{3,19},{19,3},{4,20},{20... | collective-permute-start | bytes 786440 | tf_op jit(solution)/shard_map/ppermute | solution.py:249
  96.1 19.0 %collective-permute-start.19 = (bf16[8,128,128]{2,1,0:T(8,128)(2,1)S(1)}, bf16[8,128,128]{2,1,0:T(8,128)(2,1)S(1)}, u32[]{:S(2)}, u32[]{:S(2)}) collective-permute-start(bf16[8,128,128]{2,1,0:T(8,128)(2,1)S(1)} %collective-permute-done.15.refs_3_), channel_id=1, source_target_pairs={{0,16},{16,0},{1,17},{17,1},{2,18},{18,2},{3,19},{19,3},{4,20},{20... | collective-permute-start | bytes 786440 | tf_op jit(solution)/shard_map/ppermute | solution.py:249
  111.0 8.4 %collective-permute-start.11 = (bf16[8,128,128]{2,1,0:T(8,128)(2,1)S(1)}, bf16[8,128,128]{2,1,0:T(8,128)(2,1)S(1)}, u32[]{:S(2)}, u32[]{:S(2)}) collective-permute-start(bf16[8,128,128]{2,1,0:T(8,128)(2,1)S(1)} %collective-permute-done.7.refs_2_), channel_id=1, source_target_pairs={{0,16},{16,0},{1,17},{17,1},{2,18},{18,2},{3,19},{19,3},{4,20},{20... | collective-permute-start | bytes 786440 | tf_op jit(solution)/shard_map/ppermute | solution.py:249
  111.0 10.0 %collective-permute-start.12 = (bf16[8,128,128]{2,1,0:T(8,128)(2,1)S(1)}, bf16[8,128,128]{2,1,0:T(8,128)(2,1)S(1)}, u32[]{:S(2)}, u32[]{:S(2)}) collective-permute-start(bf16[8,128,128]{2,1,0:T(8,128)(2,1)S(1)} %collective-permute-done.8.refs_3_), channel_id=1, source_target_pairs={{0,16},{16,0},{1,17},{17,1},{2,18},{18,2},{3,19},{19,3},{4,20},{20... | collective-permute-start | bytes 786440 | tf_op jit(solution)/shard_map/ppermute | solution.py:249
  112.3 7.1 %collective-permute-start.28 = (bf16[2,128,128]{2,1,0:T(8,128)(2,1)S(1)}, bf16[2,128,128]{2,1,0:T(8,128)(2,1)S(1)}, u32[]{:S(2)}, u32[]{:S(2)}) collective-permute-start(bf16[2,128,128]{2,1,0:T(8,128)(2,1)S(1)} %get-tuple-element.48), channel_id=1, source_target_pairs={{0,1},{1,0},{2,3},{3,2},{4,5},{5,4},{6,7},{7,6},{8,9},{9,8},{10,11... | collective-permute-start | bytes 196616 | tf_op jit(solution)/shard_map/ppermute | solution.py:242
  115.1 5.4 %collective-permute-start.29 = (bf16[2,128,128]{2,1,0:T(8,128)(2,1)S(1)}, bf16[2,128,128]{2,1,0:T(8,128)(2,1)S(1)}, u32[]{:S(2)}, u32[]{:S(2)}) collective-permute-start(bf16[2,128,128]{2,1,0:T(8,128)(2,1)S(1)} %get-tuple-element.49), channel_id=1, source_target_pairs={{0,2},{1,3},{2,0},{3,1},{4,6},{5,7},{6,4},{7,5},{8,10},{9,11},{10,... | collective-permute-start | bytes 196616 | tf_op jit(solution)/shard_map/ppermute | solution.py:242
  115.1 5.4 %collective-permute-start.30 = (bf16[2,128,128]{2,1,0:T(8,128)(2,1)S(1)}, bf16[2,128,128]{2,1,0:T(8,128)(2,1)S(1)}, u32[]{:S(2)}, u32[]{:S(2)}) collective-permute-start(bf16[2,128,128]{2,1,0:T(8,128)(2,1)S(1)} %get-tuple-element.50), channel_id=1, source_target_pairs={{0,3},{1,2},{2,1},{3,0},{4,7},{5,6},{6,5},{7,4},{8,11},{9,10},{10,... | collective-permute-start | bytes 196616 | tf_op jit(solution)/shard_map/ppermute | solution.py:242
  119.5 4.4 %collective-permute-start.31 = (bf16[2,128,128]{2,1,0:T(8,128)(2,1)S(1)}, bf16[2,128,128]{2,1,0:T(8,128)(2,1)S(1)}, u32[]{:S(2)}, u32[]{:S(2)}) collective-permute-start(bf16[2,128,128]{2,1,0:T(8,128)(2,1)S(1)} %get-tuple-element.47.refs_0_), channel_id=1, source_target_pairs={{0,16},{16,0},{1,17},{17,1},{2,18},{18,2},{3,19},{19,3},{4,20},{20... | collective-permute-start | bytes 196616 | tf_op jit(solution)/shard_map/ppermute | solution.py:249
  119.5 4.4 %collective-permute-start.32 = (bf16[2,128,128]{2,1,0:T(8,128)(2,1)S(1)}, bf16[2,128,128]{2,1,0:T(8,128)(2,1)S(1)}, u32[]{:S(2)}, u32[]{:S(2)}) collective-permute-start(bf16[2,128,128]{2,1,0:T(8,128)(2,1)S(1)} %collective-permute-done.28.refs_1_), channel_id=1, source_target_pairs={{0,16},{16,0},{1,17},{17,1},{2,18},{18,2},{3,19},{19,3},{4,20},{20... | collective-permute-start | bytes 196616 | tf_op jit(solution)/shard_map/ppermute | solution.py:249
  120.5 3.4 %collective-permute-start.33 = (bf16[2,128,128]{2,1,0:T(8,128)(2,1)S(1)}, bf16[2,128,128]{2,1,0:T(8,128)(2,1)S(1)}, u32[]{:S(2)}, u32[]{:S(2)}) collective-permute-start(bf16[2,128,128]{2,1,0:T(8,128)(2,1)S(1)} %collective-permute-done.29.refs_2_), channel_id=1, source_target_pairs={{0,16},{16,0},{1,17},{17,1},{2,18},{18,2},{3,19},{19,3},{4,20},{20... | collective-permute-start | bytes 196616 | tf_op jit(solution)/shard_map/ppermute | solution.py:249
  120.5 3.4 %collective-permute-start.34 = (bf16[2,128,128]{2,1,0:T(8,128)(2,1)S(1)}, bf16[2,128,128]{2,1,0:T(8,128)(2,1)S(1)}, u32[]{:S(2)}, u32[]{:S(2)}) collective-permute-start(bf16[2,128,128]{2,1,0:T(8,128)(2,1)S(1)} %collective-permute-done.30.refs_3_), channel_id=1, source_target_pairs={{0,16},{16,0},{1,17},{17,1},{2,18},{18,2},{3,19},{19,3},{4,20},{20... | collective-permute-start | bytes 196616 | tf_op jit(solution)/shard_map/ppermute | solution.py:249

commit v3 on v2

--- a/solution.py
+++ b/solution.py
@@ -93,8 +93,8 @@
                         out[j - n * per_out] = ref[m * reach + t]
 
 
-def grad_kernel(scale, tile, chunks, mine, theirs, cot_mine, cot_theirs, *refs):
-    outs, quad = refs[:INNER], refs[INNER]
+def grad_kernel(scale, tile, chunks, mine, theirs, cot_mine, cot_theirs, own, *refs):
+    outs, quad = refs[:-1], refs[-1]
     core, _, place, _ = here()
     half = cot_mine.shape[1] // 2
     columns = pl.ds(pl.multiple_of(core * half, half), half)
@@ -103,20 +103,36 @@
     per_chunk = wide // (2 * tile)
     dims = (((0,), (0,)), ((), ()))
 
-    def chunk(i, carry):
+    def chunk(part, i, carry):
+        base = i * per_chunk - part * (chunks // 2) * per_chunk
         for k in range(per_chunk):
             rows = pl.ds(pl.multiple_of(i * wide + 2 * tile * k, 2 * tile), 2 * tile)
-            part = lax.dot_general(mine[:, rows], left, dims, preferred_element_type=jnp.float32)
-            part += lax.dot_general(theirs[:, rows], right, dims, preferred_element_type=jnp.float32)
-            quad[k] = part * scale
-            for m, out in enumerate(outs):
+            value = lax.dot_general(mine[:, rows], left, dims, preferred_element_type=jnp.float32)
+            value += lax.dot_general(
+                theirs[:, rows], right, dims, preferred_element_type=jnp.float32
+            )
+            quad[k] = value * scale
+            for m in range(INNER):
                 where = place ^ m
                 row = pl.multiple_of((where // 2) * tile, tile)
                 col = pl.multiple_of((where % 2) * tile, tile)
-                out[i * per_chunk + k] = quad[k, pl.ds(row, tile), pl.ds(col, tile)].astype(BF16)
+                block = quad[k, pl.ds(row, tile), pl.ds(col, tile)].astype(BF16)
+                if m:
+                    outs[2 * (m - 1) + part][base + k] = block
+                else:
+                    own[i * per_chunk + k] = block
         return carry
 
-    lax.fori_loop(0, chunks, chunk, 0)
+    for part in range(2):
+        first = part * (chunks // 2)
+        lax.fori_loop(first, first + chunks // 2, functools.partial(chunk, part), 0)
+
+
+def fold_kernel(*refs):
+    ins, outs = refs[:4], refs[4:]
+    for n, out in enumerate(outs):
+        value = ins[2 * n][...].astype(jnp.float32) + ins[2 * n + 1][...].astype(jnp.float32)
+        out[...] = value.astype(BF16)
 
 
 def window(counts, cls, plane, blocks, span):
@@ -124,15 +140,16 @@
     return jnp.minimum((start + lead(cls, start)) // PERIOD, blocks - span)
 
 
-def plane_sum_kernel(span, counts, *refs):
-    ins, outs, total = refs[:INNER], refs[INNER:-1], refs[-1]
+def plane_sum_kernel(span, counts, own, *refs):
+    ins, outs, total = refs[:4], refs[4:-1], refs[-1]
     core, plane, place, _ = here()
     cls = class_of(core, place)
     blocks = total.shape[0]
     for j in range(blocks):
-        acc = ins[0][j].astype(jnp.float32)
-        for ref in ins[1:]:
-            acc += ref[j].astype(jnp.float32)
+        part, row = divmod(j, blocks // 2)
+        acc = own[j].astype(jnp.float32)
+        for ref in ins[2 * part : 2 * part + 2]:
+            acc += ref[row].astype(jnp.float32)
         total[j] = acc.astype(BF16)
     for shift, out in enumerate(outs):
         target = plane ^ shift
@@ -171,31 +188,44 @@
                 out[slot] = jnp.where(slot < count, value, jnp.zeros_like(value))
 
 
-def product_kernel(tile, per_step, last, tokens, cot, *refs):
-    pieces, refs = refs[: 2 * INNER], refs[2 * INNER :]
-    before = refs[0] if last else None
-    projected, token_grad, weight, acc = refs[2:] if last else refs
+def product_kernel(tile, part, tokens, cot, *refs):
+    pieces, refs = refs[:8], refs[8:]
+    before, refs = (refs[0], refs[2:]) if part else (None, refs)
+    projected, token_grad, left, weight, acc, stripes, done = refs
     core, _, place, _ = here()
-    step = pl.program_id(0)
-    for n, ref in enumerate(pieces):
-        side, where = core ^ (n // INNER), place ^ (n % INNER)
-        col = pl.multiple_of((side * 2 + where % 2) * tile, tile)
-        for k in range(per_step):
-            row = pl.multiple_of((where // 2) * tile + 2 * tile * k, tile)
-            weight[pl.ds(row, tile), pl.ds(col, tile)] = ref[k]
-
-    @pl.when(step == 0)
-    def _():
-        acc[...] = before[...] if last else jnp.zeros_like(acc)
-
-    acc[...] += jnp.dot(tokens[...], weight[...], preferred_element_type=jnp.float32)
-    token_grad[...] = lax.dot_general(
-        cot[...], weight[...], (((1,), (1,)), ((), ())), preferred_element_type=jnp.float32
-    ).astype(BF16)
-
-    @pl.when(step == pl.num_programs(0) - 1)
-    def _():
-        projected[...] = acc[...].astype(projected.dtype)
+    parity = (place // 2) ^ part
+    per_piece = pieces[0].shape[0]
+    group = left.shape[1] // tile
+    stores = []
+    for start in range(0, 2 * per_piece, group):
+        half, first = divmod(start, per_piece)
+        for k in range(group):
+            lane = pl.multiple_of((2 * (start + k) + parity) * tile, tile)
+            left[:, pl.ds(k * tile, tile)] = tokens[:, pl.ds(lane, tile)]
+            for n in range(4):
+                side, m = divmod(n, 2)
+                col = pl.multiple_of(((core ^ side) * 2 + (place ^ m) % 2) * tile, tile)
+                weight[pl.ds(k * tile, tile), pl.ds(col, tile)] = pieces[2 * n + half][first + k]
+        value = jnp.dot(left[...], weight[...], preferred_element_type=jnp.float32)
+        if start:
+            acc[...] += value
+        else:
+            acc[...] = before[...] + value if part else value
+        grads = lax.dot_general(
+            cot[...], weight[...], (((1,), (1,)), ((), ())), preferred_element_type=jnp.float32
+        ).astype(BF16)
+        for k in range(group):
+            j = start + k
+            stripes[j] = grads[:, k * tile : (k + 1) * tile]
+            lane = pl.multiple_of((2 * j + parity) * tile, tile)
+            store = pltpu.make_async_copy(
+                stripes.at[j], token_grad.at[:, pl.ds(lane, tile)], done.at[j]
+            )
+            store.start()
+            stores.append(store)
+    projected[...] = acc[...].astype(projected.dtype)
+    for store in stores:
+        store.wait()
 
 
 def whole():
@@ -280,22 +310,42 @@
     near = [spread[0]] + [beside(spread[m], m) for m in range(1, INNER)]
 
     chunks = 4
+    half = many(blocks // 2)
     grads = call(
         functools.partial(grad_kernel, 1.0 / math.sqrt(total_tokens), tile, chunks),
         my_tokens,
         their_tokens,
         my_cot,
         their_cot,
-        out_shape=[many(blocks)] * INNER,
+        out_shape=[many(blocks)] + [half] * 6,
         in_specs=[whole()] * 4,
-        out_specs=[whole()] * INNER,
+        out_specs=[whole()] * 7,
         scratch_shapes=[
             VMEM((width // (2 * tile * chunks), 2 * tile, 2 * tile), jnp.float32)
         ],
         cost_estimate=cost(2 * rows * width * key_width, 6 * rows * width),
         compiler_params=room(20),
     )
-    parts = [grads[0]] + [beside(grads[m], m) for m in range(1, INNER)]
+    own_part, x_low, x_high, y_low, y_high, far_low, far_high = grads
+    folded = call(
+        fold_kernel,
+        y_low,
+        beside(far_low, 1),
+        x_high,
+        beside(far_high, 2),
+        out_shape=[half] * 2,
+        in_specs=[whole()] * 4,
+        out_specs=[whole()] * 2,
+        cost_estimate=cost(16 * block_bytes, 48 * block_bytes),
+        compiler_params=room(8),
+    )
+    parts = [
+        own_part,
+        beside(x_low, 1),
+        beside(folded[0], 2),
+        beside(folded[1], 1),
+        beside(y_high, 2),
+    ]
 
     stacked = call(
         functools.partial(stack_kernel, reach),
@@ -306,7 +356,9 @@
         cost_estimate=cost(8 * block_bytes, 16 * block_bytes),
         compiler_params=room(8),
     )
-    held = [stacked] + [along(stacked, s) for s in range(1, planes)]
+    held = [stacked] + [along(stacked, s) for s in range(1, planes) if (s, planes) != (2, 4)]
+    if planes == 4:
+        held.insert(2, along(held[2], 1))
 
     own_classes = call(
         functools.partial(class_kernel, planes, reach),
@@ -324,7 +376,7 @@
         functools.partial(plane_sum_kernel, span),
         counts, *parts,
         out_shape=[many(span)] * planes,
-        in_specs=[scalars()] + [whole()] * INNER,
+        in_specs=[scalars()] + [whole()] * 5,
         out_specs=[whole()] * planes,
         scratch_shapes=[VMEM((blocks, tile, tile), BF16)],
         cost_estimate=cost(64 * block_bytes, 96 * block_bytes),
@@ -344,40 +396,40 @@
     )
     mine = [sent[0]] + [beside(sent[m], m) for m in range(1, INNER)]
 
-    per_step = min(4, blocks // 2)
-    steps = blocks // 2 // per_step
-    wide = 2 * tile * per_step
-
-    def products(part, carried):
-        last = part == 1
-        base = part * steps
-        own = own_classes[part]
-        plane = [own] + [beside(own, m) for m in range(1, INNER)]
-        pieces = plane + [across(c) for c in plane]
-        square = pl.BlockSpec((rows, key_width), lambda i: (0, 0))
-        stripe = pl.BlockSpec((rows, wide), lambda i: (0, base + i))
+    low, high = own_classes
+    from_x = [beside(low, 1), beside(high, 1)]
+    from_y = [beside(low, 2), beside(high, 2)]
+    from_far = [beside(from_x[0], 2), beside(from_y[1], 1)]
+    group = min(4, blocks // 2)
+
+    def products(part, own, carried):
+        held_by_both = own + [across(c) for c in own]
         return call(
-            functools.partial(product_kernel, tile, per_step, last),
+            functools.partial(product_kernel, tile, part),
             my_tokens,
             my_cot,
-            *pieces,
+            *held_by_both,
             *carried,
             out_shape=[
-                jax.ShapeDtypeStruct((rows, key_width), BF16 if last else jnp.float32),
-                jax.ShapeDtypeStruct((rows, width), BF16),
+                jax.ShapeDtypeStruct((rows, key_width), BF16 if part else jnp.float32),
+                pltpu.HBM((rows, width), BF16),
             ],
-            grid=(steps,),
-            in_specs=[stripe, square]
-            + [pl.BlockSpec((per_step, tile, tile), lambda i: (i, 0, 0))] * (2 * INNER)
-            + ([square, pl.BlockSpec(memory_space=pl.ANY)] if last else []),
-            out_specs=[square, stripe],
-            input_output_aliases={2 * INNER + 3: 1} if last else {},
-            scratch_shapes=[VMEM((wide, key_width), BF16), VMEM((rows, key_width), jnp.float32)],
+            in_specs=[whole()] * 10 + ([whole(), far()] if part else []),
+            out_specs=[whole(), far()],
+            input_output_aliases={11: 1} if part else {},
+            scratch_shapes=[
+                VMEM((rows, group * tile), BF16),
+                VMEM((group * tile, key_width), BF16),
+                VMEM((rows, key_width), jnp.float32),
+                VMEM((blocks, rows, tile), BF16),
+                pltpu.SemaphoreType.DMA((blocks,)),
+            ],
             cost_estimate=cost(2 * rows * width * key_width, 6 * rows * width),
-            compiler_params=room(28),
+            compiler_params=room(16),
         )
 
-    projected, token_grad = products(1, products(0, ()))
+    partial_sum, half_grad = products(0, [low, high] + from_x, ())
+    projected, token_grad = products(1, from_y + from_far, (partial_sum, stays(half_grad)))
 
     all_mine = mine + [across(v) for v in mine]
     block_grad = call(

time: 128 us -> 101 us (0.79)
  the two profiles are of different devices: /device:TPU:0 before, /device:TPU:17 now
where the time goes in v3:
time: 101 us
  waiting for transfers between devices  46.5 us (46%)
  starting transfers between devices  39 us (39%)
  Pallas kernels  15 us (15%)
    ppermute x6, waiting for transfers between devices, along(): return lax.ppermute(value, 'fsdp', pairs)  27.5 us
    ppermute x14, starting transfers between devices, across(): return lax.ppermute(value, 'dp', [(0, 1), (1, 0)])  23.6 us
    ppermute x18, waiting for transfers between devices, beside(): return lax.ppermute(value, 'fsdp', [(i, i ^ m) for i in range(owners)])  18.9 us
    pallas_call x10, Pallas kernels, call(): return pl.pallas_call(kernel, **how)(*operands)  15 us
    ppermute x18, starting transfers between devices, beside(): return lax.ppermute(value, 'fsdp', [(i, i ^ m) for i in range(owners)])  11.4 us
    ppermute x6, starting transfers between devices, along(): return lax.ppermute(value, 'fsdp', pairs)  3.89 us
  transfers between devices with their start and end apart: 38, of which 14 were waited for; matrix products, arithmetic and copies ran while one was open for 0% of the time, Pallas kernels for 13%

profile of v3, /device:TPU:17, one launch (start us, length us, event | category | flops | bytes accessed | tf_op | source)
XLA Modules:
  0.0 101.3 jit_solution(16573080910022836801)
XLA Ops:
  0.6 0.7 collective-permute-start.20
  1.4 1.8 %shard_map.76 = (bf16[256,4096]{1,0:T(8,128)(2,1)S(1)}, bf16[256,512]{1,0:T(8,128)(2,1)S(1)}, bf16[2,128,128]{2,1,0:T(8,128)(2,1)S(1)}, bf16[2,128,128]{2,1,0:T(...) custom-call(s32[16]{0:T(128)} %counts.7, f32[16]{0:T(128)} %scales_in.1, ...), custom_call_target="tpu_custom_call" | custom-call | flops 262144 | bytes 786432 | tf_op jit(solution)/shard_map/pallas_call | solution.py:282
  3.2 1.3 %collective-permute-start = (bf16[2,128,128]{2,1,0:T(8,128)(2,1)S(1)}, bf16[2,128,128]{2,1,0:T(8,128)(2,1)S(1)}, u32[]{:S(2)}, u32[]{:S(2)}) collective-permute-start(bf16[2,128,128]{2,1,0:T(8,128)(2,1)S(1)} %get-tuple-element.35), channel_id=1, source_target_pairs={{0,1},{1,0},{2,3},{3,2},{4,5},{5,4},{6,7},{7,6},{8,9},{9,8},{10,11... | collective-permute-start | bytes 196616 | tf_op jit(solution)/shard_map/ppermute | solution.py:272
  4.4 1.2 %collective-permute-start.1 = (bf16[2,128,128]{2,1,0:T(8,128)(2,1)S(1)}, bf16[2,128,128]{2,1,0:T(8,128)(2,1)S(1)}, u32[]{:S(2)}, u32[]{:S(2)}) collective-permute-start(bf16[2,128,128]{2,1,0:T(8,128)(2,1)S(1)} %get-tuple-element.36), channel_id=1, source_target_pairs={{0,2},{1,3},{2,0},{3,1},{4,6},{5,7},{6,4},{7,5},{8,10},{9,11},{10,... | collective-permute-start | bytes 196616 | tf_op jit(solution)/shard_map/ppermute | solution.py:272
  5.9 1.0 collective-permute-done.refs_1_
  6.9 0.7 collective-permute-done.1.refs_2_
  7.6 2.1 %collective-permute-done.2.refs_3_ = bf16[2,128,128]{2,1,0:T(8,128)(2,1)S(1)} collective-permute-done((bf16[2,128,128]{2,1,0:T(8,128)(2,1)S(1)}, bf16[2,128,128]{2,1,0:T(8,128)(2,1)S(1)}, u32[]{:S(2)}, u32[]{:S(2)}) %collective-permute-start.2) | collective-permute-done | bytes 65568 | tf_op jit(solution)/shard_map/ppermute | solution.py:272
  10.0 2.0 %collective-permute-start.21 = (bf16[256,512]{1,0:T(8,128)(2,1)S(1)}, bf16[256,512]{1,0:T(8,128)(2,1)S(1)}, u32[]{:S(2)}, u32[]{:S(2)}) collective-permute-start(bf16[256,512]{1,0:T(8,128)(2,1)S(1)} %copy-done.1), channel_id=1, source_target_pairs={{0,16},{16,0},{1,17},{17,1},{2,18},{18,2},{3,19},{19,3},{4,20},{20... | collective-permute-start | bytes 786440 | tf_op jit(solution)/shard_map/ppermute | solution.py:279
  12.0 1.1 %collective-permute-start.3 = (bf16[8,128,128]{2,1,0:T(8,128)(2,1)S(1)}, bf16[8,128,128]{2,1,0:T(8,128)(2,1)S(1)}, u32[]{:S(2)}, u32[]{:S(2)}) collective-permute-start(bf16[8,128,128]{2,1,0:T(8,128)(2,1)S(1)} %shard_map.77.refs_0_), channel_id=1, source_target_pairs={{0,4},{1,5},{2,6},{3,7},{4,0},{5,1},{6,2},{7,3},{8,12},{9,13},{10,... | collective-permute-start | bytes 786440 | tf_op jit(solution)/shard_map/ppermute | solution.py:276
  13.0 8.1 %collective-permute-done.4.refs_3_ = bf16[8,128,128]{2,1,0:T(8,128)(2,1)S(1)} collective-permute-done((bf16[8,128,128]{2,1,0:T(8,128)(2,1)S(1)}, bf16[8,128,128]{2,1,0:T(8,128)(2,1)S(1)}, u32[]{:S(2)}, u32[]{:S(2)}) %collective-permute-start.4) | collective-permute-done | bytes 262176 | tf_op jit(solution)/shard_map/ppermute | solution.py:276
  21.2 2.2 %shard_map.81 = (bf16[16,128,128]{2,1,0:T(8,128)(2,1)S(1)}, bf16[8,128,128]{2,1,0:T(8,128)(2,1)S(1)}, bf16[8,128,128]{2,1,0:T(8,128)(2,1)S(1)}, bf16[8,128,128]{...) custom-call(bf16[256,4096]{1,0:T(8,128)(2,1)S(1)} %get-tuple-element, ...), custom_call_target="tpu_custom_call" | custom-call | flops 1073741824 | bytes 6291456 | tf_op jit(solution)/shard_map/pallas_call | solution.py:282
  23.5 0.3 collective-permute-start.23
  23.8 0.5 collective-permute-start.24
  24.3 0.4 collective-permute-done.3.refs_1_
  24.7 5.6 %collective-permute-done.5.refs_2_ = bf16[8,128,128]{2,1,0:T(8,128)(2,1)S(1)} collective-permute-done((bf16[8,128,128]{2,1,0:T(8,128)(2,1)S(1)}, bf16[8,128,128]{2,1,0:T(8,128)(2,1)S(1)}, u32[]{:S(2)}, u32[]{:S(2)}) %collective-permute-start.5) | collective-permute-done | bytes 262176 | tf_op jit(solution)/shard_map/ppermute | solution.py:276
  30.3 1.5 %shard_map.78 = (bf16[8,128,128]{2,1,0:T(8,128)(2,1)S(1)}, bf16[8,128,128]{2,1,0:T(8,128)(2,1)S(1)}) custom-call(s32[16]{0:T(128)S(1)} %copy-done, bf16[8,128,128]{2,1,0:T(8,128)(2,1)S(1)} %shard_map.77.refs_0_, bf16[8,128,128]{2,1,0:T(8,128)(2,1)S(1)} %collective-permute-done.3.refs_1_, bf16[8,128,128]{2,1,0:T(8,128)(2,1)S(1)} %collective-permute-done.5.refs_2_, ...), custom_call_target="tpu_custom_call" | custom-call | flops 1048576 | bytes 1572864 | tf_op jit(solution)/shard_map/pallas_call | solution.py:282
  31.8 0.3 collective-permute-start.6
  32.1 1.3 %collective-permute-start.7 = (bf16[8,128,128]{2,1,0:T(8,128)(2,1)S(1)}, bf16[8,128,128]{2,1,0:T(8,128)(2,1)S(1)}, u32[]{:S(2)}, u32[]{:S(2)}) collective-permute-start(bf16[8,128,128]{2,1,0:T(8,128)(2,1)S(1)} %get-tuple-element.39.refs_1_), channel_id=1, source_target_pairs={{0,2},{1,3},{2,0},{3,1},{4,6},{5,7},{6,4},{7,5},{8,10},{9,11},{10,... | collective-permute-start | bytes 786440 | tf_op jit(solution)/shard_map/ppermute | solution.py:272
  33.6 1.2 %collective-permute-start.22 = (bf16[8,128,128]{2,1,0:T(8,128)(2,1)S(1)}, bf16[8,128,128]{2,1,0:T(8,128)(2,1)S(1)}, u32[]{:S(2)}, u32[]{:S(2)}) collective-permute-start(bf16[8,128,128]{2,1,0:T(8,128)(2,1)S(1)} %get-tuple-element.45), channel_id=1, source_target_pairs={{0,1},{1,0},{2,3},{3,2},{4,5},{5,4},{6,7},{7,6},{8,9},{9,8},{10,11... | collective-permute-start | bytes 786440 | tf_op jit(solution)/shard_map/ppermute | solution.py:272
  35.2 4.1 %collective-permute-done.6.refs_0_ = bf16[8,128,128]{2,1,0:T(8,128)(2,1)S(1)} collective-permute-done((bf16[8,128,128]{2,1,0:T(8,128)(2,1)S(1)}, bf16[8,128,128]{2,1,0:T(8,128)(2,1)S(1)}, u32[]{:S(2)}, u32[]{:S(2)}) %collective-permute-start.6) | collective-permute-done | bytes 262176 | tf_op jit(solution)/shard_map/ppermute | solution.py:272
  39.4 5.5 %collective-permute-done.7.refs_1_ = bf16[8,128,128]{2,1,0:T(8,128)(2,1)S(1)} collective-permute-done((bf16[8,128,128]{2,1,0:T(8,128)(2,1)S(1)}, bf16[8,128,128]{2,1,0:T(8,128)(2,1)S(1)}, u32[]{:S(2)}, u32[]{:S(2)}) %collective-permute-start.7) | collective-permute-done | bytes 262176 | tf_op jit(solution)/shard_map/ppermute | solution.py:272
  45.1 1.2 %collective-permute-start.15 = (bf16[8,128,128]{2,1,0:T(8,128)(2,1)S(1)}, bf16[8,128,128]{2,1,0:T(8,128)(2,1)S(1)}, u32[]{:S(2)}, u32[]{:S(2)}) collective-permute-start(bf16[8,128,128]{2,1,0:T(8,128)(2,1)S(1)} %get-tuple-element.39.refs_1_), channel_id=1, source_target_pairs={{0,1},{1,0},{2,3},{3,2},{4,5},{5,4},{6,7},{7,6},{8,9},{9,8},{10,11... | collective-permute-start | bytes 786440 | tf_op jit(solution)/shard_map/ppermute | solution.py:272
  46.3 2.8 %collective-permute-start.16 = (bf16[8,128,128]{2,1,0:T(8,128)(2,1)S(1)}, bf16[8,128,128]{2,1,0:T(8,128)(2,1)S(1)}, u32[]{:S(2)}, u32[]{:S(2)}) collective-permute-start(bf16[8,128,128]{2,1,0:T(8,128)(2,1)S(1)} %get-tuple-element.38.refs_0_), channel_id=1, source_target_pairs={{0,16},{16,0},{1,17},{17,1},{2,18},{18,2},{3,19},{19,3},{4,20},{20... | collective-permute-start | bytes 786440 | tf_op jit(solution)/shard_map/ppermute | solution.py:279
  49.2 1.3 %collective-permute-done.27.refs_3_ = bf16[8,128,128]{2,1,0:T(8,128)(2,1)S(1)} collective-permute-done((bf16[8,128,128]{2,1,0:T(8,128)(2,1)S(1)}, bf16[8,128,128]{2,1,0:T(8,128)(2,1)S(1)}, u32[]{:S(2)}, u32[]{:S(2)}) %collective-permute-start.27) | collective-permute-done | bytes 262176 | tf_op jit(solution)/shard_map/ppermute | solution.py:272
  50.5 2.3 %collective-permute-start.17 = (bf16[8,128,128]{2,1,0:T(8,128)(2,1)S(1)}, bf16[8,128,128]{2,1,0:T(8,128)(2,1)S(1)}, u32[]{:S(2)}, u32[]{:S(2)}) collective-permute-start(bf16[8,128,128]{2,1,0:T(8,128)(2,1)S(1)} %get-tuple-element.39.refs_1_), channel_id=1, source_target_pairs={{0,16},{16,0},{1,17},{17,1},{2,18},{18,2},{3,19},{19,3},{4,20},{20... | collective-permute-start | bytes 786440 | tf_op jit(solution)/shard_map/ppermute | solution.py:279
  52.8 3.3 %collective-permute-done.25.refs_1_ = bf16[8,128,128]{2,1,0:T(8,128)(2,1)S(1)} collective-permute-done((bf16[8,128,128]{2,1,0:T(8,128)(2,1)S(1)}, bf16[8,128,128]{2,1,0:T(8,128)(2,1)S(1)}, u32[]{:S(2)}, u32[]{:S(2)}) %collective-permute-start.25) | collective-permute-done | bytes 262176 | tf_op jit(solution)/shard_map/ppermute | solution.py:272
  56.3 0.3 collective-permute-start.10
  56.5 1.0 shard_map.83
  57.5 2.0 %collective-permute-start.11 = (bf16[8,128,128]{2,1,0:T(8,128)(2,1)S(1)}, bf16[8,128,128]{2,1,0:T(8,128)(2,1)S(1)}, u32[]{:S(2)}, u32[]{:S(2)}) collective-permute-start(bf16[8,128,128]{2,1,0:T(8,128)(2,1)S(1)} %collective-permute-done.6.refs_0_), channel_id=1, source_target_pairs={{0,16},{16,0},{1,17},{17,1},{2,18},{18,2},{3,19},{19,3},{4,20},{20... | collective-permute-start | bytes 786440 | tf_op jit(solution)/shard_map/ppermute | solution.py:279
  59.5 2.2 %collective-permute-start.28 = (bf16[8,128,128]{2,1,0:T(8,128)(2,1)S(1)}, bf16[8,128,128]{2,1,0:T(8,128)(2,1)S(1)}, u32[]{:S(2)}, u32[]{:S(2)}) collective-permute-start(bf16[8,128,128]{2,1,0:T(8,128)(2,1)S(1)} %get-tuple-element.54), channel_id=1, source_target_pairs={{0,4},{1,5},{2,6},{3,7},{4,0},{5,1},{6,2},{7,3},{8,12},{9,13},{10,... | collective-permute-start | bytes 786440 | tf_op jit(solution)/shard_map/ppermute | solution.py:276
  61.8 0.9 collective-permute-done.9.refs_2_
  62.6 0.4 collective-permute-start.30
  63.0 2.0 %collective-permute-start.12 = (bf16[8,128,128]{2,1,0:T(8,128)(2,1)S(1)}, bf16[8,128,128]{2,1,0:T(8,128)(2,1)S(1)}, u32[]{:S(2)}, u32[]{:S(2)}) collective-permute-start(bf16[8,128,128]{2,1,0:T(8,128)(2,1)S(1)} %collective-permute-done.7.refs_1_), channel_id=1, source_target_pairs={{0,16},{16,0},{1,17},{17,1},{2,18},{18,2},{3,19},{19,3},{4,20},{20... | collective-permute-start | bytes 786440 | tf_op jit(solution)/shard_map/ppermute | solution.py:279
  65.0 6.1 %collective-permute-done.28.refs_1_ = bf16[8,128,128]{2,1,0:T(8,128)(2,1)S(1)} collective-permute-done((bf16[8,128,128]{2,1,0:T(8,128)(2,1)S(1)}, bf16[8,128,128]{2,1,0:T(8,128)(2,1)S(1)}, u32[]{:S(2)}, u32[]{:S(2)}) %collective-permute-start.28) | collective-permute-done | bytes 262176 | tf_op jit(solution)/shard_map/ppermute | solution.py:276
  71.1 0.9 collective-permute-start.19
  72.0 1.0 %collective-permute-done.29.refs_2_ = bf16[8,128,128]{2,1,0:T(8,128)(2,1)S(1)} collective-permute-done((bf16[8,128,128]{2,1,0:T(8,128)(2,1)S(1)}, bf16[8,128,128]{2,1,0:T(8,128)(2,1)S(1)}, u32[]{:S(2)}, u32[]{:S(2)}) %collective-permute-start.29) | collective-permute-done | bytes 262176 | tf_op jit(solution)/shard_map/ppermute | solution.py:276
  73.1 6.9 %collective-permute-start.13 = (bf16[8,128,128]{2,1,0:T(8,128)(2,1)S(1)}, bf16[8,128,128]{2,1,0:T(8,128)(2,1)S(1)}, u32[]{:S(2)}, u32[]{:S(2)}) collective-permute-start(bf16[8,128,128]{2,1,0:T(8,128)(2,1)S(1)} %collective-permute-done.9.refs_2_), channel_id=1, source_target_pairs={{0,16},{16,0},{1,17},{17,1},{2,18},{18,2},{3,19},{19,3},{4,20},{20... | collective-permute-start | bytes 786440 | tf_op jit(solution)/shard_map/ppermute | solution.py:279
  80.0 6.2 %collective-permute-done.30.refs_3_ = bf16[8,128,128]{2,1,0:T(8,128)(2,1)S(1)} collective-permute-done((bf16[8,128,128]{2,1,0:T(8,128)(2,1)S(1)}, bf16[8,128,128]{2,1,0:T(8,128)(2,1)S(1)}, u32[]{:S(2)}, u32[]{:S(2)}) %collective-permute-start.30) | collective-permute-done | bytes 262176 | tf_op jit(solution)/shard_map/ppermute | solution.py:276
  86.2 1.0 collective-permute-start.14
  87.2 1.0 shard_map.84
  88.2 1.3 %collective-permute-start.31 = (bf16[2,128,128]{2,1,0:T(8,128)(2,1)S(1)}, bf16[2,128,128]{2,1,0:T(8,128)(2,1)S(1)}, u32[]{:S(2)}, u32[]{:S(2)}) collective-permute-start(bf16[2,128,128]{2,1,0:T(8,128)(2,1)S(1)} %get-tuple-element.58), channel_id=1, source_target_pairs={{0,1},{1,0},{2,3},{3,2},{4,5},{5,4},{6,7},{7,6},{8,9},{9,8},{10,11... | collective-permute-start | bytes 196616 | tf_op jit(solution)/shard_map/ppermute | solution.py:272
  89.4 1.3 %collective-permute-start.32 = (bf16[2,128,128]{2,1,0:T(8,128)(2,1)S(1)}, bf16[2,128,128]{2,1,0:T(8,128)(2,1)S(1)}, u32[]{:S(2)}, u32[]{:S(2)}) collective-permute-start(bf16[2,128,128]{2,1,0:T(8,128)(2,1)S(1)} %get-tuple-element.59), channel_id=1, source_target_pairs={{0,2},{1,3},{2,0},{3,1},{4,6},{5,7},{6,4},{7,5},{8,10},{9,11},{10,... | collective-permute-start | bytes 196616 | tf_op jit(solution)/shard_map/ppermute | solution.py:272
  90.9 2.5 %shard_map.79 = (f32[256,512]{1,0:T(8,128)S(1)}, bf16[256,4096]{1,0:T(8,128)(2,1)}) custom-call(bf16[256,4096]{1,0:T(8,128)(2,1)S(1)} %get-tuple-element.32.tokens.mine, bf16[256,512]{1,0:T(8,128)(2,1)S(1)} %get-tuple-element.33.cot.cot_mine, bf16[8,128,128]{2,1,0:T(8,128)(2,1)S(1)} %get-tuple-element.38.refs_0_, ...), custom_call_target="tpu_custom_call" | custom-call | flops 1073741824 | bytes 6291456 | tf_op jit(solution)/shard_map/pallas_call | solution.py:282
  93.4 0.9 collective-permute-start.34
  94.4 0.4 collective-permute-start.36
  94.9 1.6 %collective-permute-start.37 = (bf16[2,128,128]{2,1,0:T(8,128)(2,1)S(1)}, bf16[2,128,128]{2,1,0:T(8,128)(2,1)S(1)}, u32[]{:S(2)}, u32[]{:S(2)}) collective-permute-start(bf16[2,128,128]{2,1,0:T(8,128)(2,1)S(1)} %collective-permute-done.33.refs_3_), channel_id=1, source_target_pairs={{0,16},{16,0},{1,17},{17,1},{2,18},{18,2},{3,19},{19,3},{4,20},{20... | collective-permute-start | bytes 196616 | tf_op jit(solution)/shard_map/ppermute | solution.py:279
  96.4 3.3 %shard_map.80 = (bf16[256,512]{1,0:T(8,128)(2,1)}, bf16[256,4096]{1,0:T(8,128)(2,1)}) custom-call(bf16[256,4096]{1,0:T(8,128)(2,1)S(1)} %get-tuple-element.32.tokens.mine, bf16[256,512]{1,0:T(8,128)(2,1)S(1)} %get-tuple-element.33.cot.cot_mine, bf16[8,128,128]{2,1,0:T(8,128)(2,1)S(1)} %collective-permute-done.6.refs_0_, ...), custom_call_target="tpu_custom_call", output_to_operand_aliasing={{1}: (11, {})} | custom-call | flops 1073741824 | bytes 6291456 | tf_op jit(solution)/shard_map/pallas_call | solution.py:282
  99.7 1.5 %shard_map.85 = bf16[16,128,128]{2,1,0:T(8,128)(2,1)} custom-call(s32[16]{0:T(128)S(1)} %copy-done, bf16[2,128,128]{2,1,0:T(8,128)(2,1)S(1)} %get-tuple-element.57.refs_0_, bf16[2,128,128]{2,1,0:T(8,128)(2,1)S(1)} %collective-permute-done.31.refs_1_, bf16[2,128,128]{2,1,0:T(8,128)(2,1)S(1)} %collective-permute-done.32.refs_2_, ...), custom_call_target="tpu_custom_call" | custom-call | flops 524288 | bytes 1048576 | tf_op jit(solution)/shard_map/pallas_call | solution.py:282
  (42 shorter events, 1.9 us)
Async XLA Ops:
  0.6 9.3 %copy-start.1 = (bf16[256,512]{1,0:T(8,128)(2,1)S(1)}, bf16[256,512]{1,0:T(8,128)(2,1)}, u32[]{:S(2)}) copy-start(bf16[256,512]{1,0:T(8,128)(2,1)} %refs_1_.1) | copy-start | bytes 786436
  0.6 20.5 %collective-permute-start.20 = (bf16[256,4096]{1,0:T(8,128)(2,1)}, bf16[256,4096]{1,0:T(8,128)(2,1)S(1)}, u32[]{:S(2)}, u32[]{:S(2)}) collective-permute-start(bf16[256,4096]{1,0:T(8,128)(2,1)} %refs_0_.1), channel_id=1, source_target_pairs={{0,16},{16,0},{1,17},{17,1},{2,18},{18,2},{3,19},{19,3},{4,20},{20... | collective-permute-start | bytes 6291464 | tf_op jit(solution)/shard_map/ppermute | solution.py:279
  3.2 3.7 %collective-permute-start = (bf16[2,128,128]{2,1,0:T(8,128)(2,1)S(1)}, bf16[2,128,128]{2,1,0:T(8,128)(2,1)S(1)}, u32[]{:S(2)}, u32[]{:S(2)}) collective-permute-start(bf16[2,128,128]{2,1,0:T(8,128)(2,1)S(1)} %get-tuple-element.35), channel_id=1, source_target_pairs={{0,1},{1,0},{2,3},{3,2},{4,5},{5,4},{6,7},{7,6},{8,9},{9,8},{10,11... | collective-permute-start | bytes 196616 | tf_op jit(solution)/shard_map/ppermute | solution.py:272
  4.4 3.1 %collective-permute-start.1 = (bf16[2,128,128]{2,1,0:T(8,128)(2,1)S(1)}, bf16[2,128,128]{2,1,0:T(8,128)(2,1)S(1)}, u32[]{:S(2)}, u32[]{:S(2)}) collective-permute-start(bf16[2,128,128]{2,1,0:T(8,128)(2,1)S(1)} %get-tuple-element.36), channel_id=1, source_target_pairs={{0,2},{1,3},{2,0},{3,1},{4,6},{5,7},{6,4},{7,5},{8,10},{9,11},{10,... | collective-permute-start | bytes 196616 | tf_op jit(solution)/shard_map/ppermute | solution.py:272
  5.7 4.0 %collective-permute-start.2 = (bf16[2,128,128]{2,1,0:T(8,128)(2,1)S(1)}, bf16[2,128,128]{2,1,0:T(8,128)(2,1)S(1)}, u32[]{:S(2)}, u32[]{:S(2)}) collective-permute-start(bf16[2,128,128]{2,1,0:T(8,128)(2,1)S(1)} %get-tuple-element.37), channel_id=1, source_target_pairs={{0,3},{1,2},{2,1},{3,0},{4,7},{5,6},{6,5},{7,4},{8,11},{9,10},{10,... | collective-permute-start | bytes 196616 | tf_op jit(solution)/shard_map/ppermute | solution.py:272
  9.7 11.5 %collective-permute-start.4 = (bf16[8,128,128]{2,1,0:T(8,128)(2,1)S(1)}, bf16[8,128,128]{2,1,0:T(8,128)(2,1)S(1)}, u32[]{:S(2)}, u32[]{:S(2)}) collective-permute-start(bf16[8,128,128]{2,1,0:T(8,128)(2,1)S(1)} %shard_map.77.refs_0_), channel_id=1, source_target_pairs={{0,12},{1,13},{2,14},{3,15},{4,8},{5,9},{6,10},{7,11},{8,4},{9,5},... | collective-permute-start | bytes 786440 | tf_op jit(solution)/shard_map/ppermute | solution.py:276
  10.0 11.2 %collective-permute-start.21 = (bf16[256,512]{1,0:T(8,128)(2,1)S(1)}, bf16[256,512]{1,0:T(8,128)(2,1)S(1)}, u32[]{:S(2)}, u32[]{:S(2)}) collective-permute-start(bf16[256,512]{1,0:T(8,128)(2,1)S(1)} %copy-done.1), channel_id=1, source_target_pairs={{0,16},{16,0},{1,17},{17,1},{2,18},{18,2},{3,19},{19,3},{4,20},{20... | collective-permute-start | bytes 786440 | tf_op jit(solution)/shard_map/ppermute | solution.py:279
  12.0 12.7 %collective-permute-start.3 = (bf16[8,128,128]{2,1,0:T(8,128)(2,1)S(1)}, bf16[8,128,128]{2,1,0:T(8,128)(2,1)S(1)}, u32[]{:S(2)}, u32[]{:S(2)}) collective-permute-start(bf16[8,128,128]{2,1,0:T(8,128)(2,1)S(1)} %shard_map.77.refs_0_), channel_id=1, source_target_pairs={{0,4},{1,5},{2,6},{3,7},{4,0},{5,1},{6,2},{7,3},{8,12},{9,13},{10,... | collective-permute-start | bytes 786440 | tf_op jit(solution)/shard_map/ppermute | solution.py:276
  21.2 9.1 %collective-permute-start.5 = (bf16[8,128,128]{2,1,0:T(8,128)(2,1)S(1)}, bf16[8,128,128]{2,1,0:T(8,128)(2,1)S(1)}, u32[]{:S(2)}, u32[]{:S(2)}) collective-permute-start(bf16[8,128,128]{2,1,0:T(8,128)(2,1)S(1)} %collective-permute-done.4.refs_3_), channel_id=1, source_target_pairs={{0,4},{1,5},{2,6},{3,7},{4,0},{5,1},{6,2},{7,3},{8,12},{9,13},{10,... | collective-permute-start | bytes 786440 | tf_op jit(solution)/shard_map/ppermute | solution.py:276
  21.2 9.1 %copy-start = (s32[16]{0:T(128)S(1)}, s32[16]{0:T(128)}, u32[]{:S(2)}) copy-start(s32[16]{0:T(128)} %counts.7) | copy-start | bytes 196
  23.5 10.1 %collective-permute-start.23 = (bf16[8,128,128]{2,1,0:T(8,128)(2,1)S(1)}, bf16[8,128,128]{2,1,0:T(8,128)(2,1)S(1)}, u32[]{:S(2)}, u32[]{:S(2)}) collective-permute-start(bf16[8,128,128]{2,1,0:T(8,128)(2,1)S(1)} %get-tuple-element.47), channel_id=1, source_target_pairs={{0,1},{1,0},{2,3},{3,2},{4,5},{5,4},{6,7},{7,6},{8,9},{9,8},{10,11... | collective-permute-start | bytes 786440 | tf_op jit(solution)/shard_map/ppermute | solution.py:272
  23.8 11.0 %collective-permute-start.24 = (bf16[8,128,128]{2,1,0:T(8,128)(2,1)S(1)}, bf16[8,128,128]{2,1,0:T(8,128)(2,1)S(1)}, u32[]{:S(2)}, u32[]{:S(2)}) collective-permute-start(bf16[8,128,128]{2,1,0:T(8,128)(2,1)S(1)} %get-tuple-element.49), channel_id=1, source_target_pairs={{0,2},{1,3},{2,0},{3,1},{4,6},{5,7},{6,4},{7,5},{8,10},{9,11},{10,... | collective-permute-start | bytes 786440 | tf_op jit(solution)/shard_map/ppermute | solution.py:272
  31.8 7.4 %collective-permute-start.6 = (bf16[8,128,128]{2,1,0:T(8,128)(2,1)S(1)}, bf16[8,128,128]{2,1,0:T(8,128)(2,1)S(1)}, u32[]{:S(2)}, u32[]{:S(2)}) collective-permute-start(bf16[8,128,128]{2,1,0:T(8,128)(2,1)S(1)} %get-tuple-element.38.refs_0_), channel_id=1, source_target_pairs={{0,2},{1,3},{2,0},{3,1},{4,6},{5,7},{6,4},{7,5},{8,10},{9,11},{10,... | collective-permute-start | bytes 786440 | tf_op jit(solution)/shard_map/ppermute | solution.py:272
  32.1 12.8 %collective-permute-start.7 = (bf16[8,128,128]{2,1,0:T(8,128)(2,1)S(1)}, bf16[8,128,128]{2,1,0:T(8,128)(2,1)S(1)}, u32[]{:S(2)}, u32[]{:S(2)}) collective-permute-start(bf16[8,128,128]{2,1,0:T(8,128)(2,1)S(1)} %get-tuple-element.39.refs_1_), channel_id=1, source_target_pairs={{0,2},{1,3},{2,0},{3,1},{4,6},{5,7},{6,4},{7,5},{8,10},{9,11},{10,... | collective-permute-start | bytes 786440 | tf_op jit(solution)/shard_map/ppermute | solution.py:272
  33.3 11.8 %collective-permute-start.8 = (bf16[8,128,128]{2,1,0:T(8,128)(2,1)S(1)}, bf16[8,128,128]{2,1,0:T(8,128)(2,1)S(1)}, u32[]{:S(2)}, u32[]{:S(2)}) collective-permute-start(bf16[8,128,128]{2,1,0:T(8,128)(2,1)S(1)} %get-tuple-element.38.refs_0_), channel_id=1, source_target_pairs={{0,1},{1,0},{2,3},{3,2},{4,5},{5,4},{6,7},{7,6},{8,9},{9,8},{10,11... | collective-permute-start | bytes 786440 | tf_op jit(solution)/shard_map/ppermute | solution.py:272
  33.6 12.7 %collective-permute-start.22 = (bf16[8,128,128]{2,1,0:T(8,128)(2,1)S(1)}, bf16[8,128,128]{2,1,0:T(8,128)(2,1)S(1)}, u32[]{:S(2)}, u32[]{:S(2)}) collective-permute-start(bf16[8,128,128]{2,1,0:T(8,128)(2,1)S(1)} %get-tuple-element.45), channel_id=1, source_target_pairs={{0,1},{1,0},{2,3},{3,2},{4,5},{5,4},{6,7},{7,6},{8,9},{9,8},{10,11... | collective-permute-start | bytes 786440 | tf_op jit(solution)/shard_map/ppermute | solution.py:272
  34.8 15.7 %collective-permute-start.27 = (bf16[8,128,128]{2,1,0:T(8,128)(2,1)S(1)}, bf16[8,128,128]{2,1,0:T(8,128)(2,1)S(1)}, u32[]{:S(2)}, u32[]{:S(2)}) collective-permute-start(bf16[8,128,128]{2,1,0:T(8,128)(2,1)S(1)} %get-tuple-element.52), channel_id=1, source_target_pairs={{0,2},{1,3},{2,0},{3,1},{4,6},{5,7},{6,4},{7,5},{8,10},{9,11},{10,... | collective-permute-start | bytes 786440 | tf_op jit(solution)/shard_map/ppermute | solution.py:272
  39.3 16.9 %collective-permute-start.25 = (bf16[8,128,128]{2,1,0:T(8,128)(2,1)S(1)}, bf16[8,128,128]{2,1,0:T(8,128)(2,1)S(1)}, u32[]{:S(2)}, u32[]{:S(2)}) collective-permute-start(bf16[8,128,128]{2,1,0:T(8,128)(2,1)S(1)} %get-tuple-element.50), channel_id=1, source_target_pairs={{0,2},{1,3},{2,0},{3,1},{4,6},{5,7},{6,4},{7,5},{8,10},{9,11},{10,... | collective-permute-start | bytes 786440 | tf_op jit(solution)/shard_map/ppermute | solution.py:272
  44.9 11.4 %collective-permute-start.26 = (bf16[8,128,128]{2,1,0:T(8,128)(2,1)S(1)}, bf16[8,128,128]{2,1,0:T(8,128)(2,1)S(1)}, u32[]{:S(2)}, u32[]{:S(2)}) collective-permute-start(bf16[8,128,128]{2,1,0:T(8,128)(2,1)S(1)} %get-tuple-element.51), channel_id=1, source_target_pairs={{0,1},{1,0},{2,3},{3,2},{4,5},{5,4},{6,7},{7,6},{8,9},{9,8},{10,11... | collective-permute-start | bytes 786440 | tf_op jit(solution)/shard_map/ppermute | solution.py:272
  45.1 12.4 %collective-permute-start.15 = (bf16[8,128,128]{2,1,0:T(8,128)(2,1)S(1)}, bf16[8,128,128]{2,1,0:T(8,128)(2,1)S(1)}, u32[]{:S(2)}, u32[]{:S(2)}) collective-permute-start(bf16[8,128,128]{2,1,0:T(8,128)(2,1)S(1)} %get-tuple-element.39.refs_1_), channel_id=1, source_target_pairs={{0,1},{1,0},{2,3},{3,2},{4,5},{5,4},{6,7},{7,6},{8,9},{9,8},{10,11... | collective-permute-start | bytes 786440 | tf_op jit(solution)/shard_map/ppermute | solution.py:272
  46.3 13.2 %collective-permute-start.16 = (bf16[8,128,128]{2,1,0:T(8,128)(2,1)S(1)}, bf16[8,128,128]{2,1,0:T(8,128)(2,1)S(1)}, u32[]{:S(2)}, u32[]{:S(2)}) collective-permute-start(bf16[8,128,128]{2,1,0:T(8,128)(2,1)S(1)} %get-tuple-element.38.refs_0_), channel_id=1, source_target_pairs={{0,16},{16,0},{1,17},{17,1},{2,18},{18,2},{3,19},{19,3},{4,20},{20... | collective-permute-start | bytes 786440 | tf_op jit(solution)/shard_map/ppermute | solution.py:279
  50.5 11.3 %collective-permute-start.17 = (bf16[8,128,128]{2,1,0:T(8,128)(2,1)S(1)}, bf16[8,128,128]{2,1,0:T(8,128)(2,1)S(1)}, u32[]{:S(2)}, u32[]{:S(2)}) collective-permute-start(bf16[8,128,128]{2,1,0:T(8,128)(2,1)S(1)} %get-tuple-element.39.refs_1_), channel_id=1, source_target_pairs={{0,16},{16,0},{1,17},{17,1},{2,18},{18,2},{3,19},{19,3},{4,20},{20... | collective-permute-start | bytes 786440 | tf_op jit(solution)/shard_map/ppermute | solution.py:279
  56.1 6.5 %collective-permute-start.9 = (bf16[8,128,128]{2,1,0:T(8,128)(2,1)S(1)}, bf16[8,128,128]{2,1,0:T(8,128)(2,1)S(1)}, u32[]{:S(2)}, u32[]{:S(2)}) collective-permute-start(bf16[8,128,128]{2,1,0:T(8,128)(2,1)S(1)} %collective-permute-done.8.refs_2_), channel_id=1, source_target_pairs={{0,2},{1,3},{2,0},{3,1},{4,6},{5,7},{6,4},{7,5},{8,10},{9,11},{10,... | collective-permute-start | bytes 786440 | tf_op jit(solution)/shard_map/ppermute | solution.py:272
  56.3 6.8 %collective-permute-start.10 = (bf16[8,128,128]{2,1,0:T(8,128)(2,1)S(1)}, bf16[8,128,128]{2,1,0:T(8,128)(2,1)S(1)}, u32[]{:S(2)}, u32[]{:S(2)}) collective-permute-start(bf16[8,128,128]{2,1,0:T(8,128)(2,1)S(1)} %collective-permute-done.7.refs_1_), channel_id=1, source_target_pairs={{0,1},{1,0},{2,3},{3,2},{4,5},{5,4},{6,7},{7,6},{8,9},{9,8},{10,11... | collective-permute-start | bytes 786440 | tf_op jit(solution)/shard_map/ppermute | solution.py:272
  57.5 7.5 %collective-permute-start.11 = (bf16[8,128,128]{2,1,0:T(8,128)(2,1)S(1)}, bf16[8,128,128]{2,1,0:T(8,128)(2,1)S(1)}, u32[]{:S(2)}, u32[]{:S(2)}) collective-permute-start(bf16[8,128,128]{2,1,0:T(8,128)(2,1)S(1)} %collective-permute-done.6.refs_0_), channel_id=1, source_target_pairs={{0,16},{16,0},{1,17},{17,1},{2,18},{18,2},{3,19},{19,3},{4,20},{20... | collective-permute-start | bytes 786440 | tf_op jit(solution)/shard_map/ppermute | solution.py:279
  59.5 11.5 %collective-permute-start.28 = (bf16[8,128,128]{2,1,0:T(8,128)(2,1)S(1)}, bf16[8,128,128]{2,1,0:T(8,128)(2,1)S(1)}, u32[]{:S(2)}, u32[]{:S(2)}) collective-permute-start(bf16[8,128,128]{2,1,0:T(8,128)(2,1)S(1)} %get-tuple-element.54), channel_id=1, source_target_pairs={{0,4},{1,5},{2,6},{3,7},{4,0},{5,1},{6,2},{7,3},{8,12},{9,13},{10,... | collective-permute-start | bytes 786440 | tf_op jit(solution)/shard_map/ppermute | solution.py:276
  61.8 11.3 %collective-permute-start.29 = (bf16[8,128,128]{2,1,0:T(8,128)(2,1)S(1)}, bf16[8,128,128]{2,1,0:T(8,128)(2,1)S(1)}, u32[]{:S(2)}, u32[]{:S(2)}) collective-permute-start(bf16[8,128,128]{2,1,0:T(8,128)(2,1)S(1)} %get-tuple-element.55), channel_id=1, source_target_pairs={{0,8},{1,9},{2,10},{3,11},{4,12},{5,13},{6,14},{7,15},{8,0},{9,1},... | collective-permute-start | bytes 786440 | tf_op jit(solution)/shard_map/ppermute | solution.py:276
  62.6 23.6 %collective-permute-start.30 = (bf16[8,128,128]{2,1,0:T(8,128)(2,1)S(1)}, bf16[8,128,128]{2,1,0:T(8,128)(2,1)S(1)}, u32[]{:S(2)}, u32[]{:S(2)}) collective-permute-start(bf16[8,128,128]{2,1,0:T(8,128)(2,1)S(1)} %get-tuple-element.56), channel_id=1, source_target_pairs={{0,12},{1,13},{2,14},{3,15},{4,8},{5,9},{6,10},{7,11},{8,4},{9,5},... | collective-permute-start | bytes 786440 | tf_op jit(solution)/shard_map/ppermute | solution.py:276
  63.0 25.1 %collective-permute-start.12 = (bf16[8,128,128]{2,1,0:T(8,128)(2,1)S(1)}, bf16[8,128,128]{2,1,0:T(8,128)(2,1)S(1)}, u32[]{:S(2)}, u32[]{:S(2)}) collective-permute-start(bf16[8,128,128]{2,1,0:T(8,128)(2,1)S(1)} %collective-permute-done.7.refs_1_), channel_id=1, source_target_pairs={{0,16},{16,0},{1,17},{17,1},{2,18},{18,2},{3,19},{19,3},{4,20},{20... | collective-permute-start | bytes 786440 | tf_op jit(solution)/shard_map/ppermute | solution.py:279
  65.0 24.5 %collective-permute-start.18 = (bf16[8,128,128]{2,1,0:T(8,128)(2,1)S(1)}, bf16[8,128,128]{2,1,0:T(8,128)(2,1)S(1)}, u32[]{:S(2)}, u32[]{:S(2)}) collective-permute-start(bf16[8,128,128]{2,1,0:T(8,128)(2,1)S(1)} %collective-permute-done.8.refs_2_), channel_id=1, source_target_pairs={{0,16},{16,0},{1,17},{17,1},{2,18},{18,2},{3,19},{19,3},{4,20},{20... | collective-permute-start | bytes 786440 | tf_op jit(solution)/shard_map/ppermute | solution.py:279
  71.1 19.6 %collective-permute-start.19 = (bf16[8,128,128]{2,1,0:T(8,128)(2,1)S(1)}, bf16[8,128,128]{2,1,0:T(8,128)(2,1)S(1)}, u32[]{:S(2)}, u32[]{:S(2)}) collective-permute-start(bf16[8,128,128]{2,1,0:T(8,128)(2,1)S(1)} %collective-permute-done.15.refs_3_), channel_id=1, source_target_pairs={{0,16},{16,0},{1,17},{17,1},{2,18},{18,2},{3,19},{19,3},{4,20},{20... | collective-permute-start | bytes 786440 | tf_op jit(solution)/shard_map/ppermute | solution.py:279
  73.1 20.4 %collective-permute-start.13 = (bf16[8,128,128]{2,1,0:T(8,128)(2,1)S(1)}, bf16[8,128,128]{2,1,0:T(8,128)(2,1)S(1)}, u32[]{:S(2)}, u32[]{:S(2)}) collective-permute-start(bf16[8,128,128]{2,1,0:T(8,128)(2,1)S(1)} %collective-permute-done.9.refs_2_), channel_id=1, source_target_pairs={{0,16},{16,0},{1,17},{17,1},{2,18},{18,2},{3,19},{19,3},{4,20},{20... | collective-permute-start | bytes 786440 | tf_op jit(solution)/shard_map/ppermute | solution.py:279
  86.2 10.2 %collective-permute-start.14 = (bf16[8,128,128]{2,1,0:T(8,128)(2,1)S(1)}, bf16[8,128,128]{2,1,0:T(8,128)(2,1)S(1)}, u32[]{:S(2)}, u32[]{:S(2)}) collective-permute-start(bf16[8,128,128]{2,1,0:T(8,128)(2,1)S(1)} %collective-permute-done.10.refs_3_), channel_id=1, source_target_pairs={{0,16},{16,0},{1,17},{17,1},{2,18},{18,2},{3,19},{19,3},{4,20},{20... | collective-permute-start | bytes 786440 | tf_op jit(solution)/shard_map/ppermute | solution.py:279
  88.2 6.2 %collective-permute-start.31 = (bf16[2,128,128]{2,1,0:T(8,128)(2,1)S(1)}, bf16[2,128,128]{2,1,0:T(8,128)(2,1)S(1)}, u32[]{:S(2)}, u32[]{:S(2)}) collective-permute-start(bf16[2,128,128]{2,1,0:T(8,128)(2,1)S(1)} %get-tuple-element.58), channel_id=1, source_target_pairs={{0,1},{1,0},{2,3},{3,2},{4,5},{5,4},{6,7},{7,6},{8,9},{9,8},{10,11... | collective-permute-start | bytes 196616 | tf_op jit(solution)/shard_map/ppermute | solution.py:272
  89.4 5.0 %collective-permute-start.32 = (bf16[2,128,128]{2,1,0:T(8,128)(2,1)S(1)}, bf16[2,128,128]{2,1,0:T(8,128)(2,1)S(1)}, u32[]{:S(2)}, u32[]{:S(2)}) collective-permute-start(bf16[2,128,128]{2,1,0:T(8,128)(2,1)S(1)} %get-tuple-element.59), channel_id=1, source_target_pairs={{0,2},{1,3},{2,0},{3,1},{4,6},{5,7},{6,4},{7,5},{8,10},{9,11},{10,... | collective-permute-start | bytes 196616 | tf_op jit(solution)/shard_map/ppermute | solution.py:272
  90.7 4.2 %collective-permute-start.33 = (bf16[2,128,128]{2,1,0:T(8,128)(2,1)S(1)}, bf16[2,128,128]{2,1,0:T(8,128)(2,1)S(1)}, u32[]{:S(2)}, u32[]{:S(2)}) collective-permute-start(bf16[2,128,128]{2,1,0:T(8,128)(2,1)S(1)} %get-tuple-element.60), channel_id=1, source_target_pairs={{0,3},{1,2},{2,1},{3,0},{4,7},{5,6},{6,5},{7,4},{8,11},{9,10},{10,... | collective-permute-start | bytes 196616 | tf_op jit(solution)/shard_map/ppermute | solution.py:272
  93.4 6.3 %collective-permute-start.34 = (bf16[2,128,128]{2,1,0:T(8,128)(2,1)S(1)}, bf16[2,128,128]{2,1,0:T(8,128)(2,1)S(1)}, u32[]{:S(2)}, u32[]{:S(2)}) collective-permute-start(bf16[2,128,128]{2,1,0:T(8,128)(2,1)S(1)} %get-tuple-element.57.refs_0_), channel_id=1, source_target_pairs={{0,16},{16,0},{1,17},{17,1},{2,18},{18,2},{3,19},{19,3},{4,20},{20... | collective-permute-start | bytes 196616 | tf_op jit(solution)/shard_map/ppermute | solution.py:279
  94.4 5.4 %collective-permute-start.35 = (bf16[2,128,128]{2,1,0:T(8,128)(2,1)S(1)}, bf16[2,128,128]{2,1,0:T(8,128)(2,1)S(1)}, u32[]{:S(2)}, u32[]{:S(2)}) collective-permute-start(bf16[2,128,128]{2,1,0:T(8,128)(2,1)S(1)} %collective-permute-done.31.refs_1_), channel_id=1, source_target_pairs={{0,16},{16,0},{1,17},{17,1},{2,18},{18,2},{3,19},{19,3},{4,20},{20... | collective-permute-start | bytes 196616 | tf_op jit(solution)/shard_map/ppermute | solution.py:279
  94.4 5.3 %collective-permute-start.36 = (bf16[2,128,128]{2,1,0:T(8,128)(2,1)S(1)}, bf16[2,128,128]{2,1,0:T(8,128)(2,1)S(1)}, u32[]{:S(2)}, u32[]{:S(2)}) collective-permute-start(bf16[2,128,128]{2,1,0:T(8,128)(2,1)S(1)} %collective-permute-done.32.refs_2_), channel_id=1, source_target_pairs={{0,16},{16,0},{1,17},{17,1},{2,18},{18,2},{3,19},{19,3},{4,20},{20... | collective-permute-start | bytes 196616 | tf_op jit(solution)/shard_map/ppermute | solution.py:279
  94.9 4.9 %collective-permute-start.37 = (bf16[2,128,128]{2,1,0:T(8,128)(2,1)S(1)}, bf16[2,128,128]{2,1,0:T(8,128)(2,1)S(1)}, u32[]{:S(2)}, u32[]{:S(2)}) collective-permute-start(bf16[2,128,128]{2,1,0:T(8,128)(2,1)S(1)} %collective-permute-done.33.refs_3_), channel_id=1, source_target_pairs={{0,16},{16,0},{1,17},{17,1},{2,18},{18,2},{3,19},{19,3},{4,20},{20... | collective-permute-start | bytes 196616 | tf_op jit(solution)/shard_map/ppermute | solution.py:279

commit v4 on v3

--- a/solution.py
+++ b/solution.py
@@ -129,7 +129,7 @@
 
 
 def fold_kernel(*refs):
-    ins, outs = refs[:4], refs[4:]
+    ins, outs = refs[: 2 * len(refs) // 3], refs[2 * len(refs) // 3 :]
     for n, out in enumerate(outs):
         value = ins[2 * n][...].astype(jnp.float32) + ins[2 * n + 1][...].astype(jnp.float32)
         out[...] = value.astype(BF16)
@@ -156,8 +156,8 @@
         out[...] = total[pl.ds(window(counts, cls, target, blocks, span), span)]
 
 
-def owner_kernel(blocks, reach, span, planes, counts, *refs):
-    ins, outs, total = refs[:planes], refs[planes:-1], refs[-1]
+def owner_kernel(blocks, reach, span, counts, *refs):
+    ins, outs, total = refs[: -INNER - 1], refs[-INNER - 1 : -1], refs[-1]
     core, plane, place, _ = here()
     cls = class_of(core, place)
     acc = ins[0][...].astype(jnp.float32)
@@ -382,13 +382,26 @@
         cost_estimate=cost(64 * block_bytes, 96 * block_bytes),
         compiler_params=room(12),
     )
-    sums = [windows[0]] + [along(windows[s], s) for s in range(1, planes)]
+    if planes == 4:
+        through = call(
+            fold_kernel,
+            windows[3],
+            along(windows[2], 1),
+            out_shape=[many(span)],
+            in_specs=[whole()] * 2,
+            out_specs=[whole()],
+            cost_estimate=cost(8 * block_bytes, 24 * block_bytes),
+            compiler_params=room(8),
+        )
+        sums = [windows[0], along(windows[1], 1), along(through[0], 3)]
+    else:
+        sums = [windows[0]] + [along(windows[s], s) for s in range(1, planes)]
 
     sent = call(
-        functools.partial(owner_kernel, blocks, reach, span, planes),
+        functools.partial(owner_kernel, blocks, reach, span),
         counts, *sums,
         out_shape=[many(reach)] * INNER,
-        in_specs=[scalars()] + [whole()] * planes,
+        in_specs=[scalars()] + [whole()] * len(sums),
         out_specs=[whole()] * INNER,
         scratch_shapes=[VMEM((span, tile, tile), BF16)],
         cost_estimate=cost(32 * block_bytes, 48 * block_bytes),

time: 101 us -> 80.8 us (0.80)
  the two profiles are of different devices: /device:TPU:17 before, /device:TPU:0 now
where the time goes in v4:
time: 80.8 us; the launch traced here: 80.7 us
  waiting for transfers between devices  36.1 us (45%)
  starting transfers between devices  28.9 us (36%)
  Pallas kernels  14.8 us (18%)
  between operations  0.81 us (1%)
    ppermute x18, waiting for transfers between devices, beside(): return lax.ppermute(value, 'fsdp', [(i, i ^ m) for i in range(owners)])  22.2 us
    ppermute x18, starting transfers between devices, beside(): return lax.ppermute(value, 'fsdp', [(i, i ^ m) for i in range(owners)])  19.2 us
    pallas_call x11, Pallas kernels, call(): return pl.pallas_call(kernel, **how)(*operands)  14.8 us
    ppermute x6, waiting for transfers between devices, along(): return lax.ppermute(value, 'fsdp', pairs)  13.9 us
    ppermute x6, starting transfers between devices, along(): return lax.ppermute(value, 'fsdp', pairs)  7.4 us
    ppermute x14, starting transfers between devices, across(): return lax.ppermute(value, 'dp', [(0, 1), (1, 0)])  2.32 us
  transfers between devices with their start and end apart: 38, of which 14 were waited for; matrix products, arithmetic and copies ran while one was open for 0% of the time, Pallas kernels for 17%

profile of v4, /device:TPU:0, one launch (start us, length us, event | category | flops | bytes accessed | tf_op | source)
XLA Modules:
  0.0 80.7 jit_solution(5249396136361857265)
XLA Ops:
  0.6 0.6 collective-permute-start.20
  1.3 1.8 %shard_map.76 = (bf16[256,4096]{1,0:T(8,128)(2,1)S(1)}, bf16[256,512]{1,0:T(8,128)(2,1)S(1)}, bf16[2,128,128]{2,1,0:T(8,128)(2,1)S(1)}, bf16[2,128,128]{2,1,0:T(...) custom-call(s32[16]{0:T(128)} %counts.7, f32[16]{0:T(128)} %scales_in.1, ...), custom_call_target="tpu_custom_call" | custom-call | flops 262144 | bytes 786432 | tf_op jit(solution)/shard_map/pallas_call | solution.py:282
  3.1 3.0 %collective-permute-start = (bf16[2,128,128]{2,1,0:T(8,128)(2,1)S(1)}, bf16[2,128,128]{2,1,0:T(8,128)(2,1)S(1)}, u32[]{:S(2)}, u32[]{:S(2)}) collective-permute-start(bf16[2,128,128]{2,1,0:T(8,128)(2,1)S(1)} %get-tuple-element.35), channel_id=1, source_target_pairs={{0,1},{1,0},{2,3},{3,2},{4,5},{5,4},{6,7},{7,6},{8,9},{9,8},{10,11... | collective-permute-start | bytes 196616 | tf_op jit(solution)/shard_map/ppermute | solution.py:272
  6.0 1.5 %collective-permute-start.1 = (bf16[2,128,128]{2,1,0:T(8,128)(2,1)S(1)}, bf16[2,128,128]{2,1,0:T(8,128)(2,1)S(1)}, u32[]{:S(2)}, u32[]{:S(2)}) collective-permute-start(bf16[2,128,128]{2,1,0:T(8,128)(2,1)S(1)} %get-tuple-element.36), channel_id=1, source_target_pairs={{0,2},{1,3},{2,0},{3,1},{4,6},{5,7},{6,4},{7,5},{8,10},{9,11},{10,... | collective-permute-start | bytes 196616 | tf_op jit(solution)/shard_map/ppermute | solution.py:272
  7.6 0.8 collective-permute-done.refs_1_
  8.4 1.9 %collective-permute-done.1.refs_2_ = bf16[2,128,128]{2,1,0:T(8,128)(2,1)S(1)} collective-permute-done((bf16[2,128,128]{2,1,0:T(8,128)(2,1)S(1)}, bf16[2,128,128]{2,1,0:T(8,128)(2,1)S(1)}, u32[]{:S(2)}, u32[]{:S(2)}) %collective-permute-start.1) | collective-permute-done | bytes 65568 | tf_op jit(solution)/shard_map/ppermute | solution.py:272
  10.3 2.4 %collective-permute-done.2.refs_3_ = bf16[2,128,128]{2,1,0:T(8,128)(2,1)S(1)} collective-permute-done((bf16[2,128,128]{2,1,0:T(8,128)(2,1)S(1)}, bf16[2,128,128]{2,1,0:T(8,128)(2,1)S(1)}, u32[]{:S(2)}, u32[]{:S(2)}) %collective-permute-start.2) | collective-permute-done | bytes 65568 | tf_op jit(solution)/shard_map/ppermute | solution.py:272
  12.7 3.7 %collective-permute-start.4 = (bf16[8,128,128]{2,1,0:T(8,128)(2,1)S(1)}, bf16[8,128,128]{2,1,0:T(8,128)(2,1)S(1)}, u32[]{:S(2)}, u32[]{:S(2)}) collective-permute-start(bf16[8,128,128]{2,1,0:T(8,128)(2,1)S(1)} %shard_map.77.refs_0_), channel_id=1, source_target_pairs={{0,12},{1,13},{2,14},{3,15},{4,8},{5,9},{6,10},{7,11},{8,4},{9,5},... | collective-permute-start | bytes 786440 | tf_op jit(solution)/shard_map/ppermute | solution.py:276
  16.4 2.2 %shard_map.81 = (bf16[16,128,128]{2,1,0:T(8,128)(2,1)S(1)}, bf16[8,128,128]{2,1,0:T(8,128)(2,1)S(1)}, bf16[8,128,128]{2,1,0:T(8,128)(2,1)S(1)}, bf16[8,128,128]{...) custom-call(bf16[256,4096]{1,0:T(8,128)(2,1)S(1)} %get-tuple-element, ...), custom_call_target="tpu_custom_call" | custom-call | flops 1073741824 | bytes 6291456 | tf_op jit(solution)/shard_map/pallas_call | solution.py:282
  18.7 0.6 collective-permute-start.23
  19.3 0.5 collective-permute-start.24
  19.8 3.7 %collective-permute-done.4.refs_3_ = bf16[8,128,128]{2,1,0:T(8,128)(2,1)S(1)} collective-permute-done((bf16[8,128,128]{2,1,0:T(8,128)(2,1)S(1)}, bf16[8,128,128]{2,1,0:T(8,128)(2,1)S(1)}, u32[]{:S(2)}, u32[]{:S(2)}) %collective-permute-start.4) | collective-permute-done | bytes 262176 | tf_op jit(solution)/shard_map/ppermute | solution.py:276
  23.5 3.0 %collective-permute-start.5 = (bf16[8,128,128]{2,1,0:T(8,128)(2,1)S(1)}, bf16[8,128,128]{2,1,0:T(8,128)(2,1)S(1)}, u32[]{:S(2)}, u32[]{:S(2)}) collective-permute-start(bf16[8,128,128]{2,1,0:T(8,128)(2,1)S(1)} %collective-permute-done.4.refs_3_), channel_id=1, source_target_pairs={{0,4},{1,5},{2,6},{3,7},{4,0},{5,1},{6,2},{7,3},{8,12},{9,13},{10,... | collective-permute-start | bytes 786440 | tf_op jit(solution)/shard_map/ppermute | solution.py:276
  26.6 0.7 collective-permute-start.22
  27.3 0.6 collective-permute-start.27
  27.9 0.1 shard_map.82
  28.0 1.5 %collective-permute-start.25 = (bf16[8,128,128]{2,1,0:T(8,128)(2,1)S(1)}, bf16[8,128,128]{2,1,0:T(8,128)(2,1)S(1)}, u32[]{:S(2)}, u32[]{:S(2)}) collective-permute-start(bf16[8,128,128]{2,1,0:T(8,128)(2,1)S(1)} %get-tuple-element.50), channel_id=1, source_target_pairs={{0,2},{1,3},{2,0},{3,1},{4,6},{5,7},{6,4},{7,5},{8,10},{9,11},{10,... | collective-permute-start | bytes 786440 | tf_op jit(solution)/shard_map/ppermute | solution.py:272
  29.5 1.3 %collective-permute-start.26 = (bf16[8,128,128]{2,1,0:T(8,128)(2,1)S(1)}, bf16[8,128,128]{2,1,0:T(8,128)(2,1)S(1)}, u32[]{:S(2)}, u32[]{:S(2)}) collective-permute-start(bf16[8,128,128]{2,1,0:T(8,128)(2,1)S(1)} %get-tuple-element.51), channel_id=1, source_target_pairs={{0,1},{1,0},{2,3},{3,2},{4,5},{5,4},{6,7},{7,6},{8,9},{9,8},{10,11... | collective-permute-start | bytes 786440 | tf_op jit(solution)/shard_map/ppermute | solution.py:272
  30.8 2.2 %collective-permute-done.5.refs_2_ = bf16[8,128,128]{2,1,0:T(8,128)(2,1)S(1)} collective-permute-done((bf16[8,128,128]{2,1,0:T(8,128)(2,1)S(1)}, bf16[8,128,128]{2,1,0:T(8,128)(2,1)S(1)}, u32[]{:S(2)}, u32[]{:S(2)}) %collective-permute-start.5) | collective-permute-done | bytes 262176 | tf_op jit(solution)/shard_map/ppermute | solution.py:276
  33.1 1.5 %shard_map.78 = (bf16[8,128,128]{2,1,0:T(8,128)(2,1)S(1)}, bf16[8,128,128]{2,1,0:T(8,128)(2,1)S(1)}) custom-call(s32[16]{0:T(128)S(1)} %copy-done, bf16[8,128,128]{2,1,0:T(8,128)(2,1)S(1)} %shard_map.77.refs_0_, bf16[8,128,128]{2,1,0:T(8,128)(2,1)S(1)} %collective-permute-done.3.refs_1_, bf16[8,128,128]{2,1,0:T(8,128)(2,1)S(1)} %collective-permute-done.5.refs_2_, ...), custom_call_target="tpu_custom_call" | custom-call | flops 1048576 | bytes 1572864 | tf_op jit(solution)/shard_map/pallas_call | solution.py:282
  34.6 0.6 collective-permute-start.6
  35.3 0.5 collective-permute-done.22.refs_0_
  35.8 1.0 %collective-permute-start.7 = (bf16[8,128,128]{2,1,0:T(8,128)(2,1)S(1)}, bf16[8,128,128]{2,1,0:T(8,128)(2,1)S(1)}, u32[]{:S(2)}, u32[]{:S(2)}) collective-permute-start(bf16[8,128,128]{2,1,0:T(8,128)(2,1)S(1)} %get-tuple-element.39.refs_1_), channel_id=1, source_target_pairs={{0,2},{1,3},{2,0},{3,1},{4,6},{5,7},{6,4},{7,5},{8,10},{9,11},{10,... | collective-permute-start | bytes 786440 | tf_op jit(solution)/shard_map/ppermute | solution.py:272
  36.7 1.0 %collective-permute-start.8 = (bf16[8,128,128]{2,1,0:T(8,128)(2,1)S(1)}, bf16[8,128,128]{2,1,0:T(8,128)(2,1)S(1)}, u32[]{:S(2)}, u32[]{:S(2)}) collective-permute-start(bf16[8,128,128]{2,1,0:T(8,128)(2,1)S(1)} %get-tuple-element.38.refs_0_), channel_id=1, source_target_pairs={{0,1},{1,0},{2,3},{3,2},{4,5},{5,4},{6,7},{7,6},{8,9},{9,8},{10,11... | collective-permute-start | bytes 786440 | tf_op jit(solution)/shard_map/ppermute | solution.py:272
  37.8 4.3 %collective-permute-done.25.refs_1_ = bf16[8,128,128]{2,1,0:T(8,128)(2,1)S(1)} collective-permute-done((bf16[8,128,128]{2,1,0:T(8,128)(2,1)S(1)}, bf16[8,128,128]{2,1,0:T(8,128)(2,1)S(1)}, u32[]{:S(2)}, u32[]{:S(2)}) %collective-permute-start.25) | collective-permute-done | bytes 262176 | tf_op jit(solution)/shard_map/ppermute | solution.py:272
  42.1 1.3 %collective-permute-start.15 = (bf16[8,128,128]{2,1,0:T(8,128)(2,1)S(1)}, bf16[8,128,128]{2,1,0:T(8,128)(2,1)S(1)}, u32[]{:S(2)}, u32[]{:S(2)}) collective-permute-start(bf16[8,128,128]{2,1,0:T(8,128)(2,1)S(1)} %get-tuple-element.39.refs_1_), channel_id=1, source_target_pairs={{0,1},{1,0},{2,3},{3,2},{4,5},{5,4},{6,7},{7,6},{8,9},{9,8},{10,11... | collective-permute-start | bytes 786440 | tf_op jit(solution)/shard_map/ppermute | solution.py:272
  43.4 1.0 %shard_map.83 = (bf16[8,128,128]{2,1,0:T(8,128)(2,1)S(1)}, bf16[8,128,128]{2,1,0:T(8,128)(2,1)S(1)}, bf16[8,128,128]{2,1,0:T(8,128)(2,1)S(1)}, bf16[8,128,128]{2,1,0:T(8,128)(2,1)S(1)}) custom-call(s32[16]{0:T(128)S(1)} %copy-done, bf16[16,128,128]{2,1,0:T(8,128)(2,1)S(1)} %get-tuple-element.44.own, ...), custom_call_target="tpu_custom_call" | custom-call | flops 2097152 | bytes 3145728 | tf_op jit(solution)/shard_map/pallas_call | solution.py:282
  44.4 3.3 %collective-permute-done.6.refs_0_ = bf16[8,128,128]{2,1,0:T(8,128)(2,1)S(1)} collective-permute-done((bf16[8,128,128]{2,1,0:T(8,128)(2,1)S(1)}, bf16[8,128,128]{2,1,0:T(8,128)(2,1)S(1)}, u32[]{:S(2)}, u32[]{:S(2)}) %collective-permute-start.6) | collective-permute-done | bytes 262176 | tf_op jit(solution)/shard_map/ppermute | solution.py:272
  47.7 3.3 %collective-permute-done.7.refs_1_ = bf16[8,128,128]{2,1,0:T(8,128)(2,1)S(1)} collective-permute-done((bf16[8,128,128]{2,1,0:T(8,128)(2,1)S(1)}, bf16[8,128,128]{2,1,0:T(8,128)(2,1)S(1)}, u32[]{:S(2)}, u32[]{:S(2)}) %collective-permute-start.7) | collective-permute-done | bytes 262176 | tf_op jit(solution)/shard_map/ppermute | solution.py:272
  50.9 0.6 collective-permute-start.9
  51.6 1.3 %collective-permute-start.10 = (bf16[8,128,128]{2,1,0:T(8,128)(2,1)S(1)}, bf16[8,128,128]{2,1,0:T(8,128)(2,1)S(1)}, u32[]{:S(2)}, u32[]{:S(2)}) collective-permute-start(bf16[8,128,128]{2,1,0:T(8,128)(2,1)S(1)} %collective-permute-done.7.refs_1_), channel_id=1, source_target_pairs={{0,1},{1,0},{2,3},{3,2},{4,5},{5,4},{6,7},{7,6},{8,9},{9,8},{10,11... | collective-permute-start | bytes 786440 | tf_op jit(solution)/shard_map/ppermute | solution.py:272
  52.9 1.2 %collective-permute-done.29.refs_1_ = bf16[8,128,128]{2,1,0:T(8,128)(2,1)S(1)} collective-permute-done((bf16[8,128,128]{2,1,0:T(8,128)(2,1)S(1)}, bf16[8,128,128]{2,1,0:T(8,128)(2,1)S(1)}, u32[]{:S(2)}, u32[]{:S(2)}) %collective-permute-start.29) | collective-permute-done | bytes 262176 | tf_op jit(solution)/shard_map/ppermute | solution.py:276
  54.1 0.7 collective-permute-start.30
  54.8 4.8 %collective-permute-done.9.refs_2_ = bf16[8,128,128]{2,1,0:T(8,128)(2,1)S(1)} collective-permute-done((bf16[8,128,128]{2,1,0:T(8,128)(2,1)S(1)}, bf16[8,128,128]{2,1,0:T(8,128)(2,1)S(1)}, u32[]{:S(2)}, u32[]{:S(2)}) %collective-permute-start.9) | collective-permute-done | bytes 262176 | tf_op jit(solution)/shard_map/ppermute | solution.py:272
  59.7 0.3 collective-permute-done.10.refs_3_
  60.0 0.2 collective-permute-start.18
  60.2 0.3 collective-permute-start.19
  60.5 6.7 %collective-permute-done.28.refs_1_ = bf16[8,128,128]{2,1,0:T(8,128)(2,1)S(1)} collective-permute-done((bf16[8,128,128]{2,1,0:T(8,128)(2,1)S(1)}, bf16[8,128,128]{2,1,0:T(8,128)(2,1)S(1)}, u32[]{:S(2)}, u32[]{:S(2)}) %collective-permute-start.28) | collective-permute-done | bytes 262176 | tf_op jit(solution)/shard_map/ppermute | solution.py:276
  67.2 0.5 collective-permute-start.14
  67.7 0.7 shard_map.85
  68.5 0.8 collective-permute-start.31
  69.3 1.4 %collective-permute-start.32 = (bf16[2,128,128]{2,1,0:T(8,128)(2,1)S(1)}, bf16[2,128,128]{2,1,0:T(8,128)(2,1)S(1)}, u32[]{:S(2)}, u32[]{:S(2)}) collective-permute-start(bf16[2,128,128]{2,1,0:T(8,128)(2,1)S(1)} %get-tuple-element.59), channel_id=1, source_target_pairs={{0,2},{1,3},{2,0},{3,1},{4,6},{5,7},{6,4},{7,5},{8,10},{9,11},{10,... | collective-permute-start | bytes 196616 | tf_op jit(solution)/shard_map/ppermute | solution.py:272
  70.7 1.3 %collective-permute-start.33 = (bf16[2,128,128]{2,1,0:T(8,128)(2,1)S(1)}, bf16[2,128,128]{2,1,0:T(8,128)(2,1)S(1)}, u32[]{:S(2)}, u32[]{:S(2)}) collective-permute-start(bf16[2,128,128]{2,1,0:T(8,128)(2,1)S(1)} %get-tuple-element.60), channel_id=1, source_target_pairs={{0,3},{1,2},{2,1},{3,0},{4,7},{5,6},{6,5},{7,4},{8,11},{9,10},{10,... | collective-permute-start | bytes 196616 | tf_op jit(solution)/shard_map/ppermute | solution.py:272
  72.0 2.6 %shard_map.79 = (f32[256,512]{1,0:T(8,128)S(1)}, bf16[256,4096]{1,0:T(8,128)(2,1)}) custom-call(bf16[256,4096]{1,0:T(8,128)(2,1)S(1)} %get-tuple-element.32.tokens.mine, bf16[256,512]{1,0:T(8,128)(2,1)S(1)} %get-tuple-element.33.cot.cot_mine, bf16[8,128,128]{2,1,0:T(8,128)(2,1)S(1)} %get-tuple-element.38.refs_0_, ...), custom_call_target="tpu_custom_call" | custom-call | flops 1073741824 | bytes 6291456 | tf_op jit(solution)/shard_map/pallas_call | solution.py:282
  74.7 0.5 collective-permute-start.35
  75.3 0.6 collective-permute-done.33.refs_3_
  75.9 3.3 %shard_map.80 = (bf16[256,512]{1,0:T(8,128)(2,1)}, bf16[256,4096]{1,0:T(8,128)(2,1)}) custom-call(bf16[256,4096]{1,0:T(8,128)(2,1)S(1)} %get-tuple-element.32.tokens.mine, bf16[256,512]{1,0:T(8,128)(2,1)S(1)} %get-tuple-element.33.cot.cot_mine, bf16[8,128,128]{2,1,0:T(8,128)(2,1)S(1)} %collective-permute-done.6.refs_0_, ...), custom_call_target="tpu_custom_call", output_to_operand_aliasing={{1}: (11, {})} | custom-call | flops 1073741824 | bytes 6291456 | tf_op jit(solution)/shard_map/pallas_call | solution.py:282
  79.2 1.5 %shard_map.86 = bf16[16,128,128]{2,1,0:T(8,128)(2,1)} custom-call(s32[16]{0:T(128)S(1)} %copy-done, bf16[2,128,128]{2,1,0:T(8,128)(2,1)S(1)} %get-tuple-element.57.refs_0_, bf16[2,128,128]{2,1,0:T(8,128)(2,1)S(1)} %collective-permute-done.31.refs_1_, bf16[2,128,128]{2,1,0:T(8,128)(2,1)S(1)} %collective-permute-done.32.refs_2_, ...), custom_call_target="tpu_custom_call" | custom-call | flops 524288 | bytes 1048576 | tf_op jit(solution)/shard_map/pallas_call | solution.py:282
  (41 shorter events, 0.4 us)
Async XLA Ops:
  0.6 15.8 %collective-permute-start.20 = (bf16[256,4096]{1,0:T(8,128)(2,1)}, bf16[256,4096]{1,0:T(8,128)(2,1)S(1)}, u32[]{:S(2)}, u32[]{:S(2)}) collective-permute-start(bf16[256,4096]{1,0:T(8,128)(2,1)} %refs_0_.1), channel_id=1, source_target_pairs={{0,16},{16,0},{1,17},{17,1},{2,18},{18,2},{3,19},{19,3},{4,20},{20... | collective-permute-start | bytes 6291464 | tf_op jit(solution)/shard_map/ppermute | solution.py:279
  1.2 15.2 %collective-permute-start.21 = (bf16[256,512]{1,0:T(8,128)(2,1)}, bf16[256,512]{1,0:T(8,128)(2,1)S(1)}, u32[]{:S(2)}, u32[]{:S(2)}) collective-permute-start(bf16[256,512]{1,0:T(8,128)(2,1)} %refs_1_.1), channel_id=1, source_target_pairs={{0,16},{16,0},{1,17},{17,1},{2,18},{18,2},{3,19},{19,3},{4,20},{20... | collective-permute-start | bytes 786440 | tf_op jit(solution)/shard_map/ppermute | solution.py:279
  3.1 5.3 %collective-permute-start = (bf16[2,128,128]{2,1,0:T(8,128)(2,1)S(1)}, bf16[2,128,128]{2,1,0:T(8,128)(2,1)S(1)}, u32[]{:S(2)}, u32[]{:S(2)}) collective-permute-start(bf16[2,128,128]{2,1,0:T(8,128)(2,1)S(1)} %get-tuple-element.35), channel_id=1, source_target_pairs={{0,1},{1,0},{2,3},{3,2},{4,5},{5,4},{6,7},{7,6},{8,9},{9,8},{10,11... | collective-permute-start | bytes 196616 | tf_op jit(solution)/shard_map/ppermute | solution.py:272
  6.0 4.3 %collective-permute-start.1 = (bf16[2,128,128]{2,1,0:T(8,128)(2,1)S(1)}, bf16[2,128,128]{2,1,0:T(8,128)(2,1)S(1)}, u32[]{:S(2)}, u32[]{:S(2)}) collective-permute-start(bf16[2,128,128]{2,1,0:T(8,128)(2,1)S(1)} %get-tuple-element.36), channel_id=1, source_target_pairs={{0,2},{1,3},{2,0},{3,1},{4,6},{5,7},{6,4},{7,5},{8,10},{9,11},{10,... | collective-permute-start | bytes 196616 | tf_op jit(solution)/shard_map/ppermute | solution.py:272
  7.5 5.2 %collective-permute-start.2 = (bf16[2,128,128]{2,1,0:T(8,128)(2,1)S(1)}, bf16[2,128,128]{2,1,0:T(8,128)(2,1)S(1)}, u32[]{:S(2)}, u32[]{:S(2)}) collective-permute-start(bf16[2,128,128]{2,1,0:T(8,128)(2,1)S(1)} %get-tuple-element.37), channel_id=1, source_target_pairs={{0,3},{1,2},{2,1},{3,0},{4,7},{5,6},{6,5},{7,4},{8,11},{9,10},{10,... | collective-permute-start | bytes 196616 | tf_op jit(solution)/shard_map/ppermute | solution.py:272
  12.7 10.8 %collective-permute-start.4 = (bf16[8,128,128]{2,1,0:T(8,128)(2,1)S(1)}, bf16[8,128,128]{2,1,0:T(8,128)(2,1)S(1)}, u32[]{:S(2)}, u32[]{:S(2)}) collective-permute-start(bf16[8,128,128]{2,1,0:T(8,128)(2,1)S(1)} %shard_map.77.refs_0_), channel_id=1, source_target_pairs={{0,12},{1,13},{2,14},{3,15},{4,8},{5,9},{6,10},{7,11},{8,4},{9,5},... | collective-permute-start | bytes 786440 | tf_op jit(solution)/shard_map/ppermute | solution.py:276
  16.4 16.7 %copy-start = (s32[16]{0:T(128)S(1)}, s32[16]{0:T(128)}, u32[]{:S(2)}) copy-start(s32[16]{0:T(128)} %counts.7) | copy-start | bytes 196
  18.7 8.6 %collective-permute-start.23 = (bf16[8,128,128]{2,1,0:T(8,128)(2,1)S(1)}, bf16[8,128,128]{2,1,0:T(8,128)(2,1)S(1)}, u32[]{:S(2)}, u32[]{:S(2)}) collective-permute-start(bf16[8,128,128]{2,1,0:T(8,128)(2,1)S(1)} %get-tuple-element.47), channel_id=1, source_target_pairs={{0,1},{1,0},{2,3},{3,2},{4,5},{5,4},{6,7},{7,6},{8,9},{9,8},{10,11... | collective-permute-start | bytes 786440 | tf_op jit(solution)/shard_map/ppermute | solution.py:272
  19.3 8.6 %collective-permute-start.24 = (bf16[8,128,128]{2,1,0:T(8,128)(2,1)S(1)}, bf16[8,128,128]{2,1,0:T(8,128)(2,1)S(1)}, u32[]{:S(2)}, u32[]{:S(2)}) collective-permute-start(bf16[8,128,128]{2,1,0:T(8,128)(2,1)S(1)} %get-tuple-element.49), channel_id=1, source_target_pairs={{0,2},{1,3},{2,0},{3,1},{4,6},{5,7},{6,4},{7,5},{8,10},{9,11},{10,... | collective-permute-start | bytes 786440 | tf_op jit(solution)/shard_map/ppermute | solution.py:272
  19.8 9.7 %collective-permute-start.3 = (bf16[8,128,128]{2,1,0:T(8,128)(2,1)S(1)}, bf16[8,128,128]{2,1,0:T(8,128)(2,1)S(1)}, u32[]{:S(2)}, u32[]{:S(2)}) collective-permute-start(bf16[8,128,128]{2,1,0:T(8,128)(2,1)S(1)} %shard_map.77.refs_0_), channel_id=1, source_target_pairs={{0,4},{1,5},{2,6},{3,7},{4,0},{5,1},{6,2},{7,3},{8,12},{9,13},{10,... | collective-permute-start | bytes 786440 | tf_op jit(solution)/shard_map/ppermute | solution.py:276
  23.5 9.6 %collective-permute-start.5 = (bf16[8,128,128]{2,1,0:T(8,128)(2,1)S(1)}, bf16[8,128,128]{2,1,0:T(8,128)(2,1)S(1)}, u32[]{:S(2)}, u32[]{:S(2)}) collective-permute-start(bf16[8,128,128]{2,1,0:T(8,128)(2,1)S(1)} %collective-permute-done.4.refs_3_), channel_id=1, source_target_pairs={{0,4},{1,5},{2,6},{3,7},{4,0},{5,1},{6,2},{7,3},{8,12},{9,13},{10,... | collective-permute-start | bytes 786440 | tf_op jit(solution)/shard_map/ppermute | solution.py:276
  26.6 9.2 %collective-permute-start.22 = (bf16[8,128,128]{2,1,0:T(8,128)(2,1)S(1)}, bf16[8,128,128]{2,1,0:T(8,128)(2,1)S(1)}, u32[]{:S(2)}, u32[]{:S(2)}) collective-permute-start(bf16[8,128,128]{2,1,0:T(8,128)(2,1)S(1)} %get-tuple-element.45), channel_id=1, source_target_pairs={{0,1},{1,0},{2,3},{3,2},{4,5},{5,4},{6,7},{7,6},{8,9},{9,8},{10,11... | collective-permute-start | bytes 786440 | tf_op jit(solution)/shard_map/ppermute | solution.py:272
  27.3 9.5 %collective-permute-start.27 = (bf16[8,128,128]{2,1,0:T(8,128)(2,1)S(1)}, bf16[8,128,128]{2,1,0:T(8,128)(2,1)S(1)}, u32[]{:S(2)}, u32[]{:S(2)}) collective-permute-start(bf16[8,128,128]{2,1,0:T(8,128)(2,1)S(1)} %get-tuple-element.52), channel_id=1, source_target_pairs={{0,2},{1,3},{2,0},{3,1},{4,6},{5,7},{6,4},{7,5},{8,10},{9,11},{10,... | collective-permute-start | bytes 786440 | tf_op jit(solution)/shard_map/ppermute | solution.py:272
  28.0 14.0 %collective-permute-start.25 = (bf16[8,128,128]{2,1,0:T(8,128)(2,1)S(1)}, bf16[8,128,128]{2,1,0:T(8,128)(2,1)S(1)}, u32[]{:S(2)}, u32[]{:S(2)}) collective-permute-start(bf16[8,128,128]{2,1,0:T(8,128)(2,1)S(1)} %get-tuple-element.50), channel_id=1, source_target_pairs={{0,2},{1,3},{2,0},{3,1},{4,6},{5,7},{6,4},{7,5},{8,10},{9,11},{10,... | collective-permute-start | bytes 786440 | tf_op jit(solution)/shard_map/ppermute | solution.py:272
  29.5 13.9 %collective-permute-start.26 = (bf16[8,128,128]{2,1,0:T(8,128)(2,1)S(1)}, bf16[8,128,128]{2,1,0:T(8,128)(2,1)S(1)}, u32[]{:S(2)}, u32[]{:S(2)}) collective-permute-start(bf16[8,128,128]{2,1,0:T(8,128)(2,1)S(1)} %get-tuple-element.51), channel_id=1, source_target_pairs={{0,1},{1,0},{2,3},{3,2},{4,5},{5,4},{6,7},{7,6},{8,9},{9,8},{10,11... | collective-permute-start | bytes 786440 | tf_op jit(solution)/shard_map/ppermute | solution.py:272
  34.6 13.0 %collective-permute-start.6 = (bf16[8,128,128]{2,1,0:T(8,128)(2,1)S(1)}, bf16[8,128,128]{2,1,0:T(8,128)(2,1)S(1)}, u32[]{:S(2)}, u32[]{:S(2)}) collective-permute-start(bf16[8,128,128]{2,1,0:T(8,128)(2,1)S(1)} %get-tuple-element.38.refs_0_), channel_id=1, source_target_pairs={{0,2},{1,3},{2,0},{3,1},{4,6},{5,7},{6,4},{7,5},{8,10},{9,11},{10,... | collective-permute-start | bytes 786440 | tf_op jit(solution)/shard_map/ppermute | solution.py:272
  35.8 15.2 %collective-permute-start.7 = (bf16[8,128,128]{2,1,0:T(8,128)(2,1)S(1)}, bf16[8,128,128]{2,1,0:T(8,128)(2,1)S(1)}, u32[]{:S(2)}, u32[]{:S(2)}) collective-permute-start(bf16[8,128,128]{2,1,0:T(8,128)(2,1)S(1)} %get-tuple-element.39.refs_1_), channel_id=1, source_target_pairs={{0,2},{1,3},{2,0},{3,1},{4,6},{5,7},{6,4},{7,5},{8,10},{9,11},{10,... | collective-permute-start | bytes 786440 | tf_op jit(solution)/shard_map/ppermute | solution.py:272
  36.7 14.2 %collective-permute-start.8 = (bf16[8,128,128]{2,1,0:T(8,128)(2,1)S(1)}, bf16[8,128,128]{2,1,0:T(8,128)(2,1)S(1)}, u32[]{:S(2)}, u32[]{:S(2)}) collective-permute-start(bf16[8,128,128]{2,1,0:T(8,128)(2,1)S(1)} %get-tuple-element.38.refs_0_), channel_id=1, source_target_pairs={{0,1},{1,0},{2,3},{3,2},{4,5},{5,4},{6,7},{7,6},{8,9},{9,8},{10,11... | collective-permute-start | bytes 786440 | tf_op jit(solution)/shard_map/ppermute | solution.py:272
  42.1 9.5 %collective-permute-start.15 = (bf16[8,128,128]{2,1,0:T(8,128)(2,1)S(1)}, bf16[8,128,128]{2,1,0:T(8,128)(2,1)S(1)}, u32[]{:S(2)}, u32[]{:S(2)}) collective-permute-start(bf16[8,128,128]{2,1,0:T(8,128)(2,1)S(1)} %get-tuple-element.39.refs_1_), channel_id=1, source_target_pairs={{0,1},{1,0},{2,3},{3,2},{4,5},{5,4},{6,7},{7,6},{8,9},{9,8},{10,11... | collective-permute-start | bytes 786440 | tf_op jit(solution)/shard_map/ppermute | solution.py:272
  43.4 9.5 %collective-permute-start.16 = (bf16[8,128,128]{2,1,0:T(8,128)(2,1)S(1)}, bf16[8,128,128]{2,1,0:T(8,128)(2,1)S(1)}, u32[]{:S(2)}, u32[]{:S(2)}) collective-permute-start(bf16[8,128,128]{2,1,0:T(8,128)(2,1)S(1)} %get-tuple-element.38.refs_0_), channel_id=1, source_target_pairs={{0,16},{16,0},{1,17},{17,1},{2,18},{18,2},{3,19},{19,3},{4,20},{20... | collective-permute-start | bytes 786440 | tf_op jit(solution)/shard_map/ppermute | solution.py:279
  47.7 6.4 %collective-permute-start.29 = (bf16[8,128,128]{2,1,0:T(8,128)(2,1)S(1)}, bf16[8,128,128]{2,1,0:T(8,128)(2,1)S(1)}, u32[]{:S(2)}, u32[]{:S(2)}) collective-permute-start(bf16[8,128,128]{2,1,0:T(8,128)(2,1)S(1)} %get-tuple-element.56), channel_id=1, source_target_pairs={{0,4},{1,5},{2,6},{3,7},{4,0},{5,1},{6,2},{7,3},{8,12},{9,13},{10,... | collective-permute-start | bytes 786440 | tf_op jit(solution)/shard_map/ppermute | solution.py:276
  50.9 3.2 %collective-permute-start.17 = (bf16[8,128,128]{2,1,0:T(8,128)(2,1)S(1)}, bf16[8,128,128]{2,1,0:T(8,128)(2,1)S(1)}, u32[]{:S(2)}, u32[]{:S(2)}) collective-permute-start(bf16[8,128,128]{2,1,0:T(8,128)(2,1)S(1)} %get-tuple-element.39.refs_1_), channel_id=1, source_target_pairs={{0,16},{16,0},{1,17},{17,1},{2,18},{18,2},{3,19},{19,3},{4,20},{20... | collective-permute-start | bytes 786440 | tf_op jit(solution)/shard_map/ppermute | solution.py:279
  50.9 8.7 %collective-permute-start.9 = (bf16[8,128,128]{2,1,0:T(8,128)(2,1)S(1)}, bf16[8,128,128]{2,1,0:T(8,128)(2,1)S(1)}, u32[]{:S(2)}, u32[]{:S(2)}) collective-permute-start(bf16[8,128,128]{2,1,0:T(8,128)(2,1)S(1)} %collective-permute-done.8.refs_2_), channel_id=1, source_target_pairs={{0,2},{1,3},{2,0},{3,1},{4,6},{5,7},{6,4},{7,5},{8,10},{9,11},{10,... | collective-permute-start | bytes 786440 | tf_op jit(solution)/shard_map/ppermute | solution.py:272
  51.6 8.4 %collective-permute-start.10 = (bf16[8,128,128]{2,1,0:T(8,128)(2,1)S(1)}, bf16[8,128,128]{2,1,0:T(8,128)(2,1)S(1)}, u32[]{:S(2)}, u32[]{:S(2)}) collective-permute-start(bf16[8,128,128]{2,1,0:T(8,128)(2,1)S(1)} %collective-permute-done.7.refs_1_), channel_id=1, source_target_pairs={{0,1},{1,0},{2,3},{3,2},{4,5},{5,4},{6,7},{7,6},{8,9},{9,8},{10,11... | collective-permute-start | bytes 786440 | tf_op jit(solution)/shard_map/ppermute | solution.py:272
  52.9 7.3 %collective-permute-start.11 = (bf16[8,128,128]{2,1,0:T(8,128)(2,1)S(1)}, bf16[8,128,128]{2,1,0:T(8,128)(2,1)S(1)}, u32[]{:S(2)}, u32[]{:S(2)}) collective-permute-start(bf16[8,128,128]{2,1,0:T(8,128)(2,1)S(1)} %collective-permute-done.6.refs_0_), channel_id=1, source_target_pairs={{0,16},{16,0},{1,17},{17,1},{2,18},{18,2},{3,19},{19,3},{4,20},{20... | collective-permute-start | bytes 786440 | tf_op jit(solution)/shard_map/ppermute | solution.py:279
  54.1 13.2 %collective-permute-start.28 = (bf16[8,128,128]{2,1,0:T(8,128)(2,1)S(1)}, bf16[8,128,128]{2,1,0:T(8,128)(2,1)S(1)}, u32[]{:S(2)}, u32[]{:S(2)}) collective-permute-start(bf16[8,128,128]{2,1,0:T(8,128)(2,1)S(1)} %get-tuple-element.54), channel_id=1, source_target_pairs={{0,4},{1,5},{2,6},{3,7},{4,0},{5,1},{6,2},{7,3},{8,12},{9,13},{10,... | collective-permute-start | bytes 786440 | tf_op jit(solution)/shard_map/ppermute | solution.py:276
  54.1 13.1 %collective-permute-start.30 = (bf16[8,128,128]{2,1,0:T(8,128)(2,1)S(1)}, bf16[8,128,128]{2,1,0:T(8,128)(2,1)S(1)}, u32[]{:S(2)}, u32[]{:S(2)}) collective-permute-start(bf16[8,128,128]{2,1,0:T(8,128)(2,1)S(1)} %shard_map.84), channel_id=1, source_target_pairs={{0,12},{1,13},{2,14},{3,15},{4,8},{5,9},{6,10},{7,11},{8,4},{9,5},... | collective-permute-start | bytes 786440 | tf_op jit(solution)/shard_map/ppermute | solution.py:276
  59.7 8.8 %collective-permute-start.12 = (bf16[8,128,128]{2,1,0:T(8,128)(2,1)S(1)}, bf16[8,128,128]{2,1,0:T(8,128)(2,1)S(1)}, u32[]{:S(2)}, u32[]{:S(2)}) collective-permute-start(bf16[8,128,128]{2,1,0:T(8,128)(2,1)S(1)} %collective-permute-done.7.refs_1_), channel_id=1, source_target_pairs={{0,16},{16,0},{1,17},{17,1},{2,18},{18,2},{3,19},{19,3},{4,20},{20... | collective-permute-start | bytes 786440 | tf_op jit(solution)/shard_map/ppermute | solution.py:279
  60.0 9.3 %collective-permute-start.18 = (bf16[8,128,128]{2,1,0:T(8,128)(2,1)S(1)}, bf16[8,128,128]{2,1,0:T(8,128)(2,1)S(1)}, u32[]{:S(2)}, u32[]{:S(2)}) collective-permute-start(bf16[8,128,128]{2,1,0:T(8,128)(2,1)S(1)} %collective-permute-done.8.refs_2_), channel_id=1, source_target_pairs={{0,16},{16,0},{1,17},{17,1},{2,18},{18,2},{3,19},{19,3},{4,20},{20... | collective-permute-start | bytes 786440 | tf_op jit(solution)/shard_map/ppermute | solution.py:279
  60.2 10.5 %collective-permute-start.19 = (bf16[8,128,128]{2,1,0:T(8,128)(2,1)S(1)}, bf16[8,128,128]{2,1,0:T(8,128)(2,1)S(1)}, u32[]{:S(2)}, u32[]{:S(2)}) collective-permute-start(bf16[8,128,128]{2,1,0:T(8,128)(2,1)S(1)} %collective-permute-done.15.refs_3_), channel_id=1, source_target_pairs={{0,16},{16,0},{1,17},{17,1},{2,18},{18,2},{3,19},{19,3},{4,20},{20... | collective-permute-start | bytes 786440 | tf_op jit(solution)/shard_map/ppermute | solution.py:279
  67.2 7.4 %collective-permute-start.13 = (bf16[8,128,128]{2,1,0:T(8,128)(2,1)S(1)}, bf16[8,128,128]{2,1,0:T(8,128)(2,1)S(1)}, u32[]{:S(2)}, u32[]{:S(2)}) collective-permute-start(bf16[8,128,128]{2,1,0:T(8,128)(2,1)S(1)} %collective-permute-done.9.refs_2_), channel_id=1, source_target_pairs={{0,16},{16,0},{1,17},{17,1},{2,18},{18,2},{3,19},{19,3},{4,20},{20... | collective-permute-start | bytes 786440 | tf_op jit(solution)/shard_map/ppermute | solution.py:279
  67.2 8.7 %collective-permute-start.14 = (bf16[8,128,128]{2,1,0:T(8,128)(2,1)S(1)}, bf16[8,128,128]{2,1,0:T(8,128)(2,1)S(1)}, u32[]{:S(2)}, u32[]{:S(2)}) collective-permute-start(bf16[8,128,128]{2,1,0:T(8,128)(2,1)S(1)} %collective-permute-done.10.refs_3_), channel_id=1, source_target_pairs={{0,16},{16,0},{1,17},{17,1},{2,18},{18,2},{3,19},{19,3},{4,20},{20... | collective-permute-start | bytes 786440 | tf_op jit(solution)/shard_map/ppermute | solution.py:279
  68.5 6.2 %collective-permute-start.31 = (bf16[2,128,128]{2,1,0:T(8,128)(2,1)S(1)}, bf16[2,128,128]{2,1,0:T(8,128)(2,1)S(1)}, u32[]{:S(2)}, u32[]{:S(2)}) collective-permute-start(bf16[2,128,128]{2,1,0:T(8,128)(2,1)S(1)} %get-tuple-element.58), channel_id=1, source_target_pairs={{0,1},{1,0},{2,3},{3,2},{4,5},{5,4},{6,7},{7,6},{8,9},{9,8},{10,11... | collective-permute-start | bytes 196616 | tf_op jit(solution)/shard_map/ppermute | solution.py:272
  69.3 5.9 %collective-permute-start.32 = (bf16[2,128,128]{2,1,0:T(8,128)(2,1)S(1)}, bf16[2,128,128]{2,1,0:T(8,128)(2,1)S(1)}, u32[]{:S(2)}, u32[]{:S(2)}) collective-permute-start(bf16[2,128,128]{2,1,0:T(8,128)(2,1)S(1)} %get-tuple-element.59), channel_id=1, source_target_pairs={{0,2},{1,3},{2,0},{3,1},{4,6},{5,7},{6,4},{7,5},{8,10},{9,11},{10,... | collective-permute-start | bytes 196616 | tf_op jit(solution)/shard_map/ppermute | solution.py:272
  70.7 5.2 %collective-permute-start.33 = (bf16[2,128,128]{2,1,0:T(8,128)(2,1)S(1)}, bf16[2,128,128]{2,1,0:T(8,128)(2,1)S(1)}, u32[]{:S(2)}, u32[]{:S(2)}) collective-permute-start(bf16[2,128,128]{2,1,0:T(8,128)(2,1)S(1)} %get-tuple-element.60), channel_id=1, source_target_pairs={{0,3},{1,2},{2,1},{3,0},{4,7},{5,6},{6,5},{7,4},{8,11},{9,10},{10,... | collective-permute-start | bytes 196616 | tf_op jit(solution)/shard_map/ppermute | solution.py:272
  74.6 4.5 %collective-permute-start.34 = (bf16[2,128,128]{2,1,0:T(8,128)(2,1)S(1)}, bf16[2,128,128]{2,1,0:T(8,128)(2,1)S(1)}, u32[]{:S(2)}, u32[]{:S(2)}) collective-permute-start(bf16[2,128,128]{2,1,0:T(8,128)(2,1)S(1)} %get-tuple-element.57.refs_0_), channel_id=1, source_target_pairs={{0,16},{16,0},{1,17},{17,1},{2,18},{18,2},{3,19},{19,3},{4,20},{20... | collective-permute-start | bytes 196616 | tf_op jit(solution)/shard_map/ppermute | solution.py:279
  74.7 4.5 %collective-permute-start.35 = (bf16[2,128,128]{2,1,0:T(8,128)(2,1)S(1)}, bf16[2,128,128]{2,1,0:T(8,128)(2,1)S(1)}, u32[]{:S(2)}, u32[]{:S(2)}) collective-permute-start(bf16[2,128,128]{2,1,0:T(8,128)(2,1)S(1)} %collective-permute-done.31.refs_1_), channel_id=1, source_target_pairs={{0,16},{16,0},{1,17},{17,1},{2,18},{18,2},{3,19},{19,3},{4,20},{20... | collective-permute-start | bytes 196616 | tf_op jit(solution)/shard_map/ppermute | solution.py:279
  75.2 4.0 %collective-permute-start.36 = (bf16[2,128,128]{2,1,0:T(8,128)(2,1)S(1)}, bf16[2,128,128]{2,1,0:T(8,128)(2,1)S(1)}, u32[]{:S(2)}, u32[]{:S(2)}) collective-permute-start(bf16[2,128,128]{2,1,0:T(8,128)(2,1)S(1)} %collective-permute-done.32.refs_2_), channel_id=1, source_target_pairs={{0,16},{16,0},{1,17},{17,1},{2,18},{18,2},{3,19},{19,3},{4,20},{20... | collective-permute-start | bytes 196616 | tf_op jit(solution)/shard_map/ppermute | solution.py:279
  75.9 3.3 %collective-permute-start.37 = (bf16[2,128,128]{2,1,0:T(8,128)(2,1)S(1)}, bf16[2,128,128]{2,1,0:T(8,128)(2,1)S(1)}, u32[]{:S(2)}, u32[]{:S(2)}) collective-permute-start(bf16[2,128,128]{2,1,0:T(8,128)(2,1)S(1)} %collective-permute-done.33.refs_3_), channel_id=1, source_target_pairs={{0,16},{16,0},{1,17},{17,1},{2,18},{18,2},{3,19},{19,3},{4,20},{20... | collective-permute-start | bytes 196616 | tf_op jit(solution)/shard_map/ppermute | solution.py:279

commit v5 on v4

--- a/solution.py
+++ b/solution.py
@@ -19,10 +19,6 @@
     return (place // 2) * 4 + core * 2 + place % 2
 
 
-def prefix(counts, stop):
-    return lax.fori_loop(0, stop, lambda i, total: total + counts[i], jnp.int32(0))
-
-
 def lead(cls, start):
     return (cls - start) & (PERIOD - 1)
 
@@ -33,7 +29,8 @@
 
 
 def spread_kernel(slots, reach, counts_in, scales_in, codes_in, *refs):
-    (tokens_in, cot_in), (tokens, cot), outs = refs[:2], refs[2:4], refs[4 : 4 + INNER]
+    tokens_in, cot_in, tokens, cot = refs[:4]
+    outs = refs[4 : 4 + INNER]
     counts, scales, codes, done, wide_done = refs[4 + INNER :]
     wide_loads = [
         pltpu.make_async_copy(source, target, wide_done.at[n])
@@ -49,7 +46,7 @@
         load.start()
     core, _, place, me = here()
     loads[0].wait()
-    start = prefix(counts, me)
+    start = lax.fori_loop(0, me, lambda i, total: total + counts[i], jnp.int32(0))
     loads[1].wait()
     loads[2].wait()
     for step, out in enumerate(outs):
@@ -61,36 +58,40 @@
         load.wait()
 
 
+def table_kernel(owners, counts, table):
+    def note(i, total):
+        table[i] = total
+        table[owners + i] = counts[i]
+        return total + counts[i]
+
+    lax.fori_loop(0, owners, note, jnp.int32(0), unroll=owners <= 16)
+
+
 def stack_kernel(reach, *refs):
     out = refs[-1]
     for m, ref in enumerate(refs[:-1]):
         out[pl.ds(m * reach, reach)] = ref[...]
 
 
-def class_kernel(planes, reach, counts, *refs):
-    ins, outs, starts = refs[:planes], refs[planes:-1], refs[-1]
+def class_kernel(planes, reach, table, *refs):
+    ins, outs, gathered = refs[:planes], refs[planes:-1], refs[-1]
     core, plane, place, _ = here()
     cls = class_of(core, place)
+    owners = planes * INNER
+    for shift, ref in enumerate(ins):
+        for m in range(INNER):
+            owner = (plane ^ shift) * INNER + (place ^ m)
+            start, count = table[owner], table[owners + owner]
+            first = lead(cls, start)
+            for t in range(reach):
+
+                @pl.when(first + PERIOD * t < count)
+                def _(start=start, first=first, t=t, m=m, ref=ref):
+                    gathered[(start + first) // PERIOD + t] = ref[m * reach + t]
+
     per_out = outs[0].shape[0]
-
-    def note(i, total):
-        starts[i] = total
-        return total + counts[i]
-
-    lax.fori_loop(0, planes * INNER, note, jnp.int32(0))
-    for shift, ref in enumerate(ins):
-        source = plane ^ shift
-        for m in range(INNER):
-            owner = source * INNER + (place ^ m)
-            first = lead(cls, starts[owner])
-            for t in range(reach):
-                j = (starts[owner] + first) // PERIOD + t
-                held = first + PERIOD * t < counts[owner]
-                for n, out in enumerate(outs):
-
-                    @pl.when(held & (j // per_out == n))
-                    def _(j=j, t=t, m=m, n=n, ref=ref, out=out):
-                        out[j - n * per_out] = ref[m * reach + t]
+    for n, out in enumerate(outs):
+        out[...] = gathered[n * per_out : (n + 1) * per_out]
 
 
 def grad_kernel(scale, tile, chunks, mine, theirs, cot_mine, cot_theirs, own, *refs):
@@ -135,12 +136,12 @@
         out[...] = value.astype(BF16)
 
 
-def window(counts, cls, plane, blocks, span):
-    start = prefix(counts, plane * INNER)
+def window(table, cls, plane, blocks, span):
+    start = table[plane * INNER]
     return jnp.minimum((start + lead(cls, start)) // PERIOD, blocks - span)
 
 
-def plane_sum_kernel(span, counts, own, *refs):
+def plane_sum_kernel(span, table, own, *refs):
     ins, outs, total = refs[:4], refs[4:-1], refs[-1]
     core, plane, place, _ = here()
     cls = class_of(core, place)
@@ -153,39 +154,45 @@
         total[j] = acc.astype(BF16)
     for shift, out in enumerate(outs):
         target = plane ^ shift
-        out[...] = total[pl.ds(window(counts, cls, target, blocks, span), span)]
-
-
-def owner_kernel(blocks, reach, span, counts, *refs):
-    ins, outs, total = refs[: -INNER - 1], refs[-INNER - 1 : -1], refs[-1]
+        out[...] = total[pl.ds(window(table, cls, target, blocks, span), span)]
+
+
+def owner_kernel(blocks, reach, span, table, *refs):
+    ins, outs = refs[:-INNER], refs[-INNER:]
     core, plane, place, _ = here()
     cls = class_of(core, place)
-    acc = ins[0][...].astype(jnp.float32)
-    for ref in ins[1:]:
-        acc += ref[...].astype(jnp.float32)
-    total[...] = acc.astype(BF16)
-    base = window(counts, cls, plane, blocks, span)
+    base = window(table, cls, plane, blocks, span)
     for m, out in enumerate(outs):
-        start = prefix(counts, plane * INNER + (place ^ m))
+        start = table[plane * INNER + (place ^ m)]
         j = (start + lead(cls, start)) // PERIOD - base
         for t in range(reach):
-            out[t] = total[jnp.clip(j + t, 0, span - 1)]
-
-
-def slots_kernel(slots, reach, counts, *refs):
-    ins, out = refs[:-1], refs[-1]
+            row = jnp.clip(j + t, 0, span - 1)
+            acc = ins[0][row].astype(jnp.float32)
+            for ref in ins[1:]:
+                acc += ref[row].astype(jnp.float32)
+            out[t] = acc.astype(BF16)
+
+
+def slots_kernel(slots, reach, owners, table, *refs):
+    ins, (out, empty, done) = refs[:-3], refs[-3:]
     core, _, place, me = here()
-    start, count = prefix(counts, me), counts[me]
+    start, count = table[me], table[owners + me]
+    empty[...] = jnp.zeros_like(empty)
+    stores = []
     for n, ref in enumerate(ins):
         side = core ^ (n // INNER)
         first = lead(class_of(side, place ^ (n % INNER)), start)
         for t in range(reach):
             slot = first + PERIOD * t
-
-            @pl.when(slot < slots)
-            def _(slot=slot, ref=ref, t=t):
-                value = ref[t]
-                out[slot] = jnp.where(slot < count, value, jnp.zeros_like(value))
+            here_slot = jnp.minimum(slot, slots - 1)
+            flag = done.at[n * reach + t]
+            real = pltpu.make_async_copy(ref.at[t], out.at[here_slot], flag)
+            blank = pltpu.make_async_copy(empty, out.at[here_slot], flag)
+            pl.when((slot < slots) & (slot < count))(real.start)
+            pl.when((slot < slots) & (slot >= count))(blank.start)
+            stores.append((slot < slots, real))
+    for wanted, store in stores:
+        pl.when(wanted)(store.wait)
 
 
 def product_kernel(tile, part, tokens, cot, *refs):
@@ -347,6 +354,16 @@
         beside(y_high, 2),
     ]
 
+    table = call(
+        functools.partial(table_kernel, owners),
+        counts,
+        out_shape=jax.ShapeDtypeStruct((2 * owners,), jnp.int32),
+        in_specs=[scalars()],
+        out_specs=scalars(),
+        cost_estimate=cost(1000, 1000),
+        compiler_params=room(1),
+    )
+
     stacked = call(
         functools.partial(stack_kernel, reach),
         *near,
@@ -362,19 +379,20 @@
 
     own_classes = call(
         functools.partial(class_kernel, planes, reach),
-        counts,
+        table,
         *held,
         out_shape=[many(blocks // 2)] * 2,
         in_specs=[scalars()] + [whole()] * planes,
         out_specs=[whole()] * 2,
-        scratch_shapes=[pltpu.SMEM((owners,), jnp.int32)],
+        scratch_shapes=[VMEM((blocks, tile, tile), BF16)],
         cost_estimate=cost(32 * block_bytes, 48 * block_bytes),
         compiler_params=room(8),
     )
 
     windows = call(
         functools.partial(plane_sum_kernel, span),
-        counts, *parts,
+        table,
+        *parts,
         out_shape=[many(span)] * planes,
         in_specs=[scalars()] + [whole()] * 5,
         out_specs=[whole()] * planes,
@@ -399,11 +417,11 @@
 
     sent = call(
         functools.partial(owner_kernel, blocks, reach, span),
-        counts, *sums,
+        table,
+        *sums,
         out_shape=[many(reach)] * INNER,
         in_specs=[scalars()] + [whole()] * len(sums),
         out_specs=[whole()] * INNER,
-        scratch_shapes=[VMEM((span, tile, tile), BF16)],
         cost_estimate=cost(32 * block_bytes, 48 * block_bytes),
         compiler_params=room(8),
     )
@@ -413,7 +431,7 @@
     from_x = [beside(low, 1), beside(high, 1)]
     from_y = [beside(low, 2), beside(high, 2)]
     from_far = [beside(from_x[0], 2), beside(from_y[1], 1)]
-    group = min(4, blocks // 2)
+    group = min(2, blocks // 2)
 
     def products(part, own, carried):
         held_by_both = own + [across(c) for c in own]
@@ -446,11 +464,16 @@
 
     all_mine = mine + [across(v) for v in mine]
     block_grad = call(
-        functools.partial(slots_kernel, slots, reach),
-        counts, *all_mine,
+        functools.partial(slots_kernel, slots, reach, owners),
+        table,
+        *all_mine,
         out_shape=many(slots),
         in_specs=[scalars()] + [whole()] * (2 * INNER),
-        out_specs=whole(),
+        out_specs=far(),
+        scratch_shapes=[
+            VMEM((tile, tile), BF16),
+            pltpu.SemaphoreType.DMA((2 * INNER * reach,)),
+        ],
         cost_estimate=cost(16 * block_bytes, 32 * block_bytes),
         compiler_params=room(8),
     )

time: 80.8 us -> 80.6 us (level)
    ppermute x6, waiting for transfers between devices: 13.9 us -> 12.7 us  [along(): return lax.ppermute(value, 'fsdp', pairs)]
    pallas_call x11 -> x12, Pallas kernels: 14.8 us -> 14.8 us  [call(): return pl.pallas_call(kernel, **how)(*operands)]
  transfers between devices with their start and end apart: 38 -> 38, of which waited for: 14 -> 15; matrix products, arithmetic and copies ran while one was open for 0% -> 0% of each run, Pallas kernels for 17% -> 17%
where the time goes in v5:
time: 80.6 us; the launch traced here: 80.5 us
  waiting for transfers between devices  35.4 us (44%)
  starting transfers between devices  29.4 us (36%)
  Pallas kernels  14.8 us (18%)
  between operations  0.81 us (1%)
    ppermute x18, waiting for transfers between devices, beside(): return lax.ppermute(value, 'fsdp', [(i, i ^ m) for i in range(owners)])  22.6 us
    ppermute x18, starting transfers between devices, beside(): return lax.ppermute(value, 'fsdp', [(i, i ^ m) for i in range(owners)])  19.1 us
    pallas_call x12, Pallas kernels, call(): return pl.pallas_call(kernel, **how)(*operands)  14.8 us
    ppermute x6, waiting for transfers between devices, along(): return lax.ppermute(value, 'fsdp', pairs)  12.7 us
    ppermute x6, starting transfers between devices, along(): return lax.ppermute(value, 'fsdp', pairs)  8.01 us
    ppermute x14, starting transfers between devices, across(): return lax.ppermute(value, 'dp', [(0, 1), (1, 0)])  2.32 us
  transfers between devices with their start and end apart: 38, of which 15 were waited for; matrix products, arithmetic and copies ran while one was open for 0% of the time, Pallas kernels for 17%

profile of v5, /device:TPU:0, one launch (start us, length us, event | category | flops | bytes accessed | tf_op | source)
XLA Modules:
  0.0 80.5 jit_solution(13916389305682812418)
XLA Ops:
  0.6 0.6 collective-permute-start.20
  1.3 1.8 %shard_map.76 = (bf16[256,4096]{1,0:T(8,128)(2,1)S(1)}, bf16[256,512]{1,0:T(8,128)(2,1)S(1)}, bf16[2,128,128]{2,1,0:T(8,128)(2,1)S(1)}, bf16[2,128,128]{2,1,0:T(...) custom-call(s32[16]{0:T(128)} %counts.1, f32[16]{0:T(128)} %scales_in.1, ...), custom_call_target="tpu_custom_call" | custom-call | flops 262144 | bytes 786432 | tf_op jit(solution)/shard_map/pallas_call | solution.py:289
  3.1 3.0 %collective-permute-start = (bf16[2,128,128]{2,1,0:T(8,128)(2,1)S(1)}, bf16[2,128,128]{2,1,0:T(8,128)(2,1)S(1)}, u32[]{:S(2)}, u32[]{:S(2)}) collective-permute-start(bf16[2,128,128]{2,1,0:T(8,128)(2,1)S(1)} %get-tuple-element.35), channel_id=1, source_target_pairs={{0,1},{1,0},{2,3},{3,2},{4,5},{5,4},{6,7},{7,6},{8,9},{9,8},{10,11... | collective-permute-start | bytes 196616 | tf_op jit(solution)/shard_map/ppermute | solution.py:279
  6.0 1.5 %collective-permute-start.1 = (bf16[2,128,128]{2,1,0:T(8,128)(2,1)S(1)}, bf16[2,128,128]{2,1,0:T(8,128)(2,1)S(1)}, u32[]{:S(2)}, u32[]{:S(2)}) collective-permute-start(bf16[2,128,128]{2,1,0:T(8,128)(2,1)S(1)} %get-tuple-element.36), channel_id=1, source_target_pairs={{0,2},{1,3},{2,0},{3,1},{4,6},{5,7},{6,4},{7,5},{8,10},{9,11},{10,... | collective-permute-start | bytes 196616 | tf_op jit(solution)/shard_map/ppermute | solution.py:279
  7.6 0.8 collective-permute-done.refs_1_
  8.4 1.9 %collective-permute-done.1.refs_2_ = bf16[2,128,128]{2,1,0:T(8,128)(2,1)S(1)} collective-permute-done((bf16[2,128,128]{2,1,0:T(8,128)(2,1)S(1)}, bf16[2,128,128]{2,1,0:T(8,128)(2,1)S(1)}, u32[]{:S(2)}, u32[]{:S(2)}) %collective-permute-start.1) | collective-permute-done | bytes 65568 | tf_op jit(solution)/shard_map/ppermute | solution.py:279
  10.3 2.4 %collective-permute-done.2.refs_3_ = bf16[2,128,128]{2,1,0:T(8,128)(2,1)S(1)} collective-permute-done((bf16[2,128,128]{2,1,0:T(8,128)(2,1)S(1)}, bf16[2,128,128]{2,1,0:T(8,128)(2,1)S(1)}, u32[]{:S(2)}, u32[]{:S(2)}) %collective-permute-start.2) | collective-permute-done | bytes 65568 | tf_op jit(solution)/shard_map/ppermute | solution.py:279
  12.7 3.7 %collective-permute-start.4 = (bf16[8,128,128]{2,1,0:T(8,128)(2,1)S(1)}, bf16[8,128,128]{2,1,0:T(8,128)(2,1)S(1)}, u32[]{:S(2)}, u32[]{:S(2)}) collective-permute-start(bf16[8,128,128]{2,1,0:T(8,128)(2,1)S(1)} %shard_map.78.refs_0_), channel_id=1, source_target_pairs={{0,12},{1,13},{2,14},{3,15},{4,8},{5,9},{6,10},{7,11},{8,4},{9,5},... | collective-permute-start | bytes 786440 | tf_op jit(solution)/shard_map/ppermute | solution.py:283
  16.4 2.2 %shard_map.82 = (bf16[16,128,128]{2,1,0:T(8,128)(2,1)S(1)}, bf16[8,128,128]{2,1,0:T(8,128)(2,1)S(1)}, bf16[8,128,128]{2,1,0:T(8,128)(2,1)S(1)}, bf16[8,128,128]{...) custom-call(bf16[256,4096]{1,0:T(8,128)(2,1)S(1)} %get-tuple-element, ...), custom_call_target="tpu_custom_call" | custom-call | flops 1073741824 | bytes 6291456 | tf_op jit(solution)/shard_map/pallas_call | solution.py:289
  18.7 0.6 collective-permute-start.23
  19.3 0.5 collective-permute-start.24
  19.8 3.7 %collective-permute-done.4.refs_3_ = bf16[8,128,128]{2,1,0:T(8,128)(2,1)S(1)} collective-permute-done((bf16[8,128,128]{2,1,0:T(8,128)(2,1)S(1)}, bf16[8,128,128]{2,1,0:T(8,128)(2,1)S(1)}, u32[]{:S(2)}, u32[]{:S(2)}) %collective-permute-start.4) | collective-permute-done | bytes 262176 | tf_op jit(solution)/shard_map/ppermute | solution.py:283
  23.5 3.0 %collective-permute-start.5 = (bf16[8,128,128]{2,1,0:T(8,128)(2,1)S(1)}, bf16[8,128,128]{2,1,0:T(8,128)(2,1)S(1)}, u32[]{:S(2)}, u32[]{:S(2)}) collective-permute-start(bf16[8,128,128]{2,1,0:T(8,128)(2,1)S(1)} %collective-permute-done.4.refs_3_), channel_id=1, source_target_pairs={{0,4},{1,5},{2,6},{3,7},{4,0},{5,1},{6,2},{7,3},{8,12},{9,13},{10,... | collective-permute-start | bytes 786440 | tf_op jit(solution)/shard_map/ppermute | solution.py:283
  26.6 0.7 collective-permute-start.22
  27.3 0.6 collective-permute-start.27
  28.0 1.5 %collective-permute-start.25 = (bf16[8,128,128]{2,1,0:T(8,128)(2,1)S(1)}, bf16[8,128,128]{2,1,0:T(8,128)(2,1)S(1)}, u32[]{:S(2)}, u32[]{:S(2)}) collective-permute-start(bf16[8,128,128]{2,1,0:T(8,128)(2,1)S(1)} %get-tuple-element.50), channel_id=1, source_target_pairs={{0,2},{1,3},{2,0},{3,1},{4,6},{5,7},{6,4},{7,5},{8,10},{9,11},{10,... | collective-permute-start | bytes 786440 | tf_op jit(solution)/shard_map/ppermute | solution.py:279
  29.5 1.3 %collective-permute-start.26 = (bf16[8,128,128]{2,1,0:T(8,128)(2,1)S(1)}, bf16[8,128,128]{2,1,0:T(8,128)(2,1)S(1)}, u32[]{:S(2)}, u32[]{:S(2)}) collective-permute-start(bf16[8,128,128]{2,1,0:T(8,128)(2,1)S(1)} %get-tuple-element.51), channel_id=1, source_target_pairs={{0,1},{1,0},{2,3},{3,2},{4,5},{5,4},{6,7},{7,6},{8,9},{9,8},{10,11... | collective-permute-start | bytes 786440 | tf_op jit(solution)/shard_map/ppermute | solution.py:279
  30.8 1.2 %shard_map.77.table = s32[32]{0:T(128)S(1)} custom-call(s32[16]{0:T(128)S(1)} %copy-done), custom_call_target="tpu_custom_call" | custom-call | flops 1000 | bytes 1000 | tf_op jit(solution)/shard_map/pallas_call | solution.py:289
  32.0 1.1 %collective-permute-done.5.refs_2_ = bf16[8,128,128]{2,1,0:T(8,128)(2,1)S(1)} collective-permute-done((bf16[8,128,128]{2,1,0:T(8,128)(2,1)S(1)}, bf16[8,128,128]{2,1,0:T(8,128)(2,1)S(1)}, u32[]{:S(2)}, u32[]{:S(2)}) %collective-permute-start.5) | collective-permute-done | bytes 262176 | tf_op jit(solution)/shard_map/ppermute | solution.py:283
  33.1 0.9 %shard_map.79 = (bf16[8,128,128]{2,1,0:T(8,128)(2,1)S(1)}, bf16[8,128,128]{2,1,0:T(8,128)(2,1)S(1)}) custom-call(s32[32]{0:T(128)S(1)} %shard_map.77.table, bf16[8,128,128]{2,1,0:T(8,128)(2,1)S(1)} %shard_map.78.refs_0_, bf16[8,128,128]{2,1,0:T(8,128)(2,1)S(1)} %collective-permute-done.3.refs_1_, bf16[8,128,128]{2,1,0:T(8,128)(2,1)S(1)} %collective-permute-done.5.refs_2_, ...), custom_call_target="tpu_custom_call" | custom-call | flops 1048576 | bytes 1572864 | tf_op jit(solution)/shard_map/pallas_call | solution.py:289
  34.0 0.6 collective-permute-start.6
  34.7 1.1 %collective-permute-done.22.refs_0_ = bf16[8,128,128]{2,1,0:T(8,128)(2,1)S(1)} collective-permute-done((bf16[8,128,128]{2,1,0:T(8,128)(2,1)S(1)}, bf16[8,128,128]{2,1,0:T(8,128)(2,1)S(1)}, u32[]{:S(2)}, u32[]{:S(2)}) %collective-permute-start.22) | collective-permute-done | bytes 262176 | tf_op jit(solution)/shard_map/ppermute | solution.py:279
  35.8 0.6 collective-permute-start.7
  36.4 1.3 %collective-permute-start.8 = (bf16[8,128,128]{2,1,0:T(8,128)(2,1)S(1)}, bf16[8,128,128]{2,1,0:T(8,128)(2,1)S(1)}, u32[]{:S(2)}, u32[]{:S(2)}) collective-permute-start(bf16[8,128,128]{2,1,0:T(8,128)(2,1)S(1)} %get-tuple-element.38.refs_0_), channel_id=1, source_target_pairs={{0,1},{1,0},{2,3},{3,2},{4,5},{5,4},{6,7},{7,6},{8,9},{9,8},{10,11... | collective-permute-start | bytes 786440 | tf_op jit(solution)/shard_map/ppermute | solution.py:279
  37.8 4.3 %collective-permute-done.25.refs_1_ = bf16[8,128,128]{2,1,0:T(8,128)(2,1)S(1)} collective-permute-done((bf16[8,128,128]{2,1,0:T(8,128)(2,1)S(1)}, bf16[8,128,128]{2,1,0:T(8,128)(2,1)S(1)}, u32[]{:S(2)}, u32[]{:S(2)}) %collective-permute-start.25) | collective-permute-done | bytes 262176 | tf_op jit(solution)/shard_map/ppermute | solution.py:279
  42.1 1.3 %collective-permute-start.15 = (bf16[8,128,128]{2,1,0:T(8,128)(2,1)S(1)}, bf16[8,128,128]{2,1,0:T(8,128)(2,1)S(1)}, u32[]{:S(2)}, u32[]{:S(2)}) collective-permute-start(bf16[8,128,128]{2,1,0:T(8,128)(2,1)S(1)} %get-tuple-element.39.refs_1_), channel_id=1, source_target_pairs={{0,1},{1,0},{2,3},{3,2},{4,5},{5,4},{6,7},{7,6},{8,9},{9,8},{10,11... | collective-permute-start | bytes 786440 | tf_op jit(solution)/shard_map/ppermute | solution.py:279
  43.4 0.8 shard_map.84
  44.2 3.5 %collective-permute-done.6.refs_0_ = bf16[8,128,128]{2,1,0:T(8,128)(2,1)S(1)} collective-permute-done((bf16[8,128,128]{2,1,0:T(8,128)(2,1)S(1)}, bf16[8,128,128]{2,1,0:T(8,128)(2,1)S(1)}, u32[]{:S(2)}, u32[]{:S(2)}) %collective-permute-start.6) | collective-permute-done | bytes 262176 | tf_op jit(solution)/shard_map/ppermute | solution.py:279
  47.7 3.3 %collective-permute-done.7.refs_1_ = bf16[8,128,128]{2,1,0:T(8,128)(2,1)S(1)} collective-permute-done((bf16[8,128,128]{2,1,0:T(8,128)(2,1)S(1)}, bf16[8,128,128]{2,1,0:T(8,128)(2,1)S(1)}, u32[]{:S(2)}, u32[]{:S(2)}) %collective-permute-start.7) | collective-permute-done | bytes 262176 | tf_op jit(solution)/shard_map/ppermute | solution.py:279
  50.9 0.6 collective-permute-start.9
  51.6 1.3 %collective-permute-start.10 = (bf16[8,128,128]{2,1,0:T(8,128)(2,1)S(1)}, bf16[8,128,128]{2,1,0:T(8,128)(2,1)S(1)}, u32[]{:S(2)}, u32[]{:S(2)}) collective-permute-start(bf16[8,128,128]{2,1,0:T(8,128)(2,1)S(1)} %collective-permute-done.7.refs_1_), channel_id=1, source_target_pairs={{0,1},{1,0},{2,3},{3,2},{4,5},{5,4},{6,7},{7,6},{8,9},{9,8},{10,11... | collective-permute-start | bytes 786440 | tf_op jit(solution)/shard_map/ppermute | solution.py:279
  52.9 1.2 %collective-permute-done.29.refs_1_ = bf16[8,128,128]{2,1,0:T(8,128)(2,1)S(1)} collective-permute-done((bf16[8,128,128]{2,1,0:T(8,128)(2,1)S(1)}, bf16[8,128,128]{2,1,0:T(8,128)(2,1)S(1)}, u32[]{:S(2)}, u32[]{:S(2)}) %collective-permute-start.29) | collective-permute-done | bytes 262176 | tf_op jit(solution)/shard_map/ppermute | solution.py:283
  54.1 1.3 %collective-permute-start.30 = (bf16[8,128,128]{2,1,0:T(8,128)(2,1)S(1)}, bf16[8,128,128]{2,1,0:T(8,128)(2,1)S(1)}, u32[]{:S(2)}, u32[]{:S(2)}) collective-permute-start(bf16[8,128,128]{2,1,0:T(8,128)(2,1)S(1)} %shard_map.85), channel_id=1, source_target_pairs={{0,12},{1,13},{2,14},{3,15},{4,8},{5,9},{6,10},{7,11},{8,4},{9,5},... | collective-permute-start | bytes 786440 | tf_op jit(solution)/shard_map/ppermute | solution.py:283
  55.4 4.2 %collective-permute-done.9.refs_2_ = bf16[8,128,128]{2,1,0:T(8,128)(2,1)S(1)} collective-permute-done((bf16[8,128,128]{2,1,0:T(8,128)(2,1)S(1)}, bf16[8,128,128]{2,1,0:T(8,128)(2,1)S(1)}, u32[]{:S(2)}, u32[]{:S(2)}) %collective-permute-start.9) | collective-permute-done | bytes 262176 | tf_op jit(solution)/shard_map/ppermute | solution.py:279
  59.7 0.3 collective-permute-done.10.refs_3_
  60.0 0.2 collective-permute-start.18
  60.2 0.3 collective-permute-start.19
  60.5 6.7 %collective-permute-done.28.refs_1_ = bf16[8,128,128]{2,1,0:T(8,128)(2,1)S(1)} collective-permute-done((bf16[8,128,128]{2,1,0:T(8,128)(2,1)S(1)}, bf16[8,128,128]{2,1,0:T(8,128)(2,1)S(1)}, u32[]{:S(2)}, u32[]{:S(2)}) %collective-permute-start.28) | collective-permute-done | bytes 262176 | tf_op jit(solution)/shard_map/ppermute | solution.py:283
  67.2 0.5 collective-permute-start.14
  67.7 0.7 shard_map.86
  68.4 0.8 collective-permute-start.31
  69.2 1.4 %collective-permute-start.32 = (bf16[2,128,128]{2,1,0:T(8,128)(2,1)S(1)}, bf16[2,128,128]{2,1,0:T(8,128)(2,1)S(1)}, u32[]{:S(2)}, u32[]{:S(2)}) collective-permute-start(bf16[2,128,128]{2,1,0:T(8,128)(2,1)S(1)} %get-tuple-element.59), channel_id=1, source_target_pairs={{0,2},{1,3},{2,0},{3,1},{4,6},{5,7},{6,4},{7,5},{8,10},{9,11},{10,... | collective-permute-start | bytes 196616 | tf_op jit(solution)/shard_map/ppermute | solution.py:279
  70.6 1.3 %collective-permute-start.33 = (bf16[2,128,128]{2,1,0:T(8,128)(2,1)S(1)}, bf16[2,128,128]{2,1,0:T(8,128)(2,1)S(1)}, u32[]{:S(2)}, u32[]{:S(2)}) collective-permute-start(bf16[2,128,128]{2,1,0:T(8,128)(2,1)S(1)} %get-tuple-element.60), channel_id=1, source_target_pairs={{0,3},{1,2},{2,1},{3,0},{4,7},{5,6},{6,5},{7,4},{8,11},{9,10},{10,... | collective-permute-start | bytes 196616 | tf_op jit(solution)/shard_map/ppermute | solution.py:279
  72.0 2.4 %shard_map.80 = (f32[256,512]{1,0:T(8,128)S(1)}, bf16[256,4096]{1,0:T(8,128)(2,1)}) custom-call(bf16[256,4096]{1,0:T(8,128)(2,1)S(1)} %get-tuple-element.32.tokens.mine, bf16[256,512]{1,0:T(8,128)(2,1)S(1)} %get-tuple-element.33.cot.cot_mine, bf16[8,128,128]{2,1,0:T(8,128)(2,1)S(1)} %get-tuple-element.38.refs_0_, ...), custom_call_target="tpu_custom_call" | custom-call | flops 1073741824 | bytes 6291456 | tf_op jit(solution)/shard_map/pallas_call | solution.py:289
  74.5 0.5 collective-permute-start.35
  75.1 0.7 collective-permute-done.33.refs_3_
  75.8 3.1 %shard_map.81 = (bf16[256,512]{1,0:T(8,128)(2,1)}, bf16[256,4096]{1,0:T(8,128)(2,1)}) custom-call(bf16[256,4096]{1,0:T(8,128)(2,1)S(1)} %get-tuple-element.32.tokens.mine, bf16[256,512]{1,0:T(8,128)(2,1)S(1)} %get-tuple-element.33.cot.cot_mine, bf16[8,128,128]{2,1,0:T(8,128)(2,1)S(1)} %collective-permute-done.6.refs_0_, ...), custom_call_target="tpu_custom_call", output_to_operand_aliasing={{1}: (11, {})} | custom-call | flops 1073741824 | bytes 6291456 | tf_op jit(solution)/shard_map/pallas_call | solution.py:289
  79.0 1.5 %shard_map.87 = bf16[16,128,128]{2,1,0:T(8,128)(2,1)} custom-call(s32[32]{0:T(128)S(1)} %shard_map.77.table, bf16[2,128,128]{2,1,0:T(8,128)(2,1)S(1)} %get-tuple-element.57.refs_0_, bf16[2,128,128]{2,1,0:T(8,128)(2,1)S(1)} %collective-permute-done.31.refs_1_, bf16[2,128,128]{2,1,0:T(8,128)(2,1)S(1)} %collective-permute-done.32.refs_2_, ...), custom_call_target="tpu_custom_call" | custom-call | flops 524288 | bytes 1048576 | tf_op jit(solution)/shard_map/pallas_call | solution.py:289
  (42 shorter events, 0.7 us)
Async XLA Ops:
  0.6 15.8 %collective-permute-start.20 = (bf16[256,4096]{1,0:T(8,128)(2,1)}, bf16[256,4096]{1,0:T(8,128)(2,1)S(1)}, u32[]{:S(2)}, u32[]{:S(2)}) collective-permute-start(bf16[256,4096]{1,0:T(8,128)(2,1)} %refs_0_.1), channel_id=1, source_target_pairs={{0,16},{16,0},{1,17},{17,1},{2,18},{18,2},{3,19},{19,3},{4,20},{20... | collective-permute-start | bytes 6291464 | tf_op jit(solution)/shard_map/ppermute | solution.py:286
  1.2 15.2 %collective-permute-start.21 = (bf16[256,512]{1,0:T(8,128)(2,1)}, bf16[256,512]{1,0:T(8,128)(2,1)S(1)}, u32[]{:S(2)}, u32[]{:S(2)}) collective-permute-start(bf16[256,512]{1,0:T(8,128)(2,1)} %refs_1_.1), channel_id=1, source_target_pairs={{0,16},{16,0},{1,17},{17,1},{2,18},{18,2},{3,19},{19,3},{4,20},{20... | collective-permute-start | bytes 786440 | tf_op jit(solution)/shard_map/ppermute | solution.py:286
  3.1 5.3 %collective-permute-start = (bf16[2,128,128]{2,1,0:T(8,128)(2,1)S(1)}, bf16[2,128,128]{2,1,0:T(8,128)(2,1)S(1)}, u32[]{:S(2)}, u32[]{:S(2)}) collective-permute-start(bf16[2,128,128]{2,1,0:T(8,128)(2,1)S(1)} %get-tuple-element.35), channel_id=1, source_target_pairs={{0,1},{1,0},{2,3},{3,2},{4,5},{5,4},{6,7},{7,6},{8,9},{9,8},{10,11... | collective-permute-start | bytes 196616 | tf_op jit(solution)/shard_map/ppermute | solution.py:279
  6.0 4.3 %collective-permute-start.1 = (bf16[2,128,128]{2,1,0:T(8,128)(2,1)S(1)}, bf16[2,128,128]{2,1,0:T(8,128)(2,1)S(1)}, u32[]{:S(2)}, u32[]{:S(2)}) collective-permute-start(bf16[2,128,128]{2,1,0:T(8,128)(2,1)S(1)} %get-tuple-element.36), channel_id=1, source_target_pairs={{0,2},{1,3},{2,0},{3,1},{4,6},{5,7},{6,4},{7,5},{8,10},{9,11},{10,... | collective-permute-start | bytes 196616 | tf_op jit(solution)/shard_map/ppermute | solution.py:279
  7.5 5.2 %collective-permute-start.2 = (bf16[2,128,128]{2,1,0:T(8,128)(2,1)S(1)}, bf16[2,128,128]{2,1,0:T(8,128)(2,1)S(1)}, u32[]{:S(2)}, u32[]{:S(2)}) collective-permute-start(bf16[2,128,128]{2,1,0:T(8,128)(2,1)S(1)} %get-tuple-element.37), channel_id=1, source_target_pairs={{0,3},{1,2},{2,1},{3,0},{4,7},{5,6},{6,5},{7,4},{8,11},{9,10},{10,... | collective-permute-start | bytes 196616 | tf_op jit(solution)/shard_map/ppermute | solution.py:279
  12.7 10.8 %collective-permute-start.4 = (bf16[8,128,128]{2,1,0:T(8,128)(2,1)S(1)}, bf16[8,128,128]{2,1,0:T(8,128)(2,1)S(1)}, u32[]{:S(2)}, u32[]{:S(2)}) collective-permute-start(bf16[8,128,128]{2,1,0:T(8,128)(2,1)S(1)} %shard_map.78.refs_0_), channel_id=1, source_target_pairs={{0,12},{1,13},{2,14},{3,15},{4,8},{5,9},{6,10},{7,11},{8,4},{9,5},... | collective-permute-start | bytes 786440 | tf_op jit(solution)/shard_map/ppermute | solution.py:283
  16.4 14.4 %copy-start = (s32[16]{0:T(128)S(1)}, s32[16]{0:T(128)}, u32[]{:S(2)}) copy-start(s32[16]{0:T(128)} %counts.1) | copy-start | bytes 196
  18.7 8.6 %collective-permute-start.23 = (bf16[8,128,128]{2,1,0:T(8,128)(2,1)S(1)}, bf16[8,128,128]{2,1,0:T(8,128)(2,1)S(1)}, u32[]{:S(2)}, u32[]{:S(2)}) collective-permute-start(bf16[8,128,128]{2,1,0:T(8,128)(2,1)S(1)} %get-tuple-element.47), channel_id=1, source_target_pairs={{0,1},{1,0},{2,3},{3,2},{4,5},{5,4},{6,7},{7,6},{8,9},{9,8},{10,11... | collective-permute-start | bytes 786440 | tf_op jit(solution)/shard_map/ppermute | solution.py:279
  19.3 8.6 %collective-permute-start.24 = (bf16[8,128,128]{2,1,0:T(8,128)(2,1)S(1)}, bf16[8,128,128]{2,1,0:T(8,128)(2,1)S(1)}, u32[]{:S(2)}, u32[]{:S(2)}) collective-permute-start(bf16[8,128,128]{2,1,0:T(8,128)(2,1)S(1)} %get-tuple-element.49), channel_id=1, source_target_pairs={{0,2},{1,3},{2,0},{3,1},{4,6},{5,7},{6,4},{7,5},{8,10},{9,11},{10,... | collective-permute-start | bytes 786440 | tf_op jit(solution)/shard_map/ppermute | solution.py:279
  19.8 9.7 %collective-permute-start.3 = (bf16[8,128,128]{2,1,0:T(8,128)(2,1)S(1)}, bf16[8,128,128]{2,1,0:T(8,128)(2,1)S(1)}, u32[]{:S(2)}, u32[]{:S(2)}) collective-permute-start(bf16[8,128,128]{2,1,0:T(8,128)(2,1)S(1)} %shard_map.78.refs_0_), channel_id=1, source_target_pairs={{0,4},{1,5},{2,6},{3,7},{4,0},{5,1},{6,2},{7,3},{8,12},{9,13},{10,... | collective-permute-start | bytes 786440 | tf_op jit(solution)/shard_map/ppermute | solution.py:283
  23.5 9.6 %collective-permute-start.5 = (bf16[8,128,128]{2,1,0:T(8,128)(2,1)S(1)}, bf16[8,128,128]{2,1,0:T(8,128)(2,1)S(1)}, u32[]{:S(2)}, u32[]{:S(2)}) collective-permute-start(bf16[8,128,128]{2,1,0:T(8,128)(2,1)S(1)} %collective-permute-done.4.refs_3_), channel_id=1, source_target_pairs={{0,4},{1,5},{2,6},{3,7},{4,0},{5,1},{6,2},{7,3},{8,12},{9,13},{10,... | collective-permute-start | bytes 786440 | tf_op jit(solution)/shard_map/ppermute | solution.py:283
  26.6 9.2 %collective-permute-start.22 = (bf16[8,128,128]{2,1,0:T(8,128)(2,1)S(1)}, bf16[8,128,128]{2,1,0:T(8,128)(2,1)S(1)}, u32[]{:S(2)}, u32[]{:S(2)}) collective-permute-start(bf16[8,128,128]{2,1,0:T(8,128)(2,1)S(1)} %get-tuple-element.45), channel_id=1, source_target_pairs={{0,1},{1,0},{2,3},{3,2},{4,5},{5,4},{6,7},{7,6},{8,9},{9,8},{10,11... | collective-permute-start | bytes 786440 | tf_op jit(solution)/shard_map/ppermute | solution.py:279
  27.3 9.2 %collective-permute-start.27 = (bf16[8,128,128]{2,1,0:T(8,128)(2,1)S(1)}, bf16[8,128,128]{2,1,0:T(8,128)(2,1)S(1)}, u32[]{:S(2)}, u32[]{:S(2)}) collective-permute-start(bf16[8,128,128]{2,1,0:T(8,128)(2,1)S(1)} %get-tuple-element.52), channel_id=1, source_target_pairs={{0,2},{1,3},{2,0},{3,1},{4,6},{5,7},{6,4},{7,5},{8,10},{9,11},{10,... | collective-permute-start | bytes 786440 | tf_op jit(solution)/shard_map/ppermute | solution.py:279
  28.0 14.0 %collective-permute-start.25 = (bf16[8,128,128]{2,1,0:T(8,128)(2,1)S(1)}, bf16[8,128,128]{2,1,0:T(8,128)(2,1)S(1)}, u32[]{:S(2)}, u32[]{:S(2)}) collective-permute-start(bf16[8,128,128]{2,1,0:T(8,128)(2,1)S(1)} %get-tuple-element.50), channel_id=1, source_target_pairs={{0,2},{1,3},{2,0},{3,1},{4,6},{5,7},{6,4},{7,5},{8,10},{9,11},{10,... | collective-permute-start | bytes 786440 | tf_op jit(solution)/shard_map/ppermute | solution.py:279
  29.5 13.9 %collective-permute-start.26 = (bf16[8,128,128]{2,1,0:T(8,128)(2,1)S(1)}, bf16[8,128,128]{2,1,0:T(8,128)(2,1)S(1)}, u32[]{:S(2)}, u32[]{:S(2)}) collective-permute-start(bf16[8,128,128]{2,1,0:T(8,128)(2,1)S(1)} %get-tuple-element.51), channel_id=1, source_target_pairs={{0,1},{1,0},{2,3},{3,2},{4,5},{5,4},{6,7},{7,6},{8,9},{9,8},{10,11... | collective-permute-start | bytes 786440 | tf_op jit(solution)/shard_map/ppermute | solution.py:279
  34.0 13.6 %collective-permute-start.6 = (bf16[8,128,128]{2,1,0:T(8,128)(2,1)S(1)}, bf16[8,128,128]{2,1,0:T(8,128)(2,1)S(1)}, u32[]{:S(2)}, u32[]{:S(2)}) collective-permute-start(bf16[8,128,128]{2,1,0:T(8,128)(2,1)S(1)} %get-tuple-element.38.refs_0_), channel_id=1, source_target_pairs={{0,2},{1,3},{2,0},{3,1},{4,6},{5,7},{6,4},{7,5},{8,10},{9,11},{10,... | collective-permute-start | bytes 786440 | tf_op jit(solution)/shard_map/ppermute | solution.py:279
  35.8 15.2 %collective-permute-start.7 = (bf16[8,128,128]{2,1,0:T(8,128)(2,1)S(1)}, bf16[8,128,128]{2,1,0:T(8,128)(2,1)S(1)}, u32[]{:S(2)}, u32[]{:S(2)}) collective-permute-start(bf16[8,128,128]{2,1,0:T(8,128)(2,1)S(1)} %get-tuple-element.39.refs_1_), channel_id=1, source_target_pairs={{0,2},{1,3},{2,0},{3,1},{4,6},{5,7},{6,4},{7,5},{8,10},{9,11},{10,... | collective-permute-start | bytes 786440 | tf_op jit(solution)/shard_map/ppermute | solution.py:279
  36.4 14.5 %collective-permute-start.8 = (bf16[8,128,128]{2,1,0:T(8,128)(2,1)S(1)}, bf16[8,128,128]{2,1,0:T(8,128)(2,1)S(1)}, u32[]{:S(2)}, u32[]{:S(2)}) collective-permute-start(bf16[8,128,128]{2,1,0:T(8,128)(2,1)S(1)} %get-tuple-element.38.refs_0_), channel_id=1, source_target_pairs={{0,1},{1,0},{2,3},{3,2},{4,5},{5,4},{6,7},{7,6},{8,9},{9,8},{10,11... | collective-permute-start | bytes 786440 | tf_op jit(solution)/shard_map/ppermute | solution.py:279
  42.1 9.5 %collective-permute-start.15 = (bf16[8,128,128]{2,1,0:T(8,128)(2,1)S(1)}, bf16[8,128,128]{2,1,0:T(8,128)(2,1)S(1)}, u32[]{:S(2)}, u32[]{:S(2)}) collective-permute-start(bf16[8,128,128]{2,1,0:T(8,128)(2,1)S(1)} %get-tuple-element.39.refs_1_), channel_id=1, source_target_pairs={{0,1},{1,0},{2,3},{3,2},{4,5},{5,4},{6,7},{7,6},{8,9},{9,8},{10,11... | collective-permute-start | bytes 786440 | tf_op jit(solution)/shard_map/ppermute | solution.py:279
  43.4 9.5 %collective-permute-start.16 = (bf16[8,128,128]{2,1,0:T(8,128)(2,1)S(1)}, bf16[8,128,128]{2,1,0:T(8,128)(2,1)S(1)}, u32[]{:S(2)}, u32[]{:S(2)}) collective-permute-start(bf16[8,128,128]{2,1,0:T(8,128)(2,1)S(1)} %get-tuple-element.38.refs_0_), channel_id=1, source_target_pairs={{0,16},{16,0},{1,17},{17,1},{2,18},{18,2},{3,19},{19,3},{4,20},{20... | collective-permute-start | bytes 786440 | tf_op jit(solution)/shard_map/ppermute | solution.py:286
  47.7 6.4 %collective-permute-start.29 = (bf16[8,128,128]{2,1,0:T(8,128)(2,1)S(1)}, bf16[8,128,128]{2,1,0:T(8,128)(2,1)S(1)}, u32[]{:S(2)}, u32[]{:S(2)}) collective-permute-start(bf16[8,128,128]{2,1,0:T(8,128)(2,1)S(1)} %get-tuple-element.56), channel_id=1, source_target_pairs={{0,4},{1,5},{2,6},{3,7},{4,0},{5,1},{6,2},{7,3},{8,12},{9,13},{10,... | collective-permute-start | bytes 786440 | tf_op jit(solution)/shard_map/ppermute | solution.py:283
  50.9 3.2 %collective-permute-start.17 = (bf16[8,128,128]{2,1,0:T(8,128)(2,1)S(1)}, bf16[8,128,128]{2,1,0:T(8,128)(2,1)S(1)}, u32[]{:S(2)}, u32[]{:S(2)}) collective-permute-start(bf16[8,128,128]{2,1,0:T(8,128)(2,1)S(1)} %get-tuple-element.39.refs_1_), channel_id=1, source_target_pairs={{0,16},{16,0},{1,17},{17,1},{2,18},{18,2},{3,19},{19,3},{4,20},{20... | collective-permute-start | bytes 786440 | tf_op jit(solution)/shard_map/ppermute | solution.py:286
  50.9 8.7 %collective-permute-start.9 = (bf16[8,128,128]{2,1,0:T(8,128)(2,1)S(1)}, bf16[8,128,128]{2,1,0:T(8,128)(2,1)S(1)}, u32[]{:S(2)}, u32[]{:S(2)}) collective-permute-start(bf16[8,128,128]{2,1,0:T(8,128)(2,1)S(1)} %collective-permute-done.8.refs_2_), channel_id=1, source_target_pairs={{0,2},{1,3},{2,0},{3,1},{4,6},{5,7},{6,4},{7,5},{8,10},{9,11},{10,... | collective-permute-start | bytes 786440 | tf_op jit(solution)/shard_map/ppermute | solution.py:279
  51.6 8.4 %collective-permute-start.10 = (bf16[8,128,128]{2,1,0:T(8,128)(2,1)S(1)}, bf16[8,128,128]{2,1,0:T(8,128)(2,1)S(1)}, u32[]{:S(2)}, u32[]{:S(2)}) collective-permute-start(bf16[8,128,128]{2,1,0:T(8,128)(2,1)S(1)} %collective-permute-done.7.refs_1_), channel_id=1, source_target_pairs={{0,1},{1,0},{2,3},{3,2},{4,5},{5,4},{6,7},{7,6},{8,9},{9,8},{10,11... | collective-permute-start | bytes 786440 | tf_op jit(solution)/shard_map/ppermute | solution.py:279
  52.9 7.3 %collective-permute-start.11 = (bf16[8,128,128]{2,1,0:T(8,128)(2,1)S(1)}, bf16[8,128,128]{2,1,0:T(8,128)(2,1)S(1)}, u32[]{:S(2)}, u32[]{:S(2)}) collective-permute-start(bf16[8,128,128]{2,1,0:T(8,128)(2,1)S(1)} %collective-permute-done.6.refs_0_), channel_id=1, source_target_pairs={{0,16},{16,0},{1,17},{17,1},{2,18},{18,2},{3,19},{19,3},{4,20},{20... | collective-permute-start | bytes 786440 | tf_op jit(solution)/shard_map/ppermute | solution.py:286
  54.1 13.2 %collective-permute-start.28 = (bf16[8,128,128]{2,1,0:T(8,128)(2,1)S(1)}, bf16[8,128,128]{2,1,0:T(8,128)(2,1)S(1)}, u32[]{:S(2)}, u32[]{:S(2)}) collective-permute-start(bf16[8,128,128]{2,1,0:T(8,128)(2,1)S(1)} %get-tuple-element.54), channel_id=1, source_target_pairs={{0,4},{1,5},{2,6},{3,7},{4,0},{5,1},{6,2},{7,3},{8,12},{9,13},{10,... | collective-permute-start | bytes 786440 | tf_op jit(solution)/shard_map/ppermute | solution.py:283
  54.1 13.1 %collective-permute-start.30 = (bf16[8,128,128]{2,1,0:T(8,128)(2,1)S(1)}, bf16[8,128,128]{2,1,0:T(8,128)(2,1)S(1)}, u32[]{:S(2)}, u32[]{:S(2)}) collective-permute-start(bf16[8,128,128]{2,1,0:T(8,128)(2,1)S(1)} %shard_map.85), channel_id=1, source_target_pairs={{0,12},{1,13},{2,14},{3,15},{4,8},{5,9},{6,10},{7,11},{8,4},{9,5},... | collective-permute-start | bytes 786440 | tf_op jit(solution)/shard_map/ppermute | solution.py:283
  59.7 8.7 %collective-permute-start.12 = (bf16[8,128,128]{2,1,0:T(8,128)(2,1)S(1)}, bf16[8,128,128]{2,1,0:T(8,128)(2,1)S(1)}, u32[]{:S(2)}, u32[]{:S(2)}) collective-permute-start(bf16[8,128,128]{2,1,0:T(8,128)(2,1)S(1)} %collective-permute-done.7.refs_1_), channel_id=1, source_target_pairs={{0,16},{16,0},{1,17},{17,1},{2,18},{18,2},{3,19},{19,3},{4,20},{20... | collective-permute-start | bytes 786440 | tf_op jit(solution)/shard_map/ppermute | solution.py:286
  60.0 9.2 %collective-permute-start.18 = (bf16[8,128,128]{2,1,0:T(8,128)(2,1)S(1)}, bf16[8,128,128]{2,1,0:T(8,128)(2,1)S(1)}, u32[]{:S(2)}, u32[]{:S(2)}) collective-permute-start(bf16[8,128,128]{2,1,0:T(8,128)(2,1)S(1)} %collective-permute-done.8.refs_2_), channel_id=1, source_target_pairs={{0,16},{16,0},{1,17},{17,1},{2,18},{18,2},{3,19},{19,3},{4,20},{20... | collective-permute-start | bytes 786440 | tf_op jit(solution)/shard_map/ppermute | solution.py:286
  60.2 10.4 %collective-permute-start.19 = (bf16[8,128,128]{2,1,0:T(8,128)(2,1)S(1)}, bf16[8,128,128]{2,1,0:T(8,128)(2,1)S(1)}, u32[]{:S(2)}, u32[]{:S(2)}) collective-permute-start(bf16[8,128,128]{2,1,0:T(8,128)(2,1)S(1)} %collective-permute-done.15.refs_3_), channel_id=1, source_target_pairs={{0,16},{16,0},{1,17},{17,1},{2,18},{18,2},{3,19},{19,3},{4,20},{20... | collective-permute-start | bytes 786440 | tf_op jit(solution)/shard_map/ppermute | solution.py:286
  67.2 7.2 %collective-permute-start.13 = (bf16[8,128,128]{2,1,0:T(8,128)(2,1)S(1)}, bf16[8,128,128]{2,1,0:T(8,128)(2,1)S(1)}, u32[]{:S(2)}, u32[]{:S(2)}) collective-permute-start(bf16[8,128,128]{2,1,0:T(8,128)(2,1)S(1)} %collective-permute-done.9.refs_2_), channel_id=1, source_target_pairs={{0,16},{16,0},{1,17},{17,1},{2,18},{18,2},{3,19},{19,3},{4,20},{20... | collective-permute-start | bytes 786440 | tf_op jit(solution)/shard_map/ppermute | solution.py:286
  67.2 8.6 %collective-permute-start.14 = (bf16[8,128,128]{2,1,0:T(8,128)(2,1)S(1)}, bf16[8,128,128]{2,1,0:T(8,128)(2,1)S(1)}, u32[]{:S(2)}, u32[]{:S(2)}) collective-permute-start(bf16[8,128,128]{2,1,0:T(8,128)(2,1)S(1)} %collective-permute-done.10.refs_3_), channel_id=1, source_target_pairs={{0,16},{16,0},{1,17},{17,1},{2,18},{18,2},{3,19},{19,3},{4,20},{20... | collective-permute-start | bytes 786440 | tf_op jit(solution)/shard_map/ppermute | solution.py:286
  68.4 6.1 %collective-permute-start.31 = (bf16[2,128,128]{2,1,0:T(8,128)(2,1)S(1)}, bf16[2,128,128]{2,1,0:T(8,128)(2,1)S(1)}, u32[]{:S(2)}, u32[]{:S(2)}) collective-permute-start(bf16[2,128,128]{2,1,0:T(8,128)(2,1)S(1)} %get-tuple-element.58), channel_id=1, source_target_pairs={{0,1},{1,0},{2,3},{3,2},{4,5},{5,4},{6,7},{7,6},{8,9},{9,8},{10,11... | collective-permute-start | bytes 196616 | tf_op jit(solution)/shard_map/ppermute | solution.py:279
  69.2 5.8 %collective-permute-start.32 = (bf16[2,128,128]{2,1,0:T(8,128)(2,1)S(1)}, bf16[2,128,128]{2,1,0:T(8,128)(2,1)S(1)}, u32[]{:S(2)}, u32[]{:S(2)}) collective-permute-start(bf16[2,128,128]{2,1,0:T(8,128)(2,1)S(1)} %get-tuple-element.59), channel_id=1, source_target_pairs={{0,2},{1,3},{2,0},{3,1},{4,6},{5,7},{6,4},{7,5},{8,10},{9,11},{10,... | collective-permute-start | bytes 196616 | tf_op jit(solution)/shard_map/ppermute | solution.py:279
  70.6 5.2 %collective-permute-start.33 = (bf16[2,128,128]{2,1,0:T(8,128)(2,1)S(1)}, bf16[2,128,128]{2,1,0:T(8,128)(2,1)S(1)}, u32[]{:S(2)}, u32[]{:S(2)}) collective-permute-start(bf16[2,128,128]{2,1,0:T(8,128)(2,1)S(1)} %get-tuple-element.60), channel_id=1, source_target_pairs={{0,3},{1,2},{2,1},{3,0},{4,7},{5,6},{6,5},{7,4},{8,11},{9,10},{10,... | collective-permute-start | bytes 196616 | tf_op jit(solution)/shard_map/ppermute | solution.py:279
  74.4 4.5 %collective-permute-start.34 = (bf16[2,128,128]{2,1,0:T(8,128)(2,1)S(1)}, bf16[2,128,128]{2,1,0:T(8,128)(2,1)S(1)}, u32[]{:S(2)}, u32[]{:S(2)}) collective-permute-start(bf16[2,128,128]{2,1,0:T(8,128)(2,1)S(1)} %get-tuple-element.57.refs_0_), channel_id=1, source_target_pairs={{0,16},{16,0},{1,17},{17,1},{2,18},{18,2},{3,19},{19,3},{4,20},{20... | collective-permute-start | bytes 196616 | tf_op jit(solution)/shard_map/ppermute | solution.py:286
  74.5 4.4 %collective-permute-start.35 = (bf16[2,128,128]{2,1,0:T(8,128)(2,1)S(1)}, bf16[2,128,128]{2,1,0:T(8,128)(2,1)S(1)}, u32[]{:S(2)}, u32[]{:S(2)}) collective-permute-start(bf16[2,128,128]{2,1,0:T(8,128)(2,1)S(1)} %collective-permute-done.31.refs_1_), channel_id=1, source_target_pairs={{0,16},{16,0},{1,17},{17,1},{2,18},{18,2},{3,19},{19,3},{4,20},{20... | collective-permute-start | bytes 196616 | tf_op jit(solution)/shard_map/ppermute | solution.py:286
  75.0 4.0 %collective-permute-start.36 = (bf16[2,128,128]{2,1,0:T(8,128)(2,1)S(1)}, bf16[2,128,128]{2,1,0:T(8,128)(2,1)S(1)}, u32[]{:S(2)}, u32[]{:S(2)}) collective-permute-start(bf16[2,128,128]{2,1,0:T(8,128)(2,1)S(1)} %collective-permute-done.32.refs_2_), channel_id=1, source_target_pairs={{0,16},{16,0},{1,17},{17,1},{2,18},{18,2},{3,19},{19,3},{4,20},{20... | collective-permute-start | bytes 196616 | tf_op jit(solution)/shard_map/ppermute | solution.py:286
  75.8 3.2 %collective-permute-start.37 = (bf16[2,128,128]{2,1,0:T(8,128)(2,1)S(1)}, bf16[2,128,128]{2,1,0:T(8,128)(2,1)S(1)}, u32[]{:S(2)}, u32[]{:S(2)}) collective-permute-start(bf16[2,128,128]{2,1,0:T(8,128)(2,1)S(1)} %collective-permute-done.33.refs_3_), channel_id=1, source_target_pairs={{0,16},{16,0},{1,17},{17,1},{2,18},{18,2},{3,19},{19,3},{4,20},{20... | collective-permute-start | bytes 196616 | tf_op jit(solution)/shard_map/ppermute | solution.py:286
